TPU v7x, 8 devices: a whole 2x2x1 slice. The times are simulated.
8 devices in a mesh: dp: 1 (over z), tp: 8 (over y, x, core).
Axes of the slice: x: 2, y: 2, z: 1, core: 2. Of those that a mesh axis runs over, the one named last changes fastest.
Arguments:
- x_in: bfloat16 [3, 3072, 5376], P('dp', 'tp')
- positions: int32 [3, 3072], P('dp', 'tp')
- grad_out: bfloat16 [3, 3072, 5376], P('dp', 'tp')
- w_query: bfloat16 [5376, 32, 128], P(None, 'tp')
- w_key: bfloat16 [5376, 16, 128], P(None, 'tp')
- w_value: bfloat16 [5376, 16, 128], P(None, 'tp')
- w_out: bfloat16 [32, 128, 5376], P('tp')
- gain_pre: float32 [5376], replicated
- gain_post: float32 [5376], replicated
Outputs:
- output 1: bfloat16 [3, 3072, 5376], P('dp', 'tp')
- output 2: bfloat16 [3, 3072, 5376], P('dp', 'tp')
- output 3: float32 [5376, 32, 128], P('dp', 'tp')
- output 4: float32 [5376, 16, 128], P('dp', 'tp')
- output 5: float32 [5376, 16, 128], P('dp', 'tp')
- output 6: float32 [32, 128, 5376], P(('dp', 'tp'))
- output 7: float32 [5376], P('dp')
- output 8: float32 [5376], P('dp')
All inputs are finite; a program needn't handle non-finite values.
Results may differ from a plain program's by a relative error of at most 0.0177591.
Values are sent between devices in bfloat16 or wider.
A program may use at most 1 GiB of HBM per device.

v0:
```python
import jax
import jax.numpy as jnp
from jax import lax
from jax.sharding import PartitionSpec as P

WINDOW = 4096
SOFT_CAP = 50.0
NORM_EPS = 1e-6
ROPE_THETA = 10000.0


def rms_norm(hidden, scale_w):
    values = hidden.astype(jnp.float32)
    inv_rms = lax.rsqrt(jnp.mean(values * values, axis=-1, keepdims=True) + NORM_EPS)
    return (values * inv_rms * (1.0 + scale_w)).astype(jnp.bfloat16)


def rope_tables(positions, head_dim):
    half_dim = head_dim // 2
    inv_freq = ROPE_THETA ** (-2.0 * jnp.arange(half_dim, dtype=jnp.float32) / head_dim)
    angles = positions.astype(jnp.float32)[:, :, None] * inv_freq
    return jnp.cos(angles)[:, :, None, :], jnp.sin(angles)[:, :, None, :]


def apply_rope(values, cos_t, sin_t):
    half_dim = values.shape[-1] // 2
    lo_half = values[..., :half_dim]
    hi_half = values[..., half_dim:]
    return jnp.concatenate([lo_half * cos_t - hi_half * sin_t, hi_half * cos_t + lo_half * sin_t], axis=-1)


def rope_transpose(grad_in, cos_t, sin_t):
    half_dim = grad_in.shape[-1] // 2
    lo_half = grad_in[..., :half_dim]
    hi_half = grad_in[..., half_dim:]
    return jnp.concatenate([lo_half * cos_t + hi_half * sin_t, hi_half * cos_t - lo_half * sin_t], axis=-1)


def block_probs(q_blk, k_blk, pos_q, pos_k):
    scores = jnp.einsum('bqkgd,bskd->bkgqs', q_blk, k_blk, preferred_element_type=jnp.float32)
    capped = SOFT_CAP * jnp.tanh(scores / SOFT_CAP)
    pos_gap = pos_q[:, :, None] - pos_k[:, None, :]
    in_window = ((pos_gap >= 0) & (pos_gap < WINDOW))[:, None, None, :, :]
    return capped, jax.nn.softmax(jnp.where(in_window, capped, -1e30), axis=-1)


def attention_fwd(q_all, k_all, v_all, positions):
    seq_len = positions.shape[1]
    q_block = min(128, seq_len)
    slab_len = min(WINDOW + q_block, seq_len)

    def block_step(blk_idx, out_acc):
        q_start = blk_idx * q_block
        k_start = jnp.maximum(q_start + q_block - slab_len, 0)
        q_blk = lax.dynamic_slice_in_dim(q_all, q_start, q_block, axis=1)
        k_blk = lax.dynamic_slice_in_dim(k_all, k_start, slab_len, axis=1)
        v_blk = lax.dynamic_slice_in_dim(v_all, k_start, slab_len, axis=1)
        pos_q = lax.dynamic_slice_in_dim(positions, q_start, q_block, axis=1)
        pos_k = lax.dynamic_slice_in_dim(positions, k_start, slab_len, axis=1)
        prob_blk = block_probs(q_blk, k_blk, pos_q, pos_k)[1]
        out_blk = jnp.einsum('bkgqs,bskd->bqkgd', prob_blk.astype(jnp.bfloat16), v_blk, preferred_element_type=jnp.float32)
        return lax.dynamic_update_slice_in_dim(out_acc, out_blk.astype(jnp.bfloat16), q_start, axis=1)

    return lax.fori_loop(0, seq_len // q_block, block_step, jnp.zeros_like(q_all))


def attention_bwd(q_all, k_all, v_all, positions, d_out):
    seq_len = positions.shape[1]
    q_block = min(128, seq_len)
    slab_len = min(WINDOW + q_block, seq_len)

    def block_step(blk_idx, grad_acc):
        d_q, d_k, d_v = grad_acc
        q_start = blk_idx * q_block
        k_start = jnp.maximum(q_start + q_block - slab_len, 0)
        q_blk = lax.dynamic_slice_in_dim(q_all, q_start, q_block, axis=1)
        k_blk = lax.dynamic_slice_in_dim(k_all, k_start, slab_len, axis=1)
        v_blk = lax.dynamic_slice_in_dim(v_all, k_start, slab_len, axis=1)
        do_blk = lax.dynamic_slice_in_dim(d_out, q_start, q_block, axis=1)
        pos_q = lax.dynamic_slice_in_dim(positions, q_start, q_block, axis=1)
        pos_k = lax.dynamic_slice_in_dim(positions, k_start, slab_len, axis=1)
        capped, prob_blk = block_probs(q_blk, k_blk, pos_q, pos_k)
        d_prob = jnp.einsum('bqkgd,bskd->bkgqs', do_blk, v_blk, preferred_element_type=jnp.float32)
        dv_blk = jnp.einsum('bkgqs,bqkgd->bskd', prob_blk.astype(jnp.bfloat16), do_blk, preferred_element_type=jnp.float32)
        d_capped = prob_blk * (d_prob - jnp.sum(prob_blk * d_prob, axis=-1, keepdims=True))
        d_score = (d_capped * (1.0 - jnp.square(capped / SOFT_CAP))).astype(jnp.bfloat16)
        dq_blk = jnp.einsum('bkgqs,bskd->bqkgd', d_score, k_blk, preferred_element_type=jnp.float32)
        dk_blk = jnp.einsum('bkgqs,bqkgd->bskd', d_score, q_blk, preferred_element_type=jnp.float32)
        d_q = lax.dynamic_update_slice_in_dim(d_q, dq_blk, q_start, axis=1)
        d_k = lax.dynamic_update_slice_in_dim(d_k, lax.dynamic_slice_in_dim(d_k, k_start, slab_len, axis=1) + dk_blk, k_start, axis=1)
        d_v = lax.dynamic_update_slice_in_dim(d_v, lax.dynamic_slice_in_dim(d_v, k_start, slab_len, axis=1) + dv_blk, k_start, axis=1)
        return d_q, d_k, d_v

    zero_init = (jnp.zeros(q_all.shape, jnp.float32), jnp.zeros(k_all.shape, jnp.float32), jnp.zeros(v_all.shape, jnp.float32))
    return lax.fori_loop(0, seq_len // q_block, block_step, zero_init)


def solution(mesh):
    act_spec = P('dp', 'tp', None)
    head_spec = P(None, 'tp', None)
    grad_spec = P('dp', 'tp', None)
    in_specs = (act_spec, P('dp', 'tp'), act_spec, head_spec, head_spec, head_spec, P('tp', None, None), P(None), P(None))
    out_specs = (act_spec, act_spec, grad_spec, grad_spec, grad_spec, P(('dp', 'tp'), None, None), P('dp'), P('dp'))

    def local_step(x_in, positions, grad_out, w_query, w_key, w_value, w_out, gain_pre, gain_post):
        heads_loc, head_dim = w_query.shape[1], w_query.shape[2]
        kv_loc = w_key.shape[1]
        groups = heads_loc // kv_loc
        q_scale = head_dim ** -0.5
        normed, pre_pullback = jax.vjp(rms_norm, x_in, gain_pre)
        normed_all = lax.all_gather(normed, 'tp', axis=1, tiled=True)
        pos_all = lax.all_gather(positions, 'tp', axis=1, tiled=True)
        n_rows, seq_len = pos_all.shape
        cos_t, sin_t = rope_tables(pos_all, head_dim)
        q_lin = jnp.einsum('bsd,dhe->bshe', normed_all, w_query, preferred_element_type=jnp.float32)
        k_lin = jnp.einsum('bsd,dhe->bshe', normed_all, w_key, preferred_element_type=jnp.float32)
        v_lin = jnp.einsum('bsd,dhe->bshe', normed_all, w_value, preferred_element_type=jnp.float32)
        q_all = (apply_rope(q_lin, cos_t, sin_t) * q_scale).astype(jnp.bfloat16).reshape(n_rows, seq_len, kv_loc, groups, head_dim)
        k_all = apply_rope(k_lin, cos_t, sin_t).astype(jnp.bfloat16)
        v_all = v_lin.astype(jnp.bfloat16)
        attn_out = attention_fwd(q_all, k_all, v_all, pos_all).reshape(n_rows, seq_len, heads_loc, head_dim)
        part_proj = jnp.einsum('bshe,hed->bsd', attn_out, w_out, preferred_element_type=jnp.float32)
        proj_loc = lax.psum_scatter(part_proj.astype(jnp.bfloat16), 'tp', scatter_dimension=1, tiled=True)
        post_norm, post_pullback = jax.vjp(rms_norm, proj_loc, gain_post)
        y_out = (x_in.astype(jnp.float32) + post_norm.astype(jnp.float32)).astype(jnp.bfloat16)
        d_proj, d_gain_post = post_pullback(grad_out)
        d_proj_all = lax.all_gather(d_proj, 'tp', axis=1, tiled=True)
        d_attn = jnp.einsum('bsd,hed->bshe', d_proj_all, w_out, preferred_element_type=jnp.float32).astype(jnp.bfloat16)
        grad_wo = jnp.einsum('bshe,bsd->hed', attn_out, d_proj_all, preferred_element_type=jnp.float32)
        d_q, d_k, d_v = attention_bwd(q_all, k_all, v_all, pos_all, d_attn.reshape(n_rows, seq_len, kv_loc, groups, head_dim))
        dq_lin = (rope_transpose(d_q.reshape(n_rows, seq_len, heads_loc, head_dim), cos_t, sin_t) * q_scale).astype(jnp.bfloat16)
        dk_lin = rope_transpose(d_k, cos_t, sin_t).astype(jnp.bfloat16)
        dv_lin = d_v.astype(jnp.bfloat16)
        grad_wq = jnp.einsum('bsd,bshe->dhe', normed_all, dq_lin, preferred_element_type=jnp.float32)
        grad_wk = jnp.einsum('bsd,bshe->dhe', normed_all, dk_lin, preferred_element_type=jnp.float32)
        grad_wv = jnp.einsum('bsd,bshe->dhe', normed_all, dv_lin, preferred_element_type=jnp.float32)
        d_normed = (jnp.einsum('bshe,dhe->bsd', dq_lin, w_query, preferred_element_type=jnp.float32)
                    + jnp.einsum('bshe,dhe->bsd', dk_lin, w_key, preferred_element_type=jnp.float32)
                    + jnp.einsum('bshe,dhe->bsd', dv_lin, w_value, preferred_element_type=jnp.float32))
        d_normed_loc = lax.psum_scatter(d_normed.astype(jnp.bfloat16), 'tp', scatter_dimension=1, tiled=True)
        d_x_norm, d_gain_pre = pre_pullback(d_normed_loc)
        grad_x = (grad_out.astype(jnp.float32) + d_x_norm.astype(jnp.float32)).astype(jnp.bfloat16)
        grad_pre = lax.psum(d_gain_pre, 'tp')
        grad_post = lax.psum(d_gain_post, 'tp')
        return y_out, grad_x, grad_wq, grad_wk, grad_wv, grad_wo, grad_pre, grad_post

    return jax.shard_map(local_step, mesh=mesh, in_specs=in_specs, out_specs=out_specs, check_vma=False)
```

profile of v0, /device:TPU:0, one launch (start us, length us, event | category | flops | bytes accessed | tf_op | source)
XLA Modules:
  0.0 7204.3 jit_solution(17850618842992009676)
XLA Ops:
  67.0 395.4 %all-gather.3.cloned.1.call-done = bf16[3,3072,5376]{2,1,0:T(8,128)(2,1)} async-done(((bf16[3,384,5376]{2,1,0:T(8,128)(2,1)}), bf16[3,3072,5376]{2,1,0:T(8,128)(2,1)}) %all-gather.3.cloned.1.call-update) | async-done | bytes 99090448 | tf_op jit(solution)/shard_map/all_gather | solution.py:111
  462.4 39.8 fusion.85
  516.3 60.0 fusion.87
  637.2 38.9 fusion.128
  681.3 1248.5 %while.33 = (s32[]{:T(128)}, bf16[3,3072,2,2,128]{4,1,3,2,0:T(8,128)(2,1)}, s32[3,3072]{1,0:T(4,128)S(1)}, bf16[3,3072,2,2,128]{4,1,3,2,0:T(8,128)(2,1)}, bf16[3...) while((s32[]{:T(128)}, ...), condition=%wide.region_4.5_spmd, body=%wide.region_1.4_spmd.sunk | while | flops 2468023296 | bytes 88134296 | solution.py:64
  1929.8 60.5 bitcast_convert_fusion
  1991.1 521.7 %reduce-scatter.3.cloned.1.call-done = bf16[3,384,5376]{2,1,0:T(8,128)(2,1)} async-done(((bf16[3,3072,5376]{2,1,0:T(8,128)(2,1)}), bf16[3,384,5376]{2,1,0:T(8,128)(2,1)}) %reduce-scatter.3.cloned.1.call-update) | async-done | bytes 12386320 | tf_op jit(solution)/shard_map/reduce_scatter | solution.py:123
  2553.3 432.7 %all-gather.5.cloned.1.call-done = bf16[3,3072,5376]{2,1,0:T(8,128)(2,1)} async-done(((bf16[3,384,5376]{2,1,0:T(8,128)(2,1)}), bf16[3,3072,5376]{2,1,0:T(8,128)(2,1)}) %all-gather.5.cloned.1.call-update) | async-done | bytes 99090448 | tf_op jit(solution)/shard_map/all_gather | solution.py:127
  2986.0 60.3 fusion.119
  3055.0 3247.5 %while.34 = (s32[]{:T(128)}, f32[3,3072,2,2,128]{1,4,3,2,0:T(8,128)}, f32[3,3072,2,128]{1,3,2,0:T(8,128)}, f32[3,3072,2,128]{1,3,2,0:T(8,128)}, s32[3,3072]{1,0:...) while((s32[]{:T(128)}, ...), condition=%wide.region_12.0_spmd.clone, body=%wide.region_8.12_spmd.clone.sunk | while | flops 6195523584 | bytes 319363840 | solution.py:95
  3417.6 37.4 bitcast_add_fusion.6
  3688.7 37.4 bitcast_add_fusion.6
  3959.9 37.4 bitcast_add_fusion.6
  4095.4 37.4 bitcast_add_fusion.6
  4772.9 37.4 bitcast_add_fusion.6
  5585.9 37.4 bitcast_add_fusion.6
  6324.8 74.0 %fusion.122 = f32[3,3072,5376,1]{2,1,3,0:T(8,128)} fusion(bf16[5376,4,128]{2,1,0:T(4,128)(2,1)} %param.16, f32[3,3072,4,64]{1,3,2,0:T(8,128)} %get-tuple-element.437, f32[3,3072,4,64]{1,3,2,0:T(8,128)} %get-tuple-element.436), kind=kOutput, calls=%fused_computation.144 | convolution fusion | flops 50748456960 | bytes 222560256 | tf_op jit(solution)/shard_map/bshe,dhe->bsd/dot_general | solution.py:137
  6398.9 65.3 fusion.131
  6464.2 155.2 %fusion.72 = bf16[3,3072,5376]{2,1,0:T(8,128)(2,1)} fusion(f32[3,3072,5376,1]{2,1,3,0:T(8,128)} %fusion.131, f32[3,3072,5376,1]{2,1,3,0:T(8,128)} %fusion.122, bf16[5376,2,128]{2,1,0:T(2,128)(2,1)} %param.18, f32[3,3072,2,128]{1,3,2,0:T(8,128)} %get-tuple-element.342), kind=kOutput, calls=%fused_computation.80 | convolution fusion | flops 25518145536 | bytes 507641856 | tf_op jit(solution)/shard_map/bshe,dhe->bsd/dot_general | solution.py:139
  6621.1 39.1 fusion.113
  6679.4 63.5 fusion.110
  6765.7 39.2 fusion.116
  6824.2 60.1 fusion.107
  6884.3 257.6 %reduce-scatter.5.cloned.1.call-done = bf16[3,384,5376]{2,1,0:T(8,128)(2,1)} async-done(((bf16[3,3072,5376]{2,1,0:T(8,128)(2,1)}), bf16[3,384,5376]{2,1,0:T(8,128)(2,1)}) %reduce-scatter.5.cloned.1.call-update) | async-done | bytes 12386320 | tf_op jit(solution)/shard_map/reduce_scatter | solution.py:140
  (582 shorter events, 4600.6 us)
Async XLA Ops:
  7.2 455.3 %all-gather.3.cloned.1.call-start = ((), (), s32[]{:S(2)}) async-start(), calls=%async_computation.2 | async-start | bytes 111476736 | tf_op jit(solution)/shard_map/all_gather | solution.py:111
  26.9 2485.9 %reduce-scatter.3.cloned.1.call-start = ((), (), s32[]{:S(2)}) async-start(), calls=%async_computation.3 | async-start | bytes 111476736 | tf_op jit(solution)/shard_map/reduce_scatter | solution.py:123
  67.0 509.3 %copy-start.1 = (f32[3,3072,64]{1,2,0:T(8,128)}, f32[3,3072,64]{1,2,0:T(8,128)S(1)}, u32[]{:S(2)}) copy-start(f32[3,3072,64]{1,2,0:T(8,128)S(1)} %get-tuple-element.446) | copy-start | bytes 7077892
  516.3 60.0 copy-start.4
  1990.4 995.6 %all-gather.5.cloned.1.call-start = ((), (), s32[]{:S(2)}) async-start(), calls=%async_computation.4 | async-start | bytes 111476736 | tf_op jit(solution)/shard_map/all_gather | solution.py:127
  2553.3 4588.6 %reduce-scatter.5.cloned.1.call-start = ((), (), s32[]{:S(2)}) async-start(), calls=%async_computation.5 | async-start | bytes 111476736 | tf_op jit(solution)/shard_map/reduce_scatter | solution.py:140
  3728.5 54.7 slice-start.3
  3864.1 54.8 slice-start.3
  4406.1 54.7 slice-start.3
  4541.7 54.7 slice-start.3
  4812.7 54.7 slice-start.3
  5354.6 54.7 slice-start.3
  5761.2 54.7 slice-start.3
  5896.7 54.7 slice-start.3
  6032.2 54.7 slice-start.3
  6167.7 54.7 slice-start.3
  6324.8 74.0 %copy-start.8 = (bf16[5376,2,128]{2,1,0:T(2,128)(2,1)S(1)}, bf16[5376,2,128]{2,1,0:T(2,128)(2,1)}, u32[]{:S(2)}) copy-start(bf16[5376,2,128]{2,1,0:T(2,128)(2,1)} %param.17) | copy-start | bytes 8257540
  6742.9 81.2 %slice-start.5 = ((s8[9437184]{0:T(1024)(128)(4,1)}), s8[4194304]{0:T(1024)(128)(4,1)S(1)}, s32[]{:S(2)}) async-start(s8[9437184]{0:T(1024)(128)(4,1)} %bitcast.260), calls=%async_computation.11 | async-start | bytes 8388608
  6765.7 58.4 slice-start.6
  6765.7 58.4 slice-start.7
  6824.1 317.8 %copy-start.16 = (f32[5376]{0:T(1024)S(1)}, f32[5376]{0:T(1024)}, u32[]{:S(2)}) copy-start(f32[5376]{0:T(1024)} %copy-done.15) | copy-start | bytes 64516
  6824.1 317.7 %copy-start.18 = (f32[3,384]{1,0:T(4,128)S(1)}, f32[3,384]{1,0:T(4,128)}, u32[]{:S(2)}) copy-start(f32[3,384]{1,0:T(4,128)} %copy-done.17) | copy-start | bytes 13828
  6884.3 271.0 %copy-start.21 = (f32[3,384]{1,0:T(4,128)S(1)}, f32[3,384]{1,0:T(4,128)}, u32[]{:S(2)}) copy-start(f32[3,384]{1,0:T(4,128)} %copy-done.20) | copy-start | bytes 13828
  6884.3 271.0 %copy-start.19 = (f32[5376]{0:T(1024)S(1)}, f32[5376]{0:T(1024)}, u32[]{:S(2)}) copy-start(f32[5376]{0:T(1024)} %get-tuple-element.396) | copy-start | bytes 64516
  (59 other events, 2040.7 us)
Sparse Core Ops, SparseCore 0:
  27.0 435.3 all-gather.2
  1990.5 522.2 reduce-scatter.2
  2553.4 432.5 all-gather.4
  6619.6 522.2 reduce-scatter.4
where the time goes:
time: 7210 us; the launch traced here: 7200 us
  matrix products  3820 us (53%)
  waiting for transfers between devices  1610 us (22%)
  other arithmetic  1560 us (22%)
  local copies, waits for them, and re-layouts  160 us (2%)
    sub x48, other arithmetic, block_probs(): jax.nn.softmax(jnp.where(in_window, capped, -1e+30), axis=-1)  1350 us
    dot_general x24, matrix products, block_step(): jnp.einsum('bkgqs,bqkgd->bskd', d_score, q_blk, preferred_element_type=jn...  894 us
    dot_general x24, matrix products, block_step(): jnp.einsum('bkgqs,bskd->bqkgd', d_score, k_blk, preferred_element_type=jn...  770 us
    dot_general x48, matrix products, block_probs(): jnp.einsum('bqkgd,bskd->bkgqs', q_blk, k_blk, preferred_element_type=jnp....  559 us
    reduce_scatter x1, waiting for transfers between devices, local_step(): lax.psum_scatter(part_proj.astype(jnp.bfloat16), 'tp', scatter_dimension=...  522 us
    all_gather x1, waiting for transfers between devices, local_step(): d_proj_all = lax.all_gather(d_proj, 'tp', axis=1, tiled=True)  433 us
    all_gather x1, waiting for transfers between devices, local_step(): normed_all = lax.all_gather(normed, 'tp', axis=1, tiled=True)  395 us
    dot_general x24, matrix products, block_step(): jnp.einsum('bkgqs,bqkgd->bskd', prob_blk.astype(jnp.bfloat16), do_blk, pr...  357 us
  transfers between devices with their start and end apart: 4, of which 4 were waited for; matrix products, arithmetic and copies ran while one was open for 4% of the time, Pallas kernels for 0%

commit v1 on v0

v1 whole, which is shorter than its diff:
```python
import functools

import jax
import jax.numpy as jnp
from jax import lax
from jax.experimental import pallas as pl
from jax.experimental.pallas import tpu as pltpu
from jax.sharding import PartitionSpec as P


WINDOW = 4096
SOFT_CAP = 50.0
NORM_EPS = 1e-6
ROPE_THETA = 10000.0
LOG2E = 1.4426950408889634
BLK = 256
LANES = 128


def dot_f32(lhs, rhs, lhs_dim, rhs_dim):
    return lax.dot_general(lhs, rhs, (((lhs_dim,), (rhs_dim,)), ((), ())), preferred_element_type=jnp.float32)


ROWS = 128
CHUNK = 16


def row_specs(seq, depth):
    whole = pl.BlockSpec((1, ROWS, depth), lambda i: (seq, i, 0))
    one = pl.BlockSpec((ROWS, depth), lambda i: (i, 0))
    vec = pl.BlockSpec((1, depth), lambda i: (0, 0))
    return whole, one, vec


def inverse_rms(values):
    return lax.rsqrt(jnp.mean(values * values, axis=-1, keepdims=True) + NORM_EPS)


def norm_grad(values, inv, d_out, gain):
    scaled = d_out * gain
    dot = jnp.mean(scaled * values, axis=-1, keepdims=True)
    return scaled * inv - values * (inv * inv * inv * dot)


def fold_rows(block):
    return sum(block[r:r + 8] for r in range(0, CHUNK, 8))


def pre_norm_kernel(x_ref, gain_ref, n_ref):
    gain = 1.0 + gain_ref[...]

    @pl.loop(0, ROWS // CHUNK)
    def _(c):
        rows = pl.ds(pl.multiple_of(c * CHUNK, CHUNK), CHUNK)
        values = x_ref[0, rows, :].astype(jnp.float32)
        n_ref[rows, :] = (values * inverse_rms(values) * gain).astype(n_ref.dtype)


def pre_norm(x_in, gain, seq):
    _, rows, depth = x_in.shape
    whole, one, vec = row_specs(seq, depth)
    return pl.pallas_call(
        pre_norm_kernel,
        grid=(rows // ROWS,),
        in_specs=[whole, vec],
        out_specs=one,
        out_shape=jax.ShapeDtypeStruct((rows, depth), jnp.bfloat16),
        compiler_params=pltpu.CompilerParams(vmem_limit_bytes=32 * 1024 * 1024),
        cost_estimate=pl.CostEstimate(flops=rows * depth * 400, bytes_accessed=4 * rows * depth, transcendentals=rows),
        name="pre_norm",
    )(x_in, gain)


def post_norm_kernel(first, proj_ref, x_ref, go_ref, gain_ref, dg_in_ref, *refs):
    y_ref, d_proj_ref, dg_ref, dg_scr = refs[0 if first else 1:]
    step = pl.program_id(0)
    gain = 1.0 + gain_ref[...]

    @pl.when(step == 0)
    def _():
        dg_scr[...] = jnp.zeros_like(dg_scr)

    @pl.loop(0, ROWS // CHUNK)
    def _(c):
        rows = pl.ds(pl.multiple_of(c * CHUNK, CHUNK), CHUNK)
        values = proj_ref[rows, :].astype(jnp.float32)
        inv = inverse_rms(values)
        unit = values * inv
        post = (unit * gain).astype(jnp.bfloat16).astype(jnp.float32)
        y_ref[0, rows, :] = (x_ref[0, rows, :].astype(jnp.float32) + post).astype(y_ref.dtype)
        d_out = go_ref[0, rows, :].astype(jnp.float32)
        dg_scr[...] += fold_rows(d_out * unit)
        d_proj_ref[rows, :] = norm_grad(values, inv, d_out, gain).astype(d_proj_ref.dtype)

    @pl.when(step == pl.num_programs(0) - 1)
    def _():
        dg_ref[...] = dg_in_ref[...] + jnp.sum(dg_scr[...], axis=0, keepdims=True)


def post_norm(proj, x_in, grad_out, gain, dg_in, y_prev, seq):
    _, rows, depth = x_in.shape
    whole, one, vec = row_specs(seq, depth)
    first = y_prev is None
    return pl.pallas_call(
        functools.partial(post_norm_kernel, first),
        grid=(rows // ROWS,),
        in_specs=[one, whole, whole, vec, vec] + ([] if first else [pl.BlockSpec(memory_space=pl.ANY)]),
        out_specs=[whole, one, vec],
        out_shape=[
            jax.ShapeDtypeStruct(x_in.shape, jnp.bfloat16),
            jax.ShapeDtypeStruct((rows, depth), jnp.bfloat16),
            jax.ShapeDtypeStruct((1, depth), jnp.float32),
        ],
        scratch_shapes=[pltpu.VMEM((8, depth), jnp.float32)],
        input_output_aliases={} if first else {5: 0},
        compiler_params=pltpu.CompilerParams(vmem_limit_bytes=32 * 1024 * 1024),
        cost_estimate=pl.CostEstimate(flops=rows * depth * 800, bytes_accessed=10 * rows * depth, transcendentals=rows),
        name="post_norm",
    )(proj, x_in, grad_out, gain, dg_in, *([] if first else [y_prev]))


def pre_grad_kernel(first, dn_ref, x_ref, go_ref, gain_ref, dg_in_ref, *refs):
    gx_ref, dg_ref, dg_scr = refs[0 if first else 1:]
    step = pl.program_id(0)
    gain = 1.0 + gain_ref[...]

    @pl.when(step == 0)
    def _():
        dg_scr[...] = jnp.zeros_like(dg_scr)

    @pl.loop(0, ROWS // CHUNK)
    def _(c):
        rows = pl.ds(pl.multiple_of(c * CHUNK, CHUNK), CHUNK)
        values = x_ref[0, rows, :].astype(jnp.float32)
        inv = inverse_rms(values)
        d_out = dn_ref[rows, :].astype(jnp.float32)
        dg_scr[...] += fold_rows(d_out * (values * inv))
        d_x = norm_grad(values, inv, d_out, gain).astype(jnp.bfloat16).astype(jnp.float32)
        gx_ref[0, rows, :] = (go_ref[0, rows, :].astype(jnp.float32) + d_x).astype(gx_ref.dtype)

    @pl.when(step == pl.num_programs(0) - 1)
    def _():
        dg_ref[...] = dg_in_ref[...] + jnp.sum(dg_scr[...], axis=0, keepdims=True)


def pre_grad(d_normed, x_in, grad_out, gain, dg_in, gx_prev, seq):
    _, rows, depth = x_in.shape
    whole, one, vec = row_specs(seq, depth)
    first = gx_prev is None
    return pl.pallas_call(
        functools.partial(pre_grad_kernel, first),
        grid=(rows // ROWS,),
        in_specs=[one, whole, whole, vec, vec] + ([] if first else [pl.BlockSpec(memory_space=pl.ANY)]),
        out_specs=[whole, vec],
        out_shape=[jax.ShapeDtypeStruct(x_in.shape, jnp.bfloat16), jax.ShapeDtypeStruct((1, depth), jnp.float32)],
        scratch_shapes=[pltpu.VMEM((8, depth), jnp.float32)],
        input_output_aliases={} if first else {5: 0},
        compiler_params=pltpu.CompilerParams(vmem_limit_bytes=32 * 1024 * 1024),
        cost_estimate=pl.CostEstimate(flops=rows * depth * 700, bytes_accessed=8 * rows * depth, transcendentals=rows),
        name="pre_grad",
    )(d_normed, x_in, grad_out, gain, dg_in, *([] if first else [gx_prev]))


def out_proj_kernel(o_ref, w_ref, r_ref):
    o_all = jnp.concatenate([o_ref[d] for d in range(o_ref.shape[0])], axis=1)
    r_ref[...] = jnp.dot(o_all, w_ref[...], preferred_element_type=jnp.float32).astype(r_ref.dtype)


def out_proj(o_mine, w_all):
    n_dev, rows, cols = o_mine.shape
    depth = w_all.shape[1]
    tile = 768
    return pl.pallas_call(
        out_proj_kernel,
        grid=(depth // tile,),
        in_specs=[
            pl.BlockSpec((n_dev, rows, cols), lambda i: (0, 0, 0), pipeline_mode=pl.Buffered(1)),
            pl.BlockSpec((n_dev * cols, tile), lambda i: (0, i)),
        ],
        out_specs=pl.BlockSpec((rows, tile), lambda i: (0, i)),
        out_shape=jax.ShapeDtypeStruct((rows, depth), jnp.bfloat16),
        compiler_params=pltpu.CompilerParams(vmem_limit_bytes=40 * 1024 * 1024),
        cost_estimate=pl.CostEstimate(flops=2 * n_dev * rows * cols * depth, bytes_accessed=2 * n_dev * cols * depth, transcendentals=0),
        name="out_proj",
    )(o_mine, w_all)


def grad_w_kernel(n_rows, head_dim, *refs):
    a_refs, d_refs, outs = refs[:n_rows], refs[n_rows:2 * n_rows], refs[2 * n_rows:]
    total = dot_f32(a_refs[0][...], d_refs[0][...], 0, 0)
    for a_ref, d_ref in zip(a_refs[1:], d_refs[1:]):
        total = total + dot_f32(a_ref[...], d_ref[...], 0, 0)
    col = 0
    for out in outs:
        for h in range(out.shape[1]):
            out[:, h, :] = total[:, col:col + head_dim]
            col += head_dim


def grad_w(normed, d_lin, heads, head_dim):
    seq_len, depth = normed[0].shape
    cols = d_lin[0].shape[1]
    n_rows = len(normed)
    tile = 256
    return pl.pallas_call(
        functools.partial(grad_w_kernel, n_rows, head_dim),
        grid=(depth // tile,),
        in_specs=[pl.BlockSpec((seq_len, tile), lambda i: (0, i))] * n_rows
        + [pl.BlockSpec((seq_len, cols), lambda i: (0, 0), pipeline_mode=pl.Buffered(1))] * n_rows,
        out_specs=[pl.BlockSpec((tile, h, head_dim), lambda i: (i, 0, 0)) for h in heads],
        out_shape=[jax.ShapeDtypeStruct((depth, h, head_dim), jnp.float32) for h in heads],
        compiler_params=pltpu.CompilerParams(vmem_limit_bytes=58 * 1024 * 1024),
        cost_estimate=pl.CostEstimate(flops=2 * n_rows * seq_len * depth * cols, bytes_accessed=2 * n_rows * seq_len * (depth + cols), transcendentals=0),
        name="grad_w",
    )(*normed, *d_lin)


def qkv_kernel(q_cols, k_cols, head_dim, q_scale, a_ref, w_ref, cos_ref, sin_ref, q_ref, k_ref, v_ref):
    lin = jnp.dot(a_ref[...], w_ref[...], preferred_element_type=jnp.float32)
    cos_t, sin_t = cos_ref[...], sin_ref[...]
    for h in range((q_cols + k_cols) // head_dim):
        col = h * head_dim
        part = lin[:, col:col + head_dim]
        part = part * cos_t + pltpu.roll(part, head_dim // 2, 1) * sin_t
        if col < q_cols:
            q_ref[:, col:col + head_dim] = (part * q_scale).astype(q_ref.dtype)
        else:
            k_ref[:, col - q_cols:col - q_cols + head_dim] = part.astype(k_ref.dtype)
    v_ref[...] = lin[:, q_cols + k_cols:].astype(v_ref.dtype)


def qkv_project(normed, w_all, cos_t, sin_t, q_cols, k_cols, head_dim):
    rows, depth = normed.shape
    cols = w_all.shape[1]
    v_cols = cols - q_cols - k_cols
    tile = 512
    return pl.pallas_call(
        functools.partial(qkv_kernel, q_cols, k_cols, head_dim, head_dim ** -0.5),
        grid=(rows // tile,),
        in_specs=[
            pl.BlockSpec((tile, depth), lambda i: (i, 0)),
            pl.BlockSpec((depth, cols), lambda i: (0, 0), pipeline_mode=pl.Buffered(1)),
            pl.BlockSpec((tile, head_dim), lambda i: (i, 0)),
            pl.BlockSpec((tile, head_dim), lambda i: (i, 0)),
        ],
        out_specs=[
            pl.BlockSpec((tile, q_cols), lambda i: (i, 0)),
            pl.BlockSpec((tile, k_cols), lambda i: (i, 0)),
            pl.BlockSpec((tile, v_cols), lambda i: (i, 0)),
        ],
        out_shape=[
            jax.ShapeDtypeStruct((rows, q_cols), jnp.bfloat16),
            jax.ShapeDtypeStruct((rows, k_cols), jnp.bfloat16),
            jax.ShapeDtypeStruct((rows, v_cols), jnp.bfloat16),
        ],
        compiler_params=pltpu.CompilerParams(vmem_limit_bytes=56 * 1024 * 1024),
        cost_estimate=pl.CostEstimate(flops=2 * rows * depth * cols, bytes_accessed=2 * (rows * depth + depth * cols + rows * cols), transcendentals=0),
        name="qkv_project",
    )(normed, w_all, cos_t, sin_t)


def stack_heads(block, groups, head_dim):
    return jnp.concatenate([block[:, g * head_dim:(g + 1) * head_dim] for g in range(groups)], axis=0)


def attn_fwd_kernel(groups, head_dim, first_ref, q_ref, k_ref, v_ref, pos_ref, key_pos_ref, o_ref, lse_ref, m_scr, l_scr, acc_scr):
    blk = pl.program_id(1)
    q_all = stack_heads(q_ref[...], groups, head_dim)
    floor_row = jnp.concatenate([pos_ref[...]] * groups, axis=1) - WINDOW
    wide = groups * BLK

    def visit(kb, diagonal):
        start = pl.multiple_of(kb * BLK, BLK)
        k_blk = k_ref[pl.ds(start, BLK), :]
        v_blk = v_ref[pl.ds(start, BLK), :]
        scores = dot_f32(k_blk, q_all, 1, 1)
        capped = jnp.tanh(scores * (1.0 / SOFT_CAP)) * (SOFT_CAP * LOG2E)
        keep = jnp.concatenate([key_pos_ref[pl.ds(start, BLK), :]] * (wide // LANES), axis=1) > floor_row
        if diagonal:
            key_idx = lax.broadcasted_iota(jnp.int32, (BLK, wide), 0)
            q_idx = lax.broadcasted_iota(jnp.int32, (BLK, wide), 1) % BLK
            keep = keep & (key_idx <= q_idx)
        capped = jnp.where(keep, capped, -1e30)
        top = jnp.max(capped, axis=0, keepdims=True)
        if diagonal:
            prob = jnp.exp2(capped - top)
            m_scr[...] = top
            l_scr[...] = jnp.sum(prob, axis=0, keepdims=True)
            acc_scr[...] = dot_f32(v_blk, prob.astype(jnp.bfloat16), 0, 0)
        else:
            m_old = m_scr[...]
            m_new = jnp.maximum(m_old, top)
            alpha = jnp.exp2(m_old - m_new)
            prob = jnp.exp2(capped - m_new)
            m_scr[...] = m_new
            l_scr[...] = l_scr[...] * alpha + jnp.sum(prob, axis=0, keepdims=True)
            acc_scr[...] = acc_scr[...] * alpha + dot_f32(v_blk, prob.astype(jnp.bfloat16), 0, 0)

    visit(blk, True)

    @pl.loop(first_ref[blk], blk)
    def _(kb):
        visit(kb, False)

    total = l_scr[...]
    out = (acc_scr[...] / total).T
    for g in range(groups):
        o_ref[:, g * head_dim:(g + 1) * head_dim] = out[g * BLK:(g + 1) * BLK, :].astype(o_ref.dtype)
    lse_ref[0, 0] = m_scr[...] + jnp.log2(total)


def attn_fwd(q_all, k_all, v_all, pos, key_pos, first_blk, groups, head_dim):
    seq_len, q_cols = q_all.shape
    kv_heads = k_all.shape[1] // head_dim
    n_blk = seq_len // BLK
    wide = groups * BLK
    pairs = seq_len * seq_len // 4 * groups * kv_heads
    return pl.pallas_call(
        functools.partial(attn_fwd_kernel, groups, head_dim),
        grid_spec=pltpu.PrefetchScalarGridSpec(
            num_scalar_prefetch=1,
            grid=(kv_heads, n_blk),
            in_specs=[
                pl.BlockSpec((BLK, groups * head_dim), lambda h, i, first: (i, h)),
                pl.BlockSpec((seq_len, head_dim), lambda h, i, first: (0, h)),
                pl.BlockSpec((seq_len, head_dim), lambda h, i, first: (0, h)),
                pl.BlockSpec((1, BLK), lambda h, i, first: (0, i)),
                pl.BlockSpec((seq_len, LANES), lambda h, i, first: (0, 0)),
            ],
            out_specs=[
                pl.BlockSpec((BLK, groups * head_dim), lambda h, i, first: (i, h)),
                pl.BlockSpec((1, 1, 1, wide), lambda h, i, first: (h, i, 0, 0)),
            ],
            scratch_shapes=[
                pltpu.VMEM((1, wide), jnp.float32),
                pltpu.VMEM((1, wide), jnp.float32),
                pltpu.VMEM((head_dim, wide), jnp.float32),
            ],
        ),
        out_shape=[
            jax.ShapeDtypeStruct((seq_len, q_cols), jnp.bfloat16),
            jax.ShapeDtypeStruct((kv_heads, n_blk, 1, wide), jnp.float32),
        ],
        compiler_params=pltpu.CompilerParams(vmem_limit_bytes=48 * 1024 * 1024),
        cost_estimate=pl.CostEstimate(flops=8 * pairs * head_dim, bytes_accessed=8 * seq_len * q_cols, transcendentals=2 * pairs),
        name="attn_fwd",
    )(first_blk, q_all, k_all, v_all, pos, key_pos)


def attn_bwd_kernel(groups, head_dim, q_scale, first_ref, q_ref, k_ref, v_ref, o_ref, do_ref, pos_ref, key_pos_ref, lse_ref, cos_ref, sin_ref,
                    out_ref, dq_scr, dk_scr, dv_scr, dq_out, dk_out, dv_out, dq_sem, kv_sem):
    head, blk = pl.program_id(0), pl.program_id(1)
    n_head, n_blk = pl.num_programs(0), pl.num_programs(1)
    half = head_dim // 2
    wide = groups * BLK
    q_width = groups * head_dim
    slot = blk % 2

    @pl.when(blk == 0)
    def _():
        dk_scr[...] = jnp.zeros_like(dk_scr)
        dv_scr[...] = jnp.zeros_like(dv_scr)

    q_all = stack_heads(q_ref[...], groups, head_dim)
    do_all = stack_heads(do_ref[...], groups, head_dim)
    o_all = stack_heads(o_ref[...], groups, head_dim)
    floor_row = jnp.concatenate([pos_ref[...]] * groups, axis=1) - WINDOW
    lse_row = lse_ref[0, 0]
    delta = jnp.sum((do_all.astype(jnp.float32) * o_all.astype(jnp.float32)).T, axis=0, keepdims=True)

    def visit(kb, diagonal):
        start = pl.multiple_of(kb * BLK, BLK)
        k_blk = k_ref[pl.ds(start, BLK), :]
        v_blk = v_ref[pl.ds(start, BLK), :]
        scores = dot_f32(k_blk, q_all, 1, 1)
        d_prob = dot_f32(v_blk, do_all, 1, 1)
        tanh_s = jnp.tanh(scores * (1.0 / SOFT_CAP))
        keep = jnp.concatenate([key_pos_ref[pl.ds(start, BLK), :]] * (wide // LANES), axis=1) > floor_row
        if diagonal:
            key_idx = lax.broadcasted_iota(jnp.int32, (BLK, wide), 0)
            q_idx = lax.broadcasted_iota(jnp.int32, (BLK, wide), 1) % BLK
            keep = keep & (key_idx <= q_idx)
        prob = jnp.exp2(jnp.where(keep, tanh_s * (SOFT_CAP * LOG2E) - lse_row, -1e30))
        d_score = (prob * (d_prob - delta) * (1.0 - tanh_s * tanh_s)).astype(jnp.bfloat16)
        dv_scr[pl.ds(start, BLK), :] += jnp.dot(prob.astype(jnp.bfloat16), do_all, preferred_element_type=jnp.float32)
        dk_scr[pl.ds(start, BLK), :] += jnp.dot(d_score, q_all, preferred_element_type=jnp.float32)
        dq_new = dot_f32(k_blk, d_score, 0, 0)
        if diagonal:
            dq_scr[...] = dq_new
        else:
            dq_scr[...] += dq_new

    visit(blk, True)

    @pl.loop(first_ref[blk], blk)
    def _(kb):
        visit(kb, False)

    def dq_copy(h, i):
        dst = out_ref.at[pl.ds(pl.multiple_of(i * BLK, BLK), BLK), pl.ds(pl.multiple_of(h * q_width, q_width), q_width)]
        return pltpu.make_async_copy(dq_out.at[slot], dst, dq_sem.at[slot])

    def kv_copy(which, src, h):
        col = n_head * q_width + which * n_head * head_dim + h * head_dim
        dst = out_ref.at[:, pl.ds(pl.multiple_of(col, head_dim), head_dim)]
        return pltpu.make_async_copy(src, dst, kv_sem.at[which])

    @pl.when(head * n_blk + blk >= 2)
    def _():
        dq_copy(head, blk).wait()

    d_q = dq_scr[...].T
    rows = pl.ds(pl.multiple_of(blk * BLK, BLK), BLK)
    cos_t, sin_t = cos_ref[rows, :], sin_ref[rows, :]
    for g in range(groups):
        part = d_q[g * BLK:(g + 1) * BLK, :]
        part = (part * cos_t - pltpu.roll(part, half, 1) * sin_t) * q_scale
        dq_out[slot, :, g * head_dim:(g + 1) * head_dim] = part.astype(dq_out.dtype)
    dq_copy(head, blk).start()

    @pl.when(blk == n_blk - 1)
    def _():
        @pl.loop(0, n_blk)
        def _(i):
            rows = pl.ds(pl.multiple_of(i * BLK, BLK), BLK)
            part = dk_scr[rows, :]
            part = part * cos_ref[rows, :] - pltpu.roll(part, half, 1) * sin_ref[rows, :]
            dk_out[rows, :] = part.astype(dk_out.dtype)
            dv_out[rows, :] = dv_scr[rows, :].astype(dv_out.dtype)

        kv_copy(0, dk_out, head).start()
        kv_copy(1, dv_out, head).start()
        kv_copy(0, dk_out, head).wait()
        kv_copy(1, dv_out, head).wait()

    @pl.when((blk == n_blk - 1) & (head == n_head - 1))
    def _():
        for s in range(2):
            pltpu.make_async_copy(dq_out.at[s], out_ref.at[pl.ds(0, BLK), pl.ds(0, q_width)], dq_sem.at[s]).wait()


def attn_bwd(q_all, k_all, v_all, o_all, d_o, pos, key_pos, lse, first_blk, cos_t, sin_t, groups, head_dim):
    seq_len, q_cols = q_all.shape
    k_cols = k_all.shape[1]
    kv_heads = k_cols // head_dim
    n_blk = seq_len // BLK
    wide = groups * BLK
    pairs = seq_len * seq_len // 4 * groups * kv_heads
    by_q = pl.BlockSpec((BLK, groups * head_dim), lambda h, i, first: (i, h))
    by_h = pl.BlockSpec((seq_len, head_dim), lambda h, i, first: (0, h))
    table = pl.BlockSpec((seq_len, LANES), lambda h, i, first: (0, 0))
    return pl.pallas_call(
        functools.partial(attn_bwd_kernel, groups, head_dim, head_dim ** -0.5),
        grid_spec=pltpu.PrefetchScalarGridSpec(
            num_scalar_prefetch=1,
            grid=(kv_heads, n_blk),
            in_specs=[
                by_q, by_h, by_h, by_q, by_q,
                pl.BlockSpec((1, BLK), lambda h, i, first: (0, i)),
                table,
                pl.BlockSpec((1, 1, 1, wide), lambda h, i, first: (h, i, 0, 0)),
                table, table,
            ],
            out_specs=pl.BlockSpec(memory_space=pl.ANY),
            scratch_shapes=[
                pltpu.VMEM((head_dim, wide), jnp.float32),
                pltpu.VMEM((seq_len, head_dim), jnp.float32),
                pltpu.VMEM((seq_len, head_dim), jnp.float32),
                pltpu.VMEM((2, BLK, groups * head_dim), jnp.bfloat16),
                pltpu.VMEM((seq_len, head_dim), jnp.bfloat16),
                pltpu.VMEM((seq_len, head_dim), jnp.bfloat16),
                pltpu.SemaphoreType.DMA((2,)),
                pltpu.SemaphoreType.DMA((2,)),
            ],
        ),
        out_shape=jax.ShapeDtypeStruct((seq_len, q_cols + 2 * k_cols), jnp.bfloat16),
        compiler_params=pltpu.CompilerParams(vmem_limit_bytes=48 * 1024 * 1024),
        cost_estimate=pl.CostEstimate(flops=20 * pairs * head_dim, bytes_accessed=16 * seq_len * q_cols, transcendentals=2 * pairs),
        name="attn_bwd",
    )(first_blk, q_all, k_all, v_all, o_all, d_o, pos, key_pos, lse, cos_t, sin_t)


def solution(mesh):
    act_spec = P('dp', 'tp', None)
    head_spec = P(None, 'tp', None)
    grad_spec = P('dp', 'tp', None)
    in_specs = (act_spec, P('dp', 'tp'), act_spec, head_spec, head_spec, head_spec, P('tp', None, None), P(None), P(None))
    out_specs = (act_spec, act_spec, grad_spec, grad_spec, grad_spec, P(('dp', 'tp'), None, None), P('dp'), P('dp'))

    def local_body(x_in, positions, grad_out, w_query, w_key, w_value, w_out, gain_pre, gain_post):
        n_rows, _, depth = x_in.shape
        heads_loc, head_dim = w_query.shape[1], w_query.shape[2]
        kv_loc = w_key.shape[1]
        groups = heads_loc // kv_loc
        q_cols, k_cols = heads_loc * head_dim, kv_loc * head_dim

        gain_pre_row, gain_post_row = gain_pre[None, :], gain_post[None, :]
        normed_all = []
        for b in range(n_rows):
            normed = pre_norm(x_in, gain_pre_row, b)
            normed_all.append(lax.all_gather(normed, 'tp', axis=0, tiled=True))
        w_out_loc = w_out.reshape(q_cols, depth)
        w_out_all = lax.all_gather(w_out_loc, 'tp', axis=0, tiled=True)

        pos_all = lax.all_gather(positions, 'tp', axis=1, tiled=True)
        seq_len = pos_all.shape[1]
        half = head_dim // 2
        inv_freq = ROPE_THETA ** (-2.0 * jnp.arange(half, dtype=jnp.float32) / head_dim)
        before = pos_all[:, None, :] <= pos_all[:, ::BLK, None] - WINDOW
        first_blk = jnp.sum(before.astype(jnp.int32), axis=-1) // BLK
        w_all = jnp.concatenate([w_query.reshape(depth, q_cols), w_key.reshape(depth, k_cols), w_value.reshape(depth, k_cols)], axis=1)

        saved, d_proj_all = [], []
        y_out, d_post = None, jnp.zeros((1, depth), jnp.float32)
        for b in range(n_rows):
            angles = pos_all[b].astype(jnp.float32)[:, None] * inv_freq
            cos_h, sin_h = jnp.cos(angles), jnp.sin(angles)
            cos_t = jnp.concatenate([cos_h, cos_h], axis=-1)
            sin_t = jnp.concatenate([-sin_h, sin_h], axis=-1)
            pos_b = pos_all[b][None, :]
            key_pos = jnp.broadcast_to(pos_all[b][:, None], (seq_len, LANES))
            q_b, k_b, v_b = qkv_project(normed_all[b], w_all, cos_t, sin_t, q_cols, k_cols, head_dim)
            o_b, lse_b = attn_fwd(q_b, k_b, v_b, pos_b, key_pos, first_blk[b], groups, head_dim)
            o_mine = lax.all_to_all(o_b.reshape(-1, seq_len // mesh.shape['tp'], q_cols), 'tp', split_axis=0, concat_axis=0, tiled=True)
            proj = out_proj(o_mine, w_out_all)
            y_out, d_proj, d_post = post_norm(proj, x_in, grad_out, gain_post_row, d_post, y_out, b)
            d_proj_all.append(lax.all_gather(d_proj, 'tp', axis=0, tiled=True))
            saved.append((q_b, k_b, v_b, o_b, pos_b, key_pos, lse_b, cos_t, sin_t))

        grad_x, d_pre = None, jnp.zeros((1, depth), jnp.float32)
        grad_wo = jnp.zeros((), jnp.float32)
        d_lin = []
        for b in range(n_rows):
            q_b, k_b, v_b, o_b, pos_b, key_pos, lse_b, cos_t, sin_t = saved[b]
            d_o = dot_f32(d_proj_all[b], w_out_loc, 1, 1).astype(jnp.bfloat16)
            d_lin.append(attn_bwd(q_b, k_b, v_b, o_b, d_o, pos_b, key_pos, lse_b, first_blk[b], cos_t, sin_t, groups, head_dim))
            d_normed = dot_f32(d_lin[b], w_all, 1, 1).astype(jnp.bfloat16)
            d_normed_loc = lax.psum_scatter(d_normed, 'tp', scatter_dimension=0, tiled=True)
            grad_x, d_pre = pre_grad(d_normed_loc, x_in, grad_out, gain_pre_row, d_pre, grad_x, b)
            grad_wo = grad_wo + dot_f32(o_b, d_proj_all[b], 0, 0)

        grad_wq, grad_wk, grad_wv = grad_w(normed_all, d_lin, (heads_loc, kv_loc, kv_loc), head_dim)
        grad_pre = lax.psum(d_pre[0], 'tp')
        grad_post = lax.psum(d_post[0], 'tp')
        return y_out, grad_x, grad_wq, grad_wk, grad_wv, grad_wo.reshape(w_out.shape), grad_pre, grad_post

    return jax.shard_map(local_body, mesh=mesh, in_specs=in_specs, out_specs=out_specs, check_vma=False)
```

time: 7210 us -> 1910 us (0.26)
  matrix products: 3820 us -> 285 us
  other arithmetic: 1560 us -> 32.8 us
  waiting for transfers between devices: 1610 us -> 584 us
  Pallas kernels: 0 us -> 702 us
  blocking collectives: 37.6 us -> 188 us
  local copies, waits for them, and re-layouts: 160 us -> 85.7 us
    dot_general x180 -> x9, matrix products: 3820 us -> 285 us  [dot_f32(): lax.dot_general(lhs, rhs, (((lhs_dim,), (rhs_dim,)), ((), ())), preferred...]
    sub x49 -> x1, other arithmetic: 1360 us -> 0.01 us  [local_body(): before = pos_all[:, None, :] <= pos_all[:, ::BLK, None] - WINDOW]
    pallas_call x0 -> x22, Pallas kernels: none -> 702 us  [the longest x3 171 us: attn_bwd(): pl.pallas_call(functools.partial(attn_bwd_kernel, groups, head_dim, head_...]
    reduce_scatter x2 -> x3, waiting for transfers between devices: 779 us -> 227 us  [local_body(): lax.psum_scatter(d_normed, 'tp', scatter_dimension=0, tiled=True)]
    all_gather x2 -> x7, waiting for transfers between devices: 828 us -> 285 us  [the longest x3 191 us: local_body(): normed_all.append(lax.all_gather(normed, 'tp', axis=0, tiled=True))]
    all_to_all x0 -> x2, blocking collectives: none -> 150 us  [local_body(): lax.all_to_all(o_b.reshape(-1, seq_len // mesh.shape['tp'], q_cols), 'tp'...]
  transfers between devices with their start and end apart: 4 -> 11, of which waited for: 4 -> 7; matrix products, arithmetic and copies ran while one was open for 4% -> 17% of each run, Pallas kernels for 0% -> 36%
where the time goes in v1:
time: 1910 us; the launch traced here: 1900 us
  Pallas kernels  702 us (37%)
  waiting for transfers between devices  584 us (31%)
  matrix products  285 us (15%)
  blocking collectives  188 us (10%)
  local copies, waits for them, and re-layouts  85.7 us (4%)
  other arithmetic  32.8 us (2%)
    dot_general x9, matrix products, dot_f32(): lax.dot_general(lhs, rhs, (((lhs_dim,), (rhs_dim,)), ((), ())), preferred...  285 us
    reduce_scatter x3, waiting for transfers between devices, local_body(): lax.psum_scatter(d_normed, 'tp', scatter_dimension=0, tiled=True)  227 us
    all_gather x3, waiting for transfers between devices, local_body(): normed_all.append(lax.all_gather(normed, 'tp', axis=0, tiled=True))  191 us
    pallas_call x3, Pallas kernels, attn_bwd(): pl.pallas_call(functools.partial(attn_bwd_kernel, groups, head_dim, head_...  171 us
    all_to_all x2, blocking collectives, local_body(): lax.all_to_all(o_b.reshape(-1, seq_len // mesh.shape['tp'], q_cols), 'tp'...  150 us
    pallas_call x1, Pallas kernels, grad_w(): pl.pallas_call(functools.partial(grad_w_kernel, n_rows, head_dim), grid=(...  130 us
    pallas_call x3, Pallas kernels, qkv_project(): pl.pallas_call(functools.partial(qkv_kernel, q_cols, k_cols, head_dim, he...  128 us
    pallas_call x3, Pallas kernels, attn_fwd(): pl.pallas_call(functools.partial(attn_fwd_kernel, groups, head_dim), grid...  128 us
  transfers between devices with their start and end apart: 11, of which 7 were waited for; matrix products, arithmetic and copies ran while one was open for 17% of the time, Pallas kernels for 36%

profile of v1, /device:TPU:0, one launch (start us, length us, event | category | flops | bytes accessed | tf_op | source)
XLA Modules:
  0.0 1896.7 jit_solution(15311209626333314836)
XLA Ops:
  90.5 84.4 %all-gather.14.cloned.1.call-done.a_ref.refs_0_ = bf16[3072,5376]{1,0:T(8,128)(2,1)} async-done(((bf16[384,5376]{1,0:T(8,128)(2,1)}), bf16[3072,5376]{1,0:T(8,128)(2,1)}) %all-gather.14.cloned.1.call-update) | async-done | bytes 33030160 | tf_op jit(solution)/shard_map/all_gather | solution.py:501
  174.9 42.9 %qkv_project.5 = (bf16[3072,512]{1,0:T(8,128)(2,1)}, bf16[3072,256]{1,0:T(8,128)(2,1)}, bf16[3072,256]{1,0:T(8,128)(2,1)}) custom-call(bf16[3072,5376]{1,0:T(8,128)(2,1)} %all-gather.14.cloned.1.call-done.a_ref.refs_0_, bf16[5376,1024]{1,0:T(8,128)(2,1)} %bitcast_dynamic-update-slice_fusion.1.w_ref, f32[3072,128]{1,0:T(8,128)} %get-tuple-element.101.cos_ref, ...), custom_call_target="tpu_custom_call" | custom-call | flops 33822867456 | bytes 50331648 | tf_op jit(solution)/shard_map/qkv_project/pallas_call | solution.py:237
  221.7 48.8 %attn_fwd.5 = (bf16[3072,512]{1,0:T(8,128)(2,1)}, f32[2,12,1,512]{3,2,1,0:T(1,128)S(1)}) custom-call(s32[12]{0:T(128)S(1)} %get-tuple-element.88.first_ref, bf16[3072,512]{1,0:T(8,128)(2,1)} %get-tuple-element.49.q_ref, bf16[3072,256]{1,0:T(8,128)(2,1)S(1)} %copy-done.33, bf16[3072,256]{1,0:T(8,128)(2,1)S(1)} %copy-done.35, ...), custom_call_target="tpu_custom_call" | custom-call | flops 9663676416 | bytes 12582912 | tf_op jit(solution)/shard_map/attn_fwd/pallas_call | solution.py:318
  273.2 71.6 %all-to-all-done.2.o_ref = bf16[8,384,512]{2,1,0:T(8,128)(2,1)S(1)} async-done(((bf16[8,384,512]{2,1,0:T(8,128)(2,1)}), bf16[8,384,512]{2,1,0:T(8,128)(2,1)S(1)}, u32[]{:S(2)}, u32[]{:S(2)}) %all-to-all-start.2) | async-done | bytes 3145760 | tf_op jit(solution)/shard_map/all_to_all | solution.py:524
  344.8 66.0 %all-gather.10.cloned.1.call-done.w_ref = bf16[4096,5376]{1,0:T(8,128)(2,1)} async-done(((bf16[512,5376]{1,0:T(8,128)(2,1)}), bf16[4096,5376]{1,0:T(8,128)(2,1)}) %all-gather.10.cloned.1.call-update) | async-done | bytes 44040208 | tf_op jit(solution)/shard_map/all_gather | solution.py:503
  459.1 107.1 %all-gather.12.cloned.1.call-done.a_ref.refs_1_ = bf16[3072,5376]{1,0:T(8,128)(2,1)} async-done(((bf16[384,5376]{1,0:T(8,128)(2,1)}), bf16[3072,5376]{1,0:T(8,128)(2,1)}) %all-gather.12.cloned.1.call-update) | async-done | bytes 33030160 | tf_op jit(solution)/shard_map/all_gather | solution.py:501
  566.1 42.5 %qkv_project.4 = (bf16[3072,512]{1,0:T(8,128)(2,1)}, bf16[3072,256]{1,0:T(8,128)(2,1)}, bf16[3072,256]{1,0:T(8,128)(2,1)}) custom-call(bf16[3072,5376]{1,0:T(8,128)(2,1)} %all-gather.12.cloned.1.call-done.a_ref.refs_1_, bf16[5376,1024]{1,0:T(8,128)(2,1)} %bitcast_dynamic-update-slice_fusion.1.w_ref, f32[3072,128]{1,0:T(8,128)} %get-tuple-element.99.cos_ref, ...), custom_call_target="tpu_custom_call" | custom-call | flops 33822867456 | bytes 50331648 | tf_op jit(solution)/shard_map/qkv_project/pallas_call | solution.py:237
  612.5 39.5 %attn_fwd.4 = (bf16[3072,512]{1,0:T(8,128)(2,1)}, f32[2,12,1,512]{3,2,1,0:T(1,128)S(1)}) custom-call(s32[12]{0:T(128)S(1)} %get-tuple-element.89.first_ref, bf16[3072,512]{1,0:T(8,128)(2,1)} %get-tuple-element.45.q_ref, bf16[3072,256]{1,0:T(8,128)(2,1)S(1)} %copy-done.37, bf16[3072,256]{1,0:T(8,128)(2,1)S(1)} %copy-done.39, ...), custom_call_target="tpu_custom_call" | custom-call | flops 9663676416 | bytes 12582912 | tf_op jit(solution)/shard_map/attn_fwd/pallas_call | solution.py:318
  652.0 75.3 %all_to_all.15.o_ref = bf16[8,384,512]{2,1,0:T(8,128)(2,1)S(1)} all-to-all(bf16[8,384,512]{2,1,0:T(8,128)(2,1)} %bitcast.61), channel_id=1, replica_groups=mesh['dp'=1,'tp'=8] {'tp'}, dimensions={0} | all-to-all | bytes 6291456 | tf_op jit(solution)/shard_map/all_to_all | solution.py:524
  770.1 42.5 %qkv_project.3 = (bf16[3072,512]{1,0:T(8,128)(2,1)}, bf16[3072,256]{1,0:T(8,128)(2,1)}, bf16[3072,256]{1,0:T(8,128)(2,1)}) custom-call(bf16[3072,5376]{1,0:T(8,128)(2,1)} %all-gather.8.cloned.1.call-done.a_ref.refs_2_, bf16[5376,1024]{1,0:T(8,128)(2,1)} %bitcast_dynamic-update-slice_fusion.1.w_ref, f32[3072,128]{1,0:T(8,128)} %get-tuple-element.97.cos_ref, ...), custom_call_target="tpu_custom_call" | custom-call | flops 33822867456 | bytes 50331648 | tf_op jit(solution)/shard_map/qkv_project/pallas_call | solution.py:237
  816.7 39.6 %attn_fwd.3 = (bf16[3072,512]{1,0:T(8,128)(2,1)}, f32[2,12,1,512]{3,2,1,0:T(1,128)S(1)}) custom-call(s32[12]{0:T(128)S(1)} %get-tuple-element.90.first_ref, bf16[3072,512]{1,0:T(8,128)(2,1)} %get-tuple-element.41.q_ref, bf16[3072,256]{1,0:T(8,128)(2,1)S(1)} %copy-done.41, bf16[3072,256]{1,0:T(8,128)(2,1)S(1)} %copy-done.43, s32[1,3072]{1,0:T(1,128)S(1)} %copy-done.27, ...), custom_call_target="tpu_custom_call" | custom-call | flops 9663676416 | bytes 12582912 | tf_op jit(solution)/shard_map/attn_fwd/pallas_call | solution.py:318
  856.3 74.8 %all_to_all.16.o_ref = bf16[8,384,512]{2,1,0:T(8,128)(2,1)S(1)} all-to-all(bf16[8,384,512]{2,1,0:T(8,128)(2,1)} %bitcast.51), channel_id=1, replica_groups=mesh['dp'=1,'tp'=8] {'tp'}, dimensions={0} | all-to-all | bytes 6291456 | tf_op jit(solution)/shard_map/all_to_all | solution.py:524
  994.9 63.5 %attn_bwd.5.refs_3_ = bf16[3072,1024]{1,0:T(8,128)(2,1)} custom-call(s32[12]{0:T(128)S(1)} %copy-done.32, bf16[3072,512]{1,0:T(8,128)(2,1)} %get-tuple-element.49.q_ref, bf16[3072,256]{1,0:T(8,128)(2,1)S(1)} %copy-done.34, bf16[3072,256]{1,0:T(8,128)(2,1)S(1)} %copy-done.36, bf16[3072,512]{1,0:T(8,128)(2,1)} %get-tuple-element.52.o_ref, ...), custom_call_target="tpu_custom_call" | custom-call | flops 24159191040 | bytes 25165824 | tf_op jit(solution)/shard_map/attn_bwd/pallas_call | solution.py:452
  1058.5 42.7 %convolution_convert_fusion = bf16[3072,5376]{1,0:T(8,128)(2,1)} fusion(bf16[3072,1024]{1,0:T(8,128)(2,1)} %attn_bwd.5.refs_3_, bf16[5376,1024]{1,0:T(8,128)(2,1)} %bitcast_dynamic-update-slice_fusion.1.w_ref), kind=kOutput, calls=%fused_computation | convolution fusion | flops 33839382528 | bytes 50331648 | tf_op jit(solution)/shard_map/dot_general | solution.py:21
  1101.4 26.3 %convolution_convert_fusion.4.do_ref = bf16[3072,512]{1,0:T(8,128)(2,1)} fusion(bf16[3072,5376]{1,0:T(8,128)(2,1)} %all-gather.18.cloned.1.call-done, bf16[512,5376]{1,0:T(8,128)(2,1)} %bitcast.58), kind=kOutput, calls=%fused_computation.6 | convolution fusion | flops 16913006592 | bytes 41680896 | tf_op jit(solution)/shard_map/dot_general | solution.py:21
  1130.5 53.3 %attn_bwd.4.refs_4_ = bf16[3072,1024]{1,0:T(8,128)(2,1)} custom-call(s32[12]{0:T(128)S(1)} %get-tuple-element.89.first_ref, bf16[3072,512]{1,0:T(8,128)(2,1)} %get-tuple-element.45.q_ref, bf16[3072,256]{1,0:T(8,128)(2,1)S(1)} %copy-done.38, bf16[3072,256]{1,0:T(8,128)(2,1)S(1)} %copy-done.40, bf16[3072,512]{1,0:T(8,128)(2,1)} %get-tuple-element.48.o_ref, ...), custom_call_target="tpu_custom_call" | custom-call | flops 24159191040 | bytes 25165824 | tf_op jit(solution)/shard_map/attn_bwd/pallas_call | solution.py:452
  1183.8 43.1 %convolution_convert_fusion.1 = bf16[3072,5376]{1,0:T(8,128)(2,1)} fusion(bf16[3072,1024]{1,0:T(8,128)(2,1)} %attn_bwd.4.refs_4_, bf16[5376,1024]{1,0:T(8,128)(2,1)} %bitcast_dynamic-update-slice_fusion.1.w_ref), kind=kOutput, calls=%fused_computation.1 | convolution fusion | flops 33839382528 | bytes 50331648 | tf_op jit(solution)/shard_map/dot_general | solution.py:21
  1227.2 27.1 %all-gather.16.cloned.1.call-done = bf16[3072,5376]{1,0:T(8,128)(2,1)} async-done(((bf16[384,5376]{1,0:T(8,128)(2,1)}), bf16[3072,5376]{1,0:T(8,128)(2,1)}) %all-gather.16.cloned.1.call-update) | async-done | bytes 33030160 | tf_op jit(solution)/shard_map/all_gather | solution.py:527
  1279.3 53.8 %attn_bwd.3.refs_5_ = bf16[3072,1024]{1,0:T(8,128)(2,1)} custom-call(s32[12]{0:T(128)S(1)} %get-tuple-element.90.first_ref, bf16[3072,512]{1,0:T(8,128)(2,1)} %get-tuple-element.41.q_ref, bf16[3072,256]{1,0:T(8,128)(2,1)S(1)} %copy-done.42, bf16[3072,256]{1,0:T(8,128)(2,1)S(1)} %copy-done.44, bf16[3072,512]{1,0:T(8,128)(2,1)} %get-tuple-element.44.o_ref, ...), custom_call_target="tpu_custom_call" | custom-call | flops 24159191040 | bytes 25165824 | tf_op jit(solution)/shard_map/attn_bwd/pallas_call | solution.py:452
  1333.1 43.0 %convolution_convert_fusion.2 = bf16[3072,5376]{1,0:T(8,128)(2,1)} fusion(bf16[3072,1024]{1,0:T(8,128)(2,1)} %attn_bwd.3.refs_5_, bf16[5376,1024]{1,0:T(8,128)(2,1)} %bitcast_dynamic-update-slice_fusion.1.w_ref), kind=kOutput, calls=%fused_computation.2 | convolution fusion | flops 33839382528 | bytes 50331648 | tf_op jit(solution)/shard_map/dot_general | solution.py:21
  1427.3 30.1 %add_add_fusion = f32[512,5376]{1,0:T(8,128)} fusion(f32[512,5376]{1,0:T(8,128)} %fusion.6, f32[512,5376]{1,0:T(8,128)} %fusion.7, bf16[3072,512]{1,0:T(8,128)(2,1)S(1)} %copy-done.45, bf16[3072,5376]{1,0:T(8,128)(2,1)} %all-gather.16.cloned.1.call-done), kind=kOutput, calls=%fused_computation.3 | convolution fusion | flops 16916938752 | bytes 69206016 | tf_op jit(solution)/shard_map/dot_general | solution.py:21
  1457.5 129.9 %grad_w.1 = (f32[5376,4,128]{2,1,0:T(4,128)}, f32[5376,2,128]{2,1,0:T(2,128)}, f32[5376,2,128]{2,1,0:T(2,128)}) custom-call(bf16[3072,5376]{1,0:T(8,128)(2,1)} %all-gather.14.cloned.1.call-done.a_ref.refs_0_, bf16[3072,5376]{1,0:T(8,128)(2,1)} %all-gather.12.cloned.1.call-done.a_ref.refs_1_, bf16[3072,5376]{1,0:T(8,128)(2,1)} %all-gather.8.cloned.1.call-done.a_ref.refs_2_, ...), custom_call_target="tpu_custom_call" | custom-call | flops 101468602368 | bytes 117964800 | tf_op jit(solution)/shard_map/grad_w/pallas_call | solution.py:205
  1604.6 46.5 %reduce-scatter.6.cloned.1.call-done.dn_ref = bf16[384,5376]{1,0:T(8,128)(2,1)} async-done(((bf16[3072,5376]{1,0:T(8,128)(2,1)}), bf16[384,5376]{1,0:T(8,128)(2,1)}) %reduce-scatter.6.cloned.1.call-update) | async-done | bytes 4128784 | tf_op jit(solution)/shard_map/reduce_scatter | solution.py:538
  1668.7 180.7 %reduce-scatter.4.cloned.1.call-done.dn_ref = bf16[384,5376]{1,0:T(8,128)(2,1)} async-done(((bf16[3072,5376]{1,0:T(8,128)(2,1)}), bf16[384,5376]{1,0:T(8,128)(2,1)}) %reduce-scatter.4.cloned.1.call-update) | async-done | bytes 4128784 | tf_op jit(solution)/shard_map/reduce_scatter | solution.py:538
  (195 shorter events, 407.0 us)
Async XLA Ops:
  7.2 167.7 %all-gather.14.cloned.1.call-start = ((), (), s32[]{:S(2)}) async-start(), calls=%async_computation.9 | async-start | bytes 37158912 | tf_op jit(solution)/shard_map/all_gather | solution.py:501
  18.7 392.1 %all-gather.10.cloned.1.call-start = ((), (), s32[]{:S(2)}) async-start(), calls=%async_computation.7 | async-start | bytes 49545216 | tf_op jit(solution)/shard_map/all_gather | solution.py:503
  19.5 546.6 %all-gather.12.cloned.1.call-start = ((), (), s32[]{:S(2)}) async-start(), calls=%async_computation.8 | async-start | bytes 37158912 | tf_op jit(solution)/shard_map/all_gather | solution.py:501
  30.5 739.6 %all-gather.8.cloned.1.call-start = ((), (), s32[]{:S(2)}) async-start(), calls=%async_computation.6 | async-start | bytes 37158912 | tf_op jit(solution)/shard_map/all_gather | solution.py:501
  57.9 160.3 %copy-start.29 = (s32[1,3072]{1,0:T(1,128)}, s32[1,3072]{1,0:T(1,128)S(1)}, u32[]{:S(2)}) copy-start(s32[1,3072]{1,0:T(1,128)S(1)} %get-tuple-element.76.pos_ref) | copy-start | bytes 36868
  58.8 159.4 %copy-start.31 = (s32[12]{0:T(128)}, s32[12]{0:T(128)S(1)}, u32[]{:S(2)}) copy-start(s32[12]{0:T(128)S(1)} %get-tuple-element.88.first_ref) | copy-start | bytes 148
  218.3 52.2 %copy-start.16 = (s32[3072,128]{1,0:T(8,128)}, s32[3072,128]{1,0:T(8,128)S(1)}, u32[]{:S(2)}) copy-start(s32[3072,128]{1,0:T(8,128)S(1)} %broadcast_in_dim.14.key_pos_ref) | copy-start | bytes 4718596
  270.4 74.4 %all-to-all-start.2 = ((bf16[8,384,512]{2,1,0:T(8,128)(2,1)}), bf16[8,384,512]{2,1,0:T(8,128)(2,1)S(1)}, u32[]{:S(2)}, u32[]{:S(2)}) async-start(bf16[8,384,512]{2,1,0:T(8,128)(2,1)} %bitcast.60), calls=%async_computation.2 | async-start | bytes 6291456 | tf_op jit(solution)/shard_map/all_to_all | solution.py:524
  272.9 694.9 %all-gather.20.cloned.1.call-start = ((), (), s32[]{:S(2)}) async-start(), calls=%async_computation.14 | async-start | bytes 37158912 | tf_op jit(solution)/shard_map/all_gather | solution.py:527
  452.8 648.7 %all-gather.18.cloned.1.call-start = ((), (), s32[]{:S(2)}) async-start(), calls=%async_computation.12 | async-start | bytes 37158912 | tf_op jit(solution)/shard_map/all_gather | solution.py:527
  609.1 42.9 %copy-start.18 = (s32[3072,128]{1,0:T(8,128)}, s32[3072,128]{1,0:T(8,128)S(1)}, u32[]{:S(2)}) copy-start(s32[3072,128]{1,0:T(8,128)S(1)} %broadcast_in_dim.13.key_pos_ref) | copy-start | bytes 4718596
  652.0 97.9 %slice-start = ((s8[12386304]{0:T(1024)(128)(4,1)}), s8[4194304]{0:T(1024)(128)(4,1)S(1)}, s32[]{:S(2)}) async-start(s8[12386304]{0:T(1024)(128)(4,1)} %bitcast.41), calls=%async_computation.16 | async-start | bytes 8388608
  763.3 491.0 %all-gather.16.cloned.1.call-start = ((), (), s32[]{:S(2)}) async-start(), calls=%async_computation.10 | async-start | bytes 37158912 | tf_op jit(solution)/shard_map/all_gather | solution.py:527
  770.1 42.5 %copy-start.27 = (s32[1,3072]{1,0:T(1,128)S(1)}, s32[1,3072]{1,0:T(1,128)}, u32[]{:S(2)}) copy-start(s32[1,3072]{1,0:T(1,128)} %copy-done.26) | copy-start | bytes 36868
  813.0 43.3 %copy-start.20 = (s32[3072,128]{1,0:T(8,128)}, s32[3072,128]{1,0:T(8,128)S(1)}, u32[]{:S(2)}) copy-start(s32[3072,128]{1,0:T(8,128)S(1)} %broadcast_in_dim.11.key_pos_ref) | copy-start | bytes 4718596
  856.3 97.9 %slice-start.3 = ((s8[12386304]{0:T(1024)(128)(4,1)}), s8[4194304]{0:T(1024)(128)(4,1)S(1)}, s32[]{:S(2)}) async-start(s8[12386304]{0:T(1024)(128)(4,1)} %bitcast.43), calls=%async_computation.19 | async-start | bytes 8388608
  967.3 620.0 %reduce-scatter.8.cloned.1.call-start = ((), (), s32[]{:S(2)}) async-start(), calls=%async_computation.15 | async-start | bytes 37158912 | tf_op jit(solution)/shard_map/reduce_scatter | solution.py:538
  1101.2 550.0 %reduce-scatter.6.cloned.1.call-start = ((), (), s32[]{:S(2)}) async-start(), calls=%async_computation.13 | async-start | bytes 37158912 | tf_op jit(solution)/shard_map/reduce_scatter | solution.py:538
  1226.9 52.4 %copy-start.21 = (s32[3072,128]{1,0:T(8,128)S(1)}, s32[3072,128]{1,0:T(8,128)}, u32[]{:S(2)}) copy-start(s32[3072,128]{1,0:T(8,128)} %copy-done.20) | copy-start | bytes 4718596
  1226.9 52.4 %copy-start.28 = (s32[1,3072]{1,0:T(1,128)S(1)}, s32[1,3072]{1,0:T(1,128)}, u32[]{:S(2)}) copy-start(s32[1,3072]{1,0:T(1,128)} %copy-done.26) | copy-start | bytes 36868
  1227.0 52.4 %copy-start.42 = (bf16[3072,256]{1,0:T(8,128)(2,1)S(1)}, bf16[3072,256]{1,0:T(8,128)(2,1)}, u32[]{:S(2)}) copy-start(bf16[3072,256]{1,0:T(8,128)(2,1)} %get-tuple-element.42.k_ref) | copy-start | bytes 4718596
  1227.0 622.4 %reduce-scatter.4.cloned.1.call-start = ((), (), s32[]{:S(2)}) async-start(), calls=%async_computation.11 | async-start | bytes 37158912 | tf_op jit(solution)/shard_map/reduce_scatter | solution.py:538
  1457.5 129.9 %copy-start.23 = (f32[1,5376]{1,0:T(1,128)S(1)}, f32[1,5376]{1,0:T(1,128)}, u32[]{:S(2)}) copy-start(f32[1,5376]{1,0:T(1,128)} %copy-done.22) | copy-start | bytes 64516
  1457.5 129.9 %copy-start.25 = (f32[1,5376]{1,0:T(1,128)S(1)}, f32[1,5376]{1,0:T(1,128)}, u32[]{:S(2)}) copy-start(f32[1,5376]{1,0:T(1,128)} %copy-done.24) | copy-start | bytes 64516
  (49 other events, 435.3 us)
Sparse Core Ops, SparseCore 0:
  18.9 155.9 all-gather.13
  176.7 234.0 all-gather.9
  413.2 152.8 all-gather.11
  568.4 186.5 all-gather.7
  757.2 186.5 all-gather.19
  946.1 152.8 all-gather.17
  1101.4 152.8 all-gather.15
  1258.0 194.6 reduce-scatter.7
  1456.4 194.6 reduce-scatter.5
  1654.7 194.6 reduce-scatter.3

commit v2 on v1

--- a/solution.py
+++ b/solution.py
@@ -65,7 +65,7 @@
         in_specs=[whole, vec],
         out_specs=one,
         out_shape=jax.ShapeDtypeStruct((rows, depth), jnp.bfloat16),
-        compiler_params=pltpu.CompilerParams(vmem_limit_bytes=32 * 1024 * 1024),
+        compiler_params=pltpu.CompilerParams(vmem_limit_bytes=54 * 1024 * 1024),
         cost_estimate=pl.CostEstimate(flops=rows * depth * 400, bytes_accessed=4 * rows * depth, transcendentals=rows),
         name="pre_norm",
     )(x_in, gain)
@@ -113,13 +113,14 @@
         ],
         scratch_shapes=[pltpu.VMEM((8, depth), jnp.float32)],
         input_output_aliases={} if first else {5: 0},
-        compiler_params=pltpu.CompilerParams(vmem_limit_bytes=32 * 1024 * 1024),
+        compiler_params=pltpu.CompilerParams(vmem_limit_bytes=54 * 1024 * 1024),
         cost_estimate=pl.CostEstimate(flops=rows * depth * 800, bytes_accessed=10 * rows * depth, transcendentals=rows),
         name="post_norm",
     )(proj, x_in, grad_out, gain, dg_in, *([] if first else [y_prev]))
 
 
-def pre_grad_kernel(first, dn_ref, x_ref, go_ref, gain_ref, dg_in_ref, *refs):
+def pre_grad_kernel(first, *refs):
+    pieces, (x_ref, go_ref, gain_ref, dg_in_ref), refs = refs[:6], refs[6:10], refs[10:]
     gx_ref, dg_ref, dg_scr = refs[0 if first else 1:]
     step = pl.program_id(0)
     gain = 1.0 + gain_ref[...]
@@ -133,7 +134,10 @@
         rows = pl.ds(pl.multiple_of(c * CHUNK, CHUNK), CHUNK)
         values = x_ref[0, rows, :].astype(jnp.float32)
         inv = inverse_rms(values)
-        d_out = dn_ref[rows, :].astype(jnp.float32)
+        halves = []
+        for kept, near, far in (pieces[:3], pieces[3:]):
+            halves.append(kept[0, rows, :].astype(jnp.float32) + near[0, rows, :].astype(jnp.float32) + far[rows, :].astype(jnp.float32))
+        d_out = jnp.concatenate(halves, axis=1)
         dg_scr[...] += fold_rows(d_out * (values * inv))
         d_x = norm_grad(values, inv, d_out, gain).astype(jnp.bfloat16).astype(jnp.float32)
         gx_ref[0, rows, :] = (go_ref[0, rows, :].astype(jnp.float32) + d_x).astype(gx_ref.dtype)
@@ -143,22 +147,24 @@
         dg_ref[...] = dg_in_ref[...] + jnp.sum(dg_scr[...], axis=0, keepdims=True)
 
 
-def pre_grad(d_normed, x_in, grad_out, gain, dg_in, gx_prev, seq):
+def pre_grad(pieces, x_in, grad_out, gain, dg_in, gx_prev, seq):
     _, rows, depth = x_in.shape
-    whole, one, vec = row_specs(seq, depth)
+    whole, _, vec = row_specs(seq, depth)
+    pair = pl.BlockSpec((1, ROWS, depth // 2), lambda i: (0, i, 0))
+    one = pl.BlockSpec((ROWS, depth // 2), lambda i: (i, 0))
     first = gx_prev is None
     return pl.pallas_call(
         functools.partial(pre_grad_kernel, first),
         grid=(rows // ROWS,),
-        in_specs=[one, whole, whole, vec, vec] + ([] if first else [pl.BlockSpec(memory_space=pl.ANY)]),
+        in_specs=[pair, pair, one, pair, pair, one, whole, whole, vec, vec] + ([] if first else [pl.BlockSpec(memory_space=pl.ANY)]),
         out_specs=[whole, vec],
         out_shape=[jax.ShapeDtypeStruct(x_in.shape, jnp.bfloat16), jax.ShapeDtypeStruct((1, depth), jnp.float32)],
         scratch_shapes=[pltpu.VMEM((8, depth), jnp.float32)],
-        input_output_aliases={} if first else {5: 0},
-        compiler_params=pltpu.CompilerParams(vmem_limit_bytes=32 * 1024 * 1024),
-        cost_estimate=pl.CostEstimate(flops=rows * depth * 700, bytes_accessed=8 * rows * depth, transcendentals=rows),
+        input_output_aliases={} if first else {10: 0},
+        compiler_params=pltpu.CompilerParams(vmem_limit_bytes=54 * 1024 * 1024),
+        cost_estimate=pl.CostEstimate(flops=rows * depth * 700, bytes_accessed=12 * rows * depth, transcendentals=rows),
         name="pre_grad",
-    )(d_normed, x_in, grad_out, gain, dg_in, *([] if first else [gx_prev]))
+    )(*pieces, x_in, grad_out, gain, dg_in, *([] if first else [gx_prev]))
 
 
 def out_proj_kernel(o_ref, w_ref, r_ref):
@@ -179,10 +185,124 @@
         ],
         out_specs=pl.BlockSpec((rows, tile), lambda i: (0, i)),
         out_shape=jax.ShapeDtypeStruct((rows, depth), jnp.bfloat16),
-        compiler_params=pltpu.CompilerParams(vmem_limit_bytes=40 * 1024 * 1024),
+        compiler_params=pltpu.CompilerParams(vmem_limit_bytes=54 * 1024 * 1024),
         cost_estimate=pl.CostEstimate(flops=2 * n_dev * rows * cols * depth, bytes_accessed=2 * n_dev * cols * depth, transcendentals=0),
         name="out_proj",
     )(o_mine, w_all)
+
+
+def pair_core_kernel(dst_ref, d_ref, w_ref, out_ref):
+    out_ref[0] = jnp.dot(d_ref[...], w_ref[...], preferred_element_type=jnp.float32).astype(out_ref.dtype)
+
+
+def grad_normed_pair(dst, d_lin, w_t, rows):
+    cols, depth = w_t.shape
+    half = depth // 2
+    return pl.pallas_call(
+        pair_core_kernel,
+        grid_spec=pltpu.PrefetchScalarGridSpec(
+            num_scalar_prefetch=1,
+            grid=(2, 4),
+            in_specs=[
+                pl.BlockSpec((rows, cols), lambda h, r, dst: (dst[0] ^ (2 * r), 0)),
+                pl.BlockSpec((cols, half), lambda h, r, dst: (0, h)),
+            ],
+            out_specs=pl.BlockSpec((1, rows, half), lambda h, r, dst: (r, 0, h)),
+        ),
+        out_shape=jax.ShapeDtypeStruct((4, rows, depth), jnp.bfloat16),
+        compiler_params=pltpu.CompilerParams(vmem_limit_bytes=48 * 1024 * 1024),
+        cost_estimate=pl.CostEstimate(flops=8 * rows * cols * depth, bytes_accessed=2 * (4 * rows * depth + cols * depth), transcendentals=0),
+        name="grad_normed_pair",
+    )(dst, d_lin, w_t)
+
+
+def route(h, j):
+    return jnp.where(h == 0, (2 * j + 1) % 5, (j + 2) % 4)
+
+
+def own_core_kernel(dst_ref, d_ref, w_ref, add_ref, *outs):
+    step = 4 * pl.program_id(0) + pl.program_id(1)
+    value = jnp.dot(d_ref[...], w_ref[...], preferred_element_type=jnp.float32) + add_ref[0].astype(jnp.float32)
+    value = value.astype(jnp.bfloat16)
+    for i, out in enumerate(outs):
+        @pl.when((step >= 2 * i) & (step < 2 * i + 2))
+        def _(out=out):
+            out[0] = value
+
+
+def grad_normed_own(dst, d_lin, w_t, from_pair):
+    _, rows, depth = from_pair.shape
+    cols = w_t.shape[0]
+    half = depth // 2
+    outs = [pl.BlockSpec((1, rows, half), lambda h, j, dst, i=i: (jnp.clip(4 * h + j - 2 * i, 0, 1), 0, 0)) for i in range(4)]
+    return pl.pallas_call(
+        own_core_kernel,
+        grid_spec=pltpu.PrefetchScalarGridSpec(
+            num_scalar_prefetch=1,
+            grid=(2, 4),
+            in_specs=[
+                pl.BlockSpec((rows, cols), lambda h, j, dst: (dst[0] ^ (2 * route(h, j)), 0)),
+                pl.BlockSpec((cols, half), lambda h, j, dst: (0, h)),
+                pl.BlockSpec((1, rows, half), lambda h, j, dst: (route(h, j), 0, h)),
+            ],
+            out_specs=outs,
+        ),
+        out_shape=[jax.ShapeDtypeStruct((2, rows, half), jnp.bfloat16)] * 4,
+        compiler_params=pltpu.CompilerParams(vmem_limit_bytes=56 * 1024 * 1024),
+        cost_estimate=pl.CostEstimate(flops=8 * rows * cols * depth, bytes_accessed=2 * (8 * rows * depth + cols * depth), transcendentals=0),
+        name="grad_normed_own",
+    )(dst, d_lin, w_t, from_pair)
+
+
+def gain_sum_kernel(n_dev, pre_ref, post_ref, pre_out, post_out, slots, local_sem, send_sem, recv_sem):
+    me = lax.axis_index('tp')
+    sources = (pre_ref, post_ref)
+    sends, locals_ = [], []
+    for off in range(1, n_dev):
+        for which, src in enumerate(sources):
+            copy = pltpu.make_async_remote_copy(
+                src_ref=src, dst_ref=slots.at[which, me], send_sem=send_sem.at[which, off], recv_sem=recv_sem.at[which, me],
+                device_id={'tp': lax.rem(me + off, n_dev)}, device_id_type=pl.DeviceIdType.MESH)
+            copy.start()
+            sends.append(copy)
+    for which, src in enumerate(sources):
+        copy = pltpu.make_async_copy(src, slots.at[which, me], local_sem.at[which])
+        copy.start()
+        locals_.append(copy)
+    for copy in locals_:
+        copy.wait()
+    for off in range(1, n_dev):
+        other = lax.rem(me + off, n_dev)
+        for which, src in enumerate(sources):
+            pltpu.make_async_remote_copy(
+                src_ref=src, dst_ref=slots.at[which, other], send_sem=send_sem.at[which, off], recv_sem=recv_sem.at[which, other],
+                device_id={'tp': other}, device_id_type=pl.DeviceIdType.MESH).wait_recv()
+    for copy in sends:
+        copy.wait_send()
+    for which, out in enumerate((pre_out, post_out)):
+        total = slots[which, 0]
+        for d in range(1, n_dev):
+            total = total + slots[which, d]
+        out[...] = total
+
+
+def gain_sum(d_pre, d_post, n_dev):
+    depth = d_pre.shape[1]
+    vmem = pl.BlockSpec(memory_space=pltpu.VMEM)
+    return pl.pallas_call(
+        functools.partial(gain_sum_kernel, n_dev),
+        in_specs=[vmem, vmem],
+        out_specs=[vmem, vmem],
+        out_shape=[jax.ShapeDtypeStruct((1, depth), jnp.float32)] * 2,
+        scratch_shapes=[
+            pltpu.VMEM((2, n_dev, 1, depth), jnp.float32),
+            pltpu.SemaphoreType.DMA((2,)),
+            pltpu.SemaphoreType.DMA((2, n_dev)),
+            pltpu.SemaphoreType.DMA((2, n_dev)),
+        ],
+        compiler_params=pltpu.CompilerParams(has_side_effects=True),
+        name="gain_sum",
+    )(d_pre, d_post)
 
 
 def grad_w_kernel(n_rows, head_dim, *refs):
@@ -197,16 +317,16 @@
             col += head_dim
 
 
-def grad_w(normed, d_lin, heads, head_dim):
+def grad_w(normed, d_lin, heads, head_dim, col_blk):
     seq_len, depth = normed[0].shape
-    cols = d_lin[0].shape[1]
+    cols = sum(heads) * head_dim
     n_rows = len(normed)
-    tile = 256
+    tile = 384
     return pl.pallas_call(
         functools.partial(grad_w_kernel, n_rows, head_dim),
         grid=(depth // tile,),
         in_specs=[pl.BlockSpec((seq_len, tile), lambda i: (0, i))] * n_rows
-        + [pl.BlockSpec((seq_len, cols), lambda i: (0, 0), pipeline_mode=pl.Buffered(1))] * n_rows,
+        + [pl.BlockSpec((seq_len, cols), lambda i: (0, col_blk), pipeline_mode=pl.Buffered(1))] * n_rows,
         out_specs=[pl.BlockSpec((tile, h, head_dim), lambda i: (i, 0, 0)) for h in heads],
         out_shape=[jax.ShapeDtypeStruct((depth, h, head_dim), jnp.float32) for h in heads],
         compiler_params=pltpu.CompilerParams(vmem_limit_bytes=58 * 1024 * 1024),
@@ -489,6 +609,7 @@
 
     def local_body(x_in, positions, grad_out, w_query, w_key, w_value, w_out, gain_pre, gain_post):
         n_rows, _, depth = x_in.shape
+        n_dev = mesh.shape['tp']
         heads_loc, head_dim = w_query.shape[1], w_query.shape[2]
         kv_loc = w_key.shape[1]
         groups = heads_loc // kv_loc
@@ -521,11 +642,18 @@
             key_pos = jnp.broadcast_to(pos_all[b][:, None], (seq_len, LANES))
             q_b, k_b, v_b = qkv_project(normed_all[b], w_all, cos_t, sin_t, q_cols, k_cols, head_dim)
             o_b, lse_b = attn_fwd(q_b, k_b, v_b, pos_b, key_pos, first_blk[b], groups, head_dim)
-            o_mine = lax.all_to_all(o_b.reshape(-1, seq_len // mesh.shape['tp'], q_cols), 'tp', split_axis=0, concat_axis=0, tiled=True)
+            o_mine = lax.all_to_all(o_b.reshape(-1, seq_len // n_dev, q_cols), 'tp', split_axis=0, concat_axis=0, tiled=True)
             proj = out_proj(o_mine, w_out_all)
             y_out, d_proj, d_post = post_norm(proj, x_in, grad_out, gain_post_row, d_post, y_out, b)
             d_proj_all.append(lax.all_gather(d_proj, 'tp', axis=0, tiled=True))
             saved.append((q_b, k_b, v_b, o_b, pos_b, key_pos, lse_b, cos_t, sin_t))
+
+        me = lax.axis_index('tp')
+        own_dst, pair_dst = me[None], me[None] ^ 1
+        w_t = w_all.T
+
+        def swap(value, bit):
+            return lax.ppermute(value, 'tp', [(d, d ^ bit) for d in range(n_dev)])
 
         grad_x, d_pre = None, jnp.zeros((1, depth), jnp.float32)
         grad_wo = jnp.zeros((), jnp.float32)
@@ -534,14 +662,22 @@
             q_b, k_b, v_b, o_b, pos_b, key_pos, lse_b, cos_t, sin_t = saved[b]
             d_o = dot_f32(d_proj_all[b], w_out_loc, 1, 1).astype(jnp.bfloat16)
             d_lin.append(attn_bwd(q_b, k_b, v_b, o_b, d_o, pos_b, key_pos, lse_b, first_blk[b], cos_t, sin_t, groups, head_dim))
-            d_normed = dot_f32(d_lin[b], w_all, 1, 1).astype(jnp.bfloat16)
-            d_normed_loc = lax.psum_scatter(d_normed, 'tp', scatter_dimension=0, tiled=True)
-            grad_x, d_pre = pre_grad(d_normed_loc, x_in, grad_out, gain_pre_row, d_pre, grad_x, b)
+            pair = grad_normed_pair(pair_dst, d_lin[b], w_t, seq_len // n_dev)
+            from_pair = swap(pair, 1)
+            send_x, keep_x, send_y, keep_y = grad_normed_own(own_dst, d_lin[b], w_t, from_pair)
+            near_x = swap(send_x, 2)
+            near_y = swap(send_y, 4)
+            fold_x = (keep_x[1].astype(jnp.float32) + near_x[1].astype(jnp.float32)).astype(jnp.bfloat16)
+            fold_y = (keep_y[1].astype(jnp.float32) + near_y[1].astype(jnp.float32)).astype(jnp.bfloat16)
+            far_x = swap(fold_x, 4)
+            far_y = swap(fold_y, 2)
+            grad_x, d_pre = pre_grad((keep_x, near_x, far_x, keep_y, near_y, far_y), x_in, grad_out, gain_pre_row, d_pre, grad_x, b)
             grad_wo = grad_wo + dot_f32(o_b, d_proj_all[b], 0, 0)
 
-        grad_wq, grad_wk, grad_wv = grad_w(normed_all, d_lin, (heads_loc, kv_loc, kv_loc), head_dim)
-        grad_pre = lax.psum(d_pre[0], 'tp')
-        grad_post = lax.psum(d_post[0], 'tp')
+        grad_wq, = grad_w(normed_all, d_lin, (heads_loc,), head_dim, 0)
+        grad_wk, grad_wv = grad_w(normed_all, d_lin, (kv_loc, kv_loc), head_dim, 1)
+        grad_pre, grad_post = gain_sum(d_pre, d_post, n_dev)
+        grad_pre, grad_post = grad_pre[0], grad_post[0]
         return y_out, grad_x, grad_wq, grad_wk, grad_wv, grad_wo.reshape(w_out.shape), grad_pre, grad_post
 
     return jax.shard_map(local_body, mesh=mesh, in_specs=in_specs, out_specs=out_specs, check_vma=False)

time: 1910 us -> 1990 us (1.042)
  Pallas kernels: 702 us -> 912 us
  matrix products: 285 us -> 152 us
  other arithmetic: 32.8 us -> 59.9 us
  local copies, waits for them, and re-layouts: 85.7 us -> 59.8 us
  blocking collectives: 188 us -> 166 us
    ppermute x0 -> x15, waiting for transfers between devices: none -> 235 us  [swap(): return lax.ppermute(value, 'tp', [(d, d ^ bit) for d in range(n_dev)])]
    reduce_scatter x3 -> x0, waiting for transfers between devices: 227 us -> none  [local_body(): lax.psum_scatter(d_normed, 'tp', scatter_dimension=0, tiled=True)]
    pallas_call x0 -> x7, Pallas kernels: none -> 174 us  [the longest x3 89.3 us: grad_normed_own(): pl.pallas_call(own_core_kernel, grid_spec=pltpu.PrefetchScalarGridSpec(nu...]
    dot_general x9 -> x6, matrix products: 285 us -> 152 us  [dot_f32(): lax.dot_general(lhs, rhs, (((lhs_dim,), (rhs_dim,)), ((), ())), preferred...]
    unnamed x126 -> x101, local copies, waits for them, and re-layouts: 81.4 us -> 41.8 us
    all_gather x3, waiting for transfers between devices: 27.1 us -> 65.7 us  [local_body(): d_proj_all.append(lax.all_gather(d_proj, 'tp', axis=0, tiled=True))]
    all_gather x3, waiting for transfers between devices: 191 us -> 161 us  [local_body(): normed_all.append(lax.all_gather(normed, 'tp', axis=0, tiled=True))]
    psum x1 -> x0, blocking collectives: 23.3 us -> none  [local_body(): grad_pre = lax.psum(d_pre[0], 'tp')]
  transfers between devices with their start and end apart: 11 -> 23, of which waited for: 7 -> 12; matrix products, arithmetic and copies ran while one was open for 17% -> 13% of each run, Pallas kernels for 36% -> 45%
where the time goes in v2:
time: 1990 us; the launch traced here: 1980 us
  Pallas kernels  912 us (46%)
  waiting for transfers between devices  599 us (30%)
  blocking collectives  166 us (8%)
  matrix products  152 us (8%)
  other arithmetic  59.9 us (3%)
  local copies, waits for them, and re-layouts  59.8 us (3%)
    ppermute x15, waiting for transfers between devices, swap(): return lax.ppermute(value, 'tp', [(d, d ^ bit) for d in range(n_dev)])  235 us
    pallas_call x3, Pallas kernels, attn_bwd(): pl.pallas_call(functools.partial(attn_bwd_kernel, groups, head_dim, head_...  170 us
    all_gather x3, waiting for transfers between devices, local_body(): normed_all.append(lax.all_gather(normed, 'tp', axis=0, tiled=True))  161 us
    dot_general x6, matrix products, dot_f32(): lax.dot_general(lhs, rhs, (((lhs_dim,), (rhs_dim,)), ((), ())), preferred...  152 us
    all_to_all x2, blocking collectives, local_body(): lax.all_to_all(o_b.reshape(-1, seq_len // n_dev, q_cols), 'tp', split_axi...  151 us
    pallas_call x2, Pallas kernels, grad_w(): pl.pallas_call(functools.partial(grad_w_kernel, n_rows, head_dim), grid=(...  133 us
    pallas_call x3, Pallas kernels, qkv_project(): pl.pallas_call(functools.partial(qkv_kernel, q_cols, k_cols, head_dim, he...  128 us
    pallas_call x3, Pallas kernels, attn_fwd(): pl.pallas_call(functools.partial(attn_fwd_kernel, groups, head_dim), grid...  128 us
  transfers between devices with their start and end apart: 23, of which 12 were waited for; matrix products, arithmetic and copies ran while one was open for 13% of the time, Pallas kernels for 45%

profile of v2, /device:TPU:0, one launch (start us, length us, event | category | flops | bytes accessed | tf_op | source)
XLA Modules:
  0.0 1978.8 jit_solution(8964844498654589838)
XLA Ops:
  121.6 50.3 %all-gather.14.cloned.1.call-done.a_ref.refs_0_ = bf16[3072,5376]{1,0:T(8,128)(2,1)} async-done(((bf16[384,5376]{1,0:T(8,128)(2,1)}), bf16[3072,5376]{1,0:T(8,128)(2,1)}) %all-gather.14.cloned.1.call-update) | async-done | bytes 33030160 | tf_op jit(solution)/shard_map/all_gather | solution.py:622
  171.8 42.9 %qkv_project.5 = (bf16[3072,512]{1,0:T(8,128)(2,1)}, bf16[3072,256]{1,0:T(8,128)(2,1)}, bf16[3072,256]{1,0:T(8,128)(2,1)}) custom-call(bf16[3072,5376]{1,0:T(8,128)(2,1)} %all-gather.14.cloned.1.call-done.a_ref.refs_0_, bf16[5376,1024]{1,0:T(8,128)(2,1)} %copy.30.w_ref, f32[3072,128]{1,0:T(8,128)} %get-tuple-element.127.cos_ref, ...), custom_call_target="tpu_custom_call" | custom-call | flops 33822867456 | bytes 50331648 | tf_op jit(solution)/shard_map/qkv_project/pallas_call | solution.py:357
  218.6 48.7 %attn_fwd.5 = (bf16[3072,512]{1,0:T(8,128)(2,1)}, f32[2,12,1,512]{3,2,1,0:T(1,128)S(1)}) custom-call(s32[12]{0:T(128)S(1)} %get-tuple-element.114.first_ref, bf16[3072,512]{1,0:T(8,128)(2,1)} %get-tuple-element.62.q_ref, bf16[3072,256]{1,0:T(8,128)(2,1)S(1)} %copy-done.19, bf16[3072,256]{1,0:T(8,128)(2,1)S(1)} %copy-done.21, ...), custom_call_target="tpu_custom_call" | custom-call | flops 9663676416 | bytes 12582912 | tf_op jit(solution)/shard_map/attn_fwd/pallas_call | solution.py:438
  271.5 71.1 %all-to-all-done.2.o_ref = bf16[8,384,512]{2,1,0:T(8,128)(2,1)} async-done(((bf16[8,384,512]{2,1,0:T(8,128)(2,1)}), bf16[8,384,512]{2,1,0:T(8,128)(2,1)}, u32[]{:S(2)}, u32[]{:S(2)}) %all-to-all-start.2) | async-done | bytes 3145760 | tf_op jit(solution)/shard_map/all_to_all | solution.py:645
  342.6 65.1 %all-gather.10.cloned.1.call-done.w_ref = bf16[4096,5376]{1,0:T(8,128)(2,1)} async-done(((bf16[512,5376]{1,0:T(8,128)(2,1)}), bf16[4096,5376]{1,0:T(8,128)(2,1)}) %all-gather.10.cloned.1.call-update) | async-done | bytes 44040208 | tf_op jit(solution)/shard_map/all_gather | solution.py:624
  451.3 111.2 %all-gather.12.cloned.1.call-done.a_ref.refs_1_ = bf16[3072,5376]{1,0:T(8,128)(2,1)} async-done(((bf16[384,5376]{1,0:T(8,128)(2,1)}), bf16[3072,5376]{1,0:T(8,128)(2,1)}) %all-gather.12.cloned.1.call-update) | async-done | bytes 33030160 | tf_op jit(solution)/shard_map/all_gather | solution.py:622
  562.5 42.6 %qkv_project.4 = (bf16[3072,512]{1,0:T(8,128)(2,1)}, bf16[3072,256]{1,0:T(8,128)(2,1)}, bf16[3072,256]{1,0:T(8,128)(2,1)}) custom-call(bf16[3072,5376]{1,0:T(8,128)(2,1)} %all-gather.12.cloned.1.call-done.a_ref.refs_1_, bf16[5376,1024]{1,0:T(8,128)(2,1)} %copy.30.w_ref, f32[3072,128]{1,0:T(8,128)} %get-tuple-element.125.cos_ref, ...), custom_call_target="tpu_custom_call" | custom-call | flops 33822867456 | bytes 50331648 | tf_op jit(solution)/shard_map/qkv_project/pallas_call | solution.py:357
  608.9 39.5 %attn_fwd.4 = (bf16[3072,512]{1,0:T(8,128)(2,1)}, f32[2,12,1,512]{3,2,1,0:T(1,128)S(1)}) custom-call(s32[12]{0:T(128)S(1)} %get-tuple-element.115.first_ref, bf16[3072,512]{1,0:T(8,128)(2,1)} %get-tuple-element.58.q_ref, bf16[3072,256]{1,0:T(8,128)(2,1)S(1)} %copy-done.23, bf16[3072,256]{1,0:T(8,128)(2,1)S(1)} %copy-done.25, ...), custom_call_target="tpu_custom_call" | custom-call | flops 9663676416 | bytes 12582912 | tf_op jit(solution)/shard_map/attn_fwd/pallas_call | solution.py:438
  648.4 75.2 %all_to_all.15.o_ref = bf16[8,384,512]{2,1,0:T(8,128)(2,1)} all-to-all(bf16[8,384,512]{2,1,0:T(8,128)(2,1)} %bitcast.59), channel_id=1, replica_groups=mesh['dp'=1,'tp'=8] {'tp'}, dimensions={0} | all-to-all | bytes 6291456 | tf_op jit(solution)/shard_map/all_to_all | solution.py:645
  768.3 42.4 %qkv_project.3 = (bf16[3072,512]{1,0:T(8,128)(2,1)}, bf16[3072,256]{1,0:T(8,128)(2,1)}, bf16[3072,256]{1,0:T(8,128)(2,1)}) custom-call(bf16[3072,5376]{1,0:T(8,128)(2,1)} %all-gather.8.cloned.1.call-done.a_ref.refs_2_, bf16[5376,1024]{1,0:T(8,128)(2,1)} %copy.30.w_ref, f32[3072,128]{1,0:T(8,128)} %get-tuple-element.123.cos_ref, ...), custom_call_target="tpu_custom_call" | custom-call | flops 33822867456 | bytes 50331648 | tf_op jit(solution)/shard_map/qkv_project/pallas_call | solution.py:357
  815.3 39.6 %attn_fwd.3 = (bf16[3072,512]{1,0:T(8,128)(2,1)}, f32[2,12,1,512]{3,2,1,0:T(1,128)S(1)}) custom-call(s32[12]{0:T(128)S(1)} %get-tuple-element.116.first_ref, bf16[3072,512]{1,0:T(8,128)(2,1)} %get-tuple-element.54.q_ref, bf16[3072,256]{1,0:T(8,128)(2,1)S(1)} %copy-done.27, bf16[3072,256]{1,0:T(8,128)(2,1)S(1)} %copy-done.29, s32[1,3072]{1,0:T(1,128)S(1)} %copy-done.7, ...), custom_call_target="tpu_custom_call" | custom-call | flops 9663676416 | bytes 12582912 | tf_op jit(solution)/shard_map/attn_fwd/pallas_call | solution.py:438
  854.9 75.5 %all_to_all.16.o_ref = bf16[8,384,512]{2,1,0:T(8,128)(2,1)} all-to-all(bf16[8,384,512]{2,1,0:T(8,128)(2,1)} %bitcast.50), channel_id=1, replica_groups=mesh['dp'=1,'tp'=8] {'tp'}, dimensions={0} | all-to-all | bytes 6291456 | tf_op jit(solution)/shard_map/all_to_all | solution.py:645
  993.8 63.6 %attn_bwd.5.d_ref.refs_3_ = bf16[3072,1024]{1,0:T(8,128)(2,1)} custom-call(s32[12]{0:T(128)S(1)} %copy-done.18, bf16[3072,512]{1,0:T(8,128)(2,1)} %get-tuple-element.62.q_ref, bf16[3072,256]{1,0:T(8,128)(2,1)S(1)} %copy-done.20, bf16[3072,256]{1,0:T(8,128)(2,1)S(1)} %copy-done.22, bf16[3072,512]{1,0:T(8,128)(2,1)} %get-tuple-element.65.o_ref, ...), custom_call_target="tpu_custom_call" | custom-call | flops 24159191040 | bytes 25165824 | tf_op jit(solution)/shard_map/attn_bwd/pallas_call | solution.py:572
  1121.4 53.5 %attn_bwd.4.d_ref.refs_4_ = bf16[3072,1024]{1,0:T(8,128)(2,1)} custom-call(s32[12]{0:T(128)S(1)} %copy-done.16, bf16[3072,512]{1,0:T(8,128)(2,1)} %get-tuple-element.58.q_ref, bf16[3072,256]{1,0:T(8,128)(2,1)S(1)} %copy-done.24, bf16[3072,256]{1,0:T(8,128)(2,1)S(1)} %copy-done.26, bf16[3072,512]{1,0:T(8,128)(2,1)} %get-tuple-element.61.o_ref, ...), custom_call_target="tpu_custom_call" | custom-call | flops 24159191040 | bytes 25165824 | tf_op jit(solution)/shard_map/attn_bwd/pallas_call | solution.py:572
  1200.2 52.1 %all-gather.16.cloned.1.call-done = bf16[3072,5376]{1,0:T(8,128)(2,1)} async-done(((bf16[384,5376]{1,0:T(8,128)(2,1)}), bf16[3072,5376]{1,0:T(8,128)(2,1)}) %all-gather.16.cloned.1.call-update) | async-done | bytes 33030160 | tf_op jit(solution)/shard_map/all_gather | solution.py:648
  1276.7 53.2 %attn_bwd.3.d_ref.refs_5_ = bf16[3072,1024]{1,0:T(8,128)(2,1)} custom-call(s32[12]{0:T(128)S(1)} %copy-done.14, bf16[3072,512]{1,0:T(8,128)(2,1)} %get-tuple-element.54.q_ref, bf16[3072,256]{1,0:T(8,128)(2,1)S(1)} %copy-done.28, bf16[3072,256]{1,0:T(8,128)(2,1)S(1)} %copy-done.30, bf16[3072,512]{1,0:T(8,128)(2,1)} %get-tuple-element.57.o_ref, ...), custom_call_target="tpu_custom_call" | custom-call | flops 24159191040 | bytes 25165824 | tf_op jit(solution)/shard_map/attn_bwd/pallas_call | solution.py:572
  1379.9 66.5 %grad_w.2 = f32[5376,4,128]{2,1,0:T(4,128)} custom-call(bf16[3072,5376]{1,0:T(8,128)(2,1)} %all-gather.14.cloned.1.call-done.a_ref.refs_0_, bf16[3072,5376]{1,0:T(8,128)(2,1)} %all-gather.12.cloned.1.call-done.a_ref.refs_1_, bf16[3072,5376]{1,0:T(8,128)(2,1)} %all-gather.8.cloned.1.call-done.a_ref.refs_2_, bf16[3072,1024]{1,0:T(8,128)(2,1)} %attn_bwd.5.d_ref.refs_3_, ...), custom_call_target="tpu_custom_call" | custom-call | flops 50734301184 | bytes 108527616 | tf_op jit(solution)/shard_map/grad_w/pallas_call | solution.py:325
  1446.4 66.2 %grad_w.3 = (f32[5376,2,128]{2,1,0:T(2,128)}, f32[5376,2,128]{2,1,0:T(2,128)}) custom-call(bf16[3072,5376]{1,0:T(8,128)(2,1)} %all-gather.14.cloned.1.call-done.a_ref.refs_0_, bf16[3072,5376]{1,0:T(8,128)(2,1)} %all-gather.12.cloned.1.call-done.a_ref.refs_1_, bf16[3072,5376]{1,0:T(8,128)(2,1)} %all-gather.8.cloned.1.call-done.a_ref.refs_2_, ...), custom_call_target="tpu_custom_call" | custom-call | flops 50734301184 | bytes 108527616 | tf_op jit(solution)/shard_map/grad_w/pallas_call | solution.py:325
  1512.6 30.1 %grad_normed_own.5 = (bf16[2,384,2688]{2,1,0:T(8,128)(2,1)}, bf16[2,384,2688]{2,1,0:T(8,128)(2,1)}, bf16[2,384,2688]{2,1,0:T(8,128)(2,1)}, bf16[2,384,2688]{2,1,0:T(8,128)(2,1)}) custom-call(s32[1]{0:T(128)} %bitcast.13.dst_ref, bf16[3072,1024]{1,0:T(8,128)(2,1)} %attn_bwd.5.d_ref.refs_3_, bf16[1024,5376]{1,0:T(8,128)(2,1)} %get-tuple-element.100.w_ref, ...), custom_call_target="tpu_custom_call" | custom-call | flops 16911433728 | bytes 44040192 | tf_op jit(solution)/shard_map/grad_normed_own/pallas_call | solution.py:238
  1576.3 29.6 %grad_normed_own.3 = (bf16[2,384,2688]{2,1,0:T(8,128)(2,1)}, bf16[2,384,2688]{2,1,0:T(8,128)(2,1)}, bf16[2,384,2688]{2,1,0:T(8,128)(2,1)}, bf16[2,384,2688]{2,1,0:T(8,128)(2,1)}) custom-call(s32[1]{0:T(128)} %bitcast.13.dst_ref, bf16[3072,1024]{1,0:T(8,128)(2,1)} %attn_bwd.3.d_ref.refs_5_, bf16[1024,5376]{1,0:T(8,128)(2,1)} %get-tuple-element.100.w_ref, ...), custom_call_target="tpu_custom_call" | custom-call | flops 16911433728 | bytes 44040192 | tf_op jit(solution)/shard_map/grad_normed_own/pallas_call | solution.py:238
  1641.1 82.4 %collective-permute-done.6.refs_1_ = bf16[2,384,2688]{2,1,0:T(8,128)(2,1)S(1)} collective-permute-done((bf16[2,384,2688]{2,1,0:T(8,128)(2,1)}, bf16[2,384,2688]{2,1,0:T(8,128)(2,1)S(1)}, u32[]{:S(2)}, u32[]{:S(2)}) %collective-permute-start.6) | collective-permute-done | bytes 4128800 | tf_op jit(solution)/shard_map/ppermute | solution.py:656
  1731.0 80.9 %collective-permute-done.1.refs_1_ = bf16[2,384,2688]{2,1,0:T(8,128)(2,1)S(1)} collective-permute-done((bf16[2,384,2688]{2,1,0:T(8,128)(2,1)}, bf16[2,384,2688]{2,1,0:T(8,128)(2,1)S(1)}, u32[]{:S(2)}, u32[]{:S(2)}) %collective-permute-start.1) | collective-permute-done | bytes 4128800 | tf_op jit(solution)/shard_map/ppermute | solution.py:656
  1817.7 40.0 %collective-permute-done.12.refs_2_ = bf16[384,2688]{1,0:T(8,128)(2,1)S(1)} collective-permute-done((bf16[384,2688]{1,0:T(8,128)(2,1)S(1)}, bf16[384,2688]{1,0:T(8,128)(2,1)S(1)}, u32[]{:S(2)}, u32[]{:S(2)}) %collective-permute-start.12) | collective-permute-done | bytes 2064416 | tf_op jit(solution)/shard_map/ppermute | solution.py:656
  1859.5 29.7 %add_add_fusion = f32[512,5376]{1,0:T(8,128)} fusion(f32[512,5376]{1,0:T(8,128)} %fusion.13, f32[512,5376]{1,0:T(8,128)} %fusion.14, bf16[3072,512]{1,0:T(8,128)(2,1)S(1)} %copy-done.31, bf16[3072,5376]{1,0:T(8,128)(2,1)} %all-gather.16.cloned.1.call-done), kind=kOutput, calls=%fused_computation.1 | convolution fusion | flops 16916938752 | bytes 69206016 | tf_op jit(solution)/shard_map/dot_general | solution.py:21
  (199 shorter events, 612.3 us)
Async XLA Ops:
  7.2 164.7 %all-gather.14.cloned.1.call-start = ((), (), s32[]{:S(2)}) async-start(), calls=%async_computation.6 | async-start | bytes 37158912 | tf_op jit(solution)/shard_map/all_gather | solution.py:622
  15.7 392.1 %all-gather.10.cloned.1.call-start = ((), (), s32[]{:S(2)}) async-start(), calls=%async_computation.4 | async-start | bytes 49545216 | tf_op jit(solution)/shard_map/all_gather | solution.py:624
  16.4 546.0 %all-gather.12.cloned.1.call-start = ((), (), s32[]{:S(2)}) async-start(), calls=%async_computation.5 | async-start | bytes 37158912 | tf_op jit(solution)/shard_map/all_gather | solution.py:622
  23.6 744.7 %all-gather.8.cloned.1.call-start = ((), (), s32[]{:S(2)}) async-start(), calls=%async_computation.3 | async-start | bytes 37158912 | tf_op jit(solution)/shard_map/all_gather | solution.py:622
  99.9 711.3 %copy-start.13 = (s32[12]{0:T(128)}, s32[12]{0:T(128)S(1)}, u32[]{:S(2)}) copy-start(s32[12]{0:T(128)S(1)} %get-tuple-element.116.first_ref) | copy-start | bytes 148
  267.3 75.3 %all-to-all-start.2 = ((bf16[8,384,512]{2,1,0:T(8,128)(2,1)}), bf16[8,384,512]{2,1,0:T(8,128)(2,1)}, u32[]{:S(2)}, u32[]{:S(2)}) async-start(bf16[8,384,512]{2,1,0:T(8,128)(2,1)} %bitcast.60), calls=%async_computation.2 | async-start | bytes 6291456 | tf_op jit(solution)/shard_map/all_to_all | solution.py:645
  270.7 698.6 %all-gather.20.cloned.1.call-start = ((), (), s32[]{:S(2)}) async-start(), calls=%async_computation.9 | async-start | bytes 37158912 | tf_op jit(solution)/shard_map/all_gather | solution.py:648
  447.4 649.6 %all-gather.18.cloned.1.call-start = ((), (), s32[]{:S(2)}) async-start(), calls=%async_computation.8 | async-start | bytes 37158912 | tf_op jit(solution)/shard_map/all_gather | solution.py:648
  761.5 490.8 %all-gather.16.cloned.1.call-start = ((), (), s32[]{:S(2)}) async-start(), calls=%async_computation.7 | async-start | bytes 37158912 | tf_op jit(solution)/shard_map/all_gather | solution.py:648
  1083.4 429.2 %collective-permute-start.10 = (bf16[4,384,5376]{2,1,0:T(8,128)(2,1)}, bf16[4,384,5376]{2,1,0:T(8,128)(2,1)}, u32[]{:S(2)}, u32[]{:S(2)}) collective-permute-start(bf16[4,384,5376]{2,1,0:T(8,128)(2,1)} %grad_normed_pair.5), channel_id=1, source_target_pairs={{0,1},{1,0},{2,3},{3,2},{4,5},{5,4},{6,7},{7,6}} | collective-permute-start | bytes 49545224 | tf_op jit(solution)/shard_map/ppermute | solution.py:656
  1200.0 344.8 %collective-permute-start.5 = (bf16[4,384,5376]{2,1,0:T(8,128)(2,1)}, bf16[4,384,5376]{2,1,0:T(8,128)(2,1)}, u32[]{:S(2)}, u32[]{:S(2)}) collective-permute-start(bf16[4,384,5376]{2,1,0:T(8,128)(2,1)} %grad_normed_pair.4), channel_id=1, source_target_pairs={{0,1},{1,0},{2,3},{3,2},{4,5},{5,4},{6,7},{7,6}} | collective-permute-start | bytes 49545224 | tf_op jit(solution)/shard_map/ppermute | solution.py:656
  1355.1 221.2 %collective-permute-start = (bf16[4,384,5376]{2,1,0:T(8,128)(2,1)}, bf16[4,384,5376]{2,1,0:T(8,128)(2,1)}, u32[]{:S(2)}, u32[]{:S(2)}) collective-permute-start(bf16[4,384,5376]{2,1,0:T(8,128)(2,1)} %grad_normed_pair.3), channel_id=1, source_target_pairs={{0,1},{1,0},{2,3},{3,2},{4,5},{5,4},{6,7},{7,6}} | collective-permute-start | bytes 49545224 | tf_op jit(solution)/shard_map/ppermute | solution.py:656
  1542.7 92.2 %collective-permute-start.11 = (bf16[2,384,2688]{2,1,0:T(8,128)(2,1)}, bf16[2,384,2688]{2,1,0:T(8,128)(2,1)S(1)}, u32[]{:S(2)}, u32[]{:S(2)}) collective-permute-start(bf16[2,384,2688]{2,1,0:T(8,128)(2,1)} %get-tuple-element.86), channel_id=1, source_target_pairs={{0,2},{1,3},{2,0},{3,1},{4,6},{5,7},{6,4},{7,5}} | collective-permute-start | bytes 12386312 | tf_op jit(solution)/shard_map/ppermute | solution.py:656
  1544.2 92.4 %collective-permute-start.13 = (bf16[2,384,2688]{2,1,0:T(8,128)(2,1)}, bf16[2,384,2688]{2,1,0:T(8,128)(2,1)}, u32[]{:S(2)}, u32[]{:S(2)}) collective-permute-start(bf16[2,384,2688]{2,1,0:T(8,128)(2,1)} %get-tuple-element.88), channel_id=1, source_target_pairs={{0,4},{1,5},{2,6},{3,7},{4,0},{5,1},{6,2},{7,3}} | collective-permute-start | bytes 12386312 | tf_op jit(solution)/shard_map/ppermute | solution.py:656
  1574.3 149.1 %collective-permute-start.6 = (bf16[2,384,2688]{2,1,0:T(8,128)(2,1)}, bf16[2,384,2688]{2,1,0:T(8,128)(2,1)S(1)}, u32[]{:S(2)}, u32[]{:S(2)}) collective-permute-start(bf16[2,384,2688]{2,1,0:T(8,128)(2,1)} %get-tuple-element.80), channel_id=1, source_target_pairs={{0,2},{1,3},{2,0},{3,1},{4,6},{5,7},{6,4},{7,5}} | collective-permute-start | bytes 12386312 | tf_op jit(solution)/shard_map/ppermute | solution.py:656
  1574.7 152.1 %collective-permute-start.8 = (bf16[2,384,2688]{2,1,0:T(8,128)(2,1)}, bf16[2,384,2688]{2,1,0:T(8,128)(2,1)}, u32[]{:S(2)}, u32[]{:S(2)}) collective-permute-start(bf16[2,384,2688]{2,1,0:T(8,128)(2,1)} %get-tuple-element.82), channel_id=1, source_target_pairs={{0,4},{1,5},{2,6},{3,7},{4,0},{5,1},{6,2},{7,3}} | collective-permute-start | bytes 12386312 | tf_op jit(solution)/shard_map/ppermute | solution.py:656
  1606.0 205.9 %collective-permute-start.1 = (bf16[2,384,2688]{2,1,0:T(8,128)(2,1)}, bf16[2,384,2688]{2,1,0:T(8,128)(2,1)S(1)}, u32[]{:S(2)}, u32[]{:S(2)}) collective-permute-start(bf16[2,384,2688]{2,1,0:T(8,128)(2,1)} %get-tuple-element.74), channel_id=1, source_target_pairs={{0,2},{1,3},{2,0},{3,1},{4,6},{5,7},{6,4},{7,5}} | collective-permute-start | bytes 12386312 | tf_op jit(solution)/shard_map/ppermute | solution.py:656
  1635.0 180.3 %collective-permute-start.3 = (bf16[2,384,2688]{2,1,0:T(8,128)(2,1)}, bf16[2,384,2688]{2,1,0:T(8,128)(2,1)S(1)}, u32[]{:S(2)}, u32[]{:S(2)}) collective-permute-start(bf16[2,384,2688]{2,1,0:T(8,128)(2,1)} %get-tuple-element.76), channel_id=1, source_target_pairs={{0,4},{1,5},{2,6},{3,7},{4,0},{5,1},{6,2},{7,3}} | collective-permute-start | bytes 12386312 | tf_op jit(solution)/shard_map/ppermute | solution.py:656
  1636.5 221.1 %collective-permute-start.12 = (bf16[384,2688]{1,0:T(8,128)(2,1)S(1)}, bf16[384,2688]{1,0:T(8,128)(2,1)S(1)}, u32[]{:S(2)}, u32[]{:S(2)}) collective-permute-start(bf16[384,2688]{1,0:T(8,128)(2,1)S(1)} %fusion.4), channel_id=1, source_target_pairs={{0,4},{1,5},{2,6},{3,7},{4,0},{5,1},{6,2},{7,3}} | collective-permute-start | bytes 6193160 | tf_op jit(solution)/shard_map/ppermute | solution.py:656
  1723.4 165.7 %collective-permute-start.14 = (bf16[384,2688]{1,0:T(8,128)(2,1)}, bf16[384,2688]{1,0:T(8,128)(2,1)}, u32[]{:S(2)}, u32[]{:S(2)}) collective-permute-start(bf16[384,2688]{1,0:T(8,128)(2,1)} %fusion.5), channel_id=1, source_target_pairs={{0,2},{1,3},{2,0},{3,1},{4,6},{5,7},{6,4},{7,5}} | collective-permute-start | bytes 6193160 | tf_op jit(solution)/shard_map/ppermute | solution.py:656
  1726.8 176.3 %collective-permute-start.7 = (bf16[384,2688]{1,0:T(8,128)(2,1)}, bf16[384,2688]{1,0:T(8,128)(2,1)}, u32[]{:S(2)}, u32[]{:S(2)}) collective-permute-start(bf16[384,2688]{1,0:T(8,128)(2,1)} %fusion.2), channel_id=1, source_target_pairs={{0,4},{1,5},{2,6},{3,7},{4,0},{5,1},{6,2},{7,3}} | collective-permute-start | bytes 6193160 | tf_op jit(solution)/shard_map/ppermute | solution.py:656
  1811.9 91.2 %collective-permute-start.9 = (bf16[384,2688]{1,0:T(8,128)(2,1)}, bf16[384,2688]{1,0:T(8,128)(2,1)}, u32[]{:S(2)}, u32[]{:S(2)}) collective-permute-start(bf16[384,2688]{1,0:T(8,128)(2,1)} %fusion.3), channel_id=1, source_target_pairs={{0,2},{1,3},{2,0},{3,1},{4,6},{5,7},{6,4},{7,5}} | collective-permute-start | bytes 6193160 | tf_op jit(solution)/shard_map/ppermute | solution.py:656
  1815.2 129.9 %collective-permute-start.2 = (bf16[384,2688]{1,0:T(8,128)(2,1)}, bf16[384,2688]{1,0:T(8,128)(2,1)S(1)}, u32[]{:S(2)}, u32[]{:S(2)}) collective-permute-start(bf16[384,2688]{1,0:T(8,128)(2,1)} %fusion), channel_id=1, source_target_pairs={{0,4},{1,5},{2,6},{3,7},{4,0},{5,1},{6,2},{7,3}} | collective-permute-start | bytes 6193160 | tf_op jit(solution)/shard_map/ppermute | solution.py:656
  1858.9 86.2 %collective-permute-start.4 = (bf16[384,2688]{1,0:T(8,128)(2,1)}, bf16[384,2688]{1,0:T(8,128)(2,1)}, u32[]{:S(2)}, u32[]{:S(2)}) collective-permute-start(bf16[384,2688]{1,0:T(8,128)(2,1)} %fusion.1), channel_id=1, source_target_pairs={{0,2},{1,3},{2,0},{3,1},{4,6},{5,7},{6,4},{7,5}} | collective-permute-start | bytes 6193160 | tf_op jit(solution)/shard_map/ppermute | solution.py:656
  (48 other events, 2694.8 us)
Sparse Core Ops, SparseCore 0:
  15.8 155.9 all-gather.13
  173.7 234.0 all-gather.9
  409.6 152.8 all-gather.11
  564.7 186.5 all-gather.7
  753.6 186.5 all-gather.19
  941.9 155.0 all-gather.17
  1099.4 152.8 all-gather.15

commit v3 on v2

--- a/solution.py
+++ b/solution.py
@@ -21,7 +21,7 @@
     return lax.dot_general(lhs, rhs, (((lhs_dim,), (rhs_dim,)), ((), ())), preferred_element_type=jnp.float32)
 
 
-ROWS = 128
+ROWS = 64
 CHUNK = 16
 
 
@@ -56,17 +56,17 @@
         n_ref[rows, :] = (values * inverse_rms(values) * gain).astype(n_ref.dtype)
 
 
-def pre_norm(x_in, gain, seq):
+def pre_norm(x_in, gain, first_seq, count):
     _, rows, depth = x_in.shape
-    whole, one, vec = row_specs(seq, depth)
+    steps = rows // ROWS
     return pl.pallas_call(
         pre_norm_kernel,
-        grid=(rows // ROWS,),
-        in_specs=[whole, vec],
-        out_specs=one,
-        out_shape=jax.ShapeDtypeStruct((rows, depth), jnp.bfloat16),
+        grid=(count, steps),
+        in_specs=[pl.BlockSpec((1, ROWS, depth), lambda s, i: (first_seq + s, i, 0)), pl.BlockSpec((1, depth), lambda s, i: (0, 0))],
+        out_specs=pl.BlockSpec((ROWS, depth), lambda s, i: (s * steps + i, 0)),
+        out_shape=jax.ShapeDtypeStruct((count * rows, depth), jnp.bfloat16),
         compiler_params=pltpu.CompilerParams(vmem_limit_bytes=54 * 1024 * 1024),
-        cost_estimate=pl.CostEstimate(flops=rows * depth * 400, bytes_accessed=4 * rows * depth, transcendentals=rows),
+        cost_estimate=pl.CostEstimate(flops=count * rows * depth * 400, bytes_accessed=4 * count * rows * depth, transcendentals=count * rows),
         name="pre_norm",
     )(x_in, gain)
 
@@ -252,6 +252,28 @@
         cost_estimate=pl.CostEstimate(flops=8 * rows * cols * depth, bytes_accessed=2 * (8 * rows * depth + cols * depth), transcendentals=0),
         name="grad_normed_own",
     )(dst, d_lin, w_t, from_pair)
+
+
+def fold_kernel(keep_x_ref, near_x_ref, keep_y_ref, near_y_ref, x_ref, y_ref):
+    for out, kept, near in ((x_ref, keep_x_ref, near_x_ref), (y_ref, keep_y_ref, near_y_ref)):
+        out[...] = (kept[0].astype(jnp.float32) + near[0].astype(jnp.float32)).astype(out.dtype)
+
+
+def fold(keep_x, near_x, keep_y, near_y):
+    _, rows, half = keep_x.shape
+    tile = 96
+    second = pl.BlockSpec((1, tile, half), lambda i: (1, i, 0))
+    out = pl.BlockSpec((tile, half), lambda i: (i, 0))
+    return pl.pallas_call(
+        fold_kernel,
+        grid=(rows // tile,),
+        in_specs=[second] * 4,
+        out_specs=[out, out],
+        out_shape=[jax.ShapeDtypeStruct((rows, half), jnp.bfloat16)] * 2,
+        compiler_params=pltpu.CompilerParams(vmem_limit_bytes=54 * 1024 * 1024),
+        cost_estimate=pl.CostEstimate(flops=rows * half * 800, bytes_accessed=12 * rows * half, transcendentals=0),
+        name="fold",
+    )(keep_x, near_x, keep_y, near_y)
 
 
 def gain_sum_kernel(n_dev, pre_ref, post_ref, pre_out, post_out, slots, local_sem, send_sem, recv_sem):
@@ -305,38 +327,42 @@
     )(d_pre, d_post)
 
 
-def grad_w_kernel(n_rows, head_dim, *refs):
-    a_refs, d_refs, outs = refs[:n_rows], refs[n_rows:2 * n_rows], refs[2 * n_rows:]
-    total = dot_f32(a_refs[0][...], d_refs[0][...], 0, 0)
-    for a_ref, d_ref in zip(a_refs[1:], d_refs[1:]):
-        total = total + dot_f32(a_ref[...], d_ref[...], 0, 0)
+def grad_w_kernel(n_out, head_dim, a_ref, d_ref, *refs):
+    prev, outs = refs[:-n_out], refs[-n_out:]
+    n_dev, rows, tile = a_ref.shape
+    total = dot_f32(a_ref[...].reshape(n_dev * rows, tile), d_ref[...], 0, 0)
     col = 0
-    for out in outs:
+    for i, out in enumerate(outs):
         for h in range(out.shape[1]):
-            out[:, h, :] = total[:, col:col + head_dim]
+            part = total[:, col:col + head_dim]
+            out[:, h, :] = part + prev[i][:, h, :] if prev else part
             col += head_dim
 
 
-def grad_w(normed, d_lin, heads, head_dim, col_blk):
-    seq_len, depth = normed[0].shape
-    cols = sum(heads) * head_dim
-    n_rows = len(normed)
+def grad_w(gathered, slot, rows, d_lin, heads, head_dim, prev):
+    n_dev, _, depth = gathered.shape
+    seq_len, cols = d_lin.shape
     tile = 384
-    return pl.pallas_call(
-        functools.partial(grad_w_kernel, n_rows, head_dim),
+    outs = [pl.BlockSpec((tile, h, head_dim), lambda i: (i, 0, 0)) for h in heads]
+    return pl.pallas_call(
+        functools.partial(grad_w_kernel, len(heads), head_dim),
         grid=(depth // tile,),
-        in_specs=[pl.BlockSpec((seq_len, tile), lambda i: (0, i))] * n_rows
-        + [pl.BlockSpec((seq_len, cols), lambda i: (0, col_blk), pipeline_mode=pl.Buffered(1))] * n_rows,
-        out_specs=[pl.BlockSpec((tile, h, head_dim), lambda i: (i, 0, 0)) for h in heads],
+        in_specs=[
+            pl.BlockSpec((n_dev, rows, tile), lambda i: (0, slot, i)),
+            pl.BlockSpec((seq_len, cols), lambda i: (0, 0), pipeline_mode=pl.Buffered(1)),
+        ] + (outs if prev else []),
+        out_specs=outs,
         out_shape=[jax.ShapeDtypeStruct((depth, h, head_dim), jnp.float32) for h in heads],
-        compiler_params=pltpu.CompilerParams(vmem_limit_bytes=58 * 1024 * 1024),
-        cost_estimate=pl.CostEstimate(flops=2 * n_rows * seq_len * depth * cols, bytes_accessed=2 * n_rows * seq_len * (depth + cols), transcendentals=0),
+        input_output_aliases={2 + i: i for i in range(len(prev))},
+        compiler_params=pltpu.CompilerParams(vmem_limit_bytes=56 * 1024 * 1024),
+        cost_estimate=pl.CostEstimate(flops=2 * seq_len * depth * cols, bytes_accessed=2 * seq_len * (depth + cols) + 8 * depth * cols, transcendentals=0),
         name="grad_w",
-    )(*normed, *d_lin)
+    )(gathered, d_lin, *prev)
 
 
 def qkv_kernel(q_cols, k_cols, head_dim, q_scale, a_ref, w_ref, cos_ref, sin_ref, q_ref, k_ref, v_ref):
-    lin = jnp.dot(a_ref[...], w_ref[...], preferred_element_type=jnp.float32)
+    n_dev, rows, depth = a_ref.shape
+    lin = jnp.dot(a_ref[...].reshape(n_dev * rows, depth), w_ref[...], preferred_element_type=jnp.float32)
     cos_t, sin_t = cos_ref[...], sin_ref[...]
     for h in range((q_cols + k_cols) // head_dim):
         col = h * head_dim
@@ -349,38 +375,54 @@
     v_ref[...] = lin[:, q_cols + k_cols:].astype(v_ref.dtype)
 
 
-def qkv_project(normed, w_all, cos_t, sin_t, q_cols, k_cols, head_dim):
-    rows, depth = normed.shape
+def qkv_project(gathered, slot, rows, w_all, cos_t, sin_t, q_cols, k_cols, head_dim):
+    n_dev, _, depth = gathered.shape
     cols = w_all.shape[1]
     v_cols = cols - q_cols - k_cols
-    tile = 512
+    seq_len, tile = n_dev * rows, 2 * rows
+    by_row = [pl.BlockSpec((tile, width), lambda i: (i, 0)) for width in (head_dim, head_dim, q_cols, k_cols, v_cols)]
     return pl.pallas_call(
         functools.partial(qkv_kernel, q_cols, k_cols, head_dim, head_dim ** -0.5),
-        grid=(rows // tile,),
+        grid=(n_dev // 2,),
         in_specs=[
-            pl.BlockSpec((tile, depth), lambda i: (i, 0)),
+            pl.BlockSpec((2, rows, depth), lambda i: (i, slot, 0)),
             pl.BlockSpec((depth, cols), lambda i: (0, 0), pipeline_mode=pl.Buffered(1)),
-            pl.BlockSpec((tile, head_dim), lambda i: (i, 0)),
-            pl.BlockSpec((tile, head_dim), lambda i: (i, 0)),
-        ],
-        out_specs=[
-            pl.BlockSpec((tile, q_cols), lambda i: (i, 0)),
-            pl.BlockSpec((tile, k_cols), lambda i: (i, 0)),
-            pl.BlockSpec((tile, v_cols), lambda i: (i, 0)),
-        ],
-        out_shape=[
-            jax.ShapeDtypeStruct((rows, q_cols), jnp.bfloat16),
-            jax.ShapeDtypeStruct((rows, k_cols), jnp.bfloat16),
-            jax.ShapeDtypeStruct((rows, v_cols), jnp.bfloat16),
-        ],
-        compiler_params=pltpu.CompilerParams(vmem_limit_bytes=56 * 1024 * 1024),
-        cost_estimate=pl.CostEstimate(flops=2 * rows * depth * cols, bytes_accessed=2 * (rows * depth + depth * cols + rows * cols), transcendentals=0),
+        ] + by_row[:2],
+        out_specs=by_row[2:],
+        out_shape=[jax.ShapeDtypeStruct((seq_len, width), jnp.bfloat16) for width in (q_cols, k_cols, v_cols)],
+        compiler_params=pltpu.CompilerParams(vmem_limit_bytes=58 * 1024 * 1024),
+        cost_estimate=pl.CostEstimate(flops=2 * seq_len * depth * cols, bytes_accessed=2 * (seq_len * depth + depth * cols + seq_len * cols), transcendentals=0),
         name="qkv_project",
-    )(normed, w_all, cos_t, sin_t)
+    )(gathered, w_all, cos_t, sin_t)
 
 
 def stack_heads(block, groups, head_dim):
     return jnp.concatenate([block[:, g * head_dim:(g + 1) * head_dim] for g in range(groups)], axis=0)
+
+
+def keep_mask(key_pos, floor_row, wide, diagonal):
+    keep = jnp.concatenate([key_pos] * (wide // LANES), axis=1) > floor_row
+    if diagonal:
+        key_idx = lax.broadcasted_iota(jnp.int32, (BLK, wide), 0)
+        q_idx = lax.broadcasted_iota(jnp.int32, (BLK, wide), 1) % BLK
+        keep = keep & (key_idx <= q_idx)
+    return keep
+
+
+def visit_pairs(visit, first, blk):
+    odd = (blk - first) % 2
+
+    @pl.when(odd == 0)
+    def _():
+        visit([blk], True)
+
+    @pl.when(odd == 1)
+    def _():
+        visit([blk, blk - 1], True)
+
+    @pl.loop(0, (blk - first) // 2)
+    def _(i):
+        visit([first + 2 * i, first + 2 * i + 1], False)
 
 
 def attn_fwd_kernel(groups, head_dim, first_ref, q_ref, k_ref, v_ref, pos_ref, key_pos_ref, o_ref, lse_ref, m_scr, l_scr, acc_scr):
@@ -389,38 +431,30 @@
     floor_row = jnp.concatenate([pos_ref[...]] * groups, axis=1) - WINDOW
     wide = groups * BLK
 
-    def visit(kb, diagonal):
-        start = pl.multiple_of(kb * BLK, BLK)
-        k_blk = k_ref[pl.ds(start, BLK), :]
-        v_blk = v_ref[pl.ds(start, BLK), :]
-        scores = dot_f32(k_blk, q_all, 1, 1)
-        capped = jnp.tanh(scores * (1.0 / SOFT_CAP)) * (SOFT_CAP * LOG2E)
-        keep = jnp.concatenate([key_pos_ref[pl.ds(start, BLK), :]] * (wide // LANES), axis=1) > floor_row
-        if diagonal:
-            key_idx = lax.broadcasted_iota(jnp.int32, (BLK, wide), 0)
-            q_idx = lax.broadcasted_iota(jnp.int32, (BLK, wide), 1) % BLK
-            keep = keep & (key_idx <= q_idx)
-        capped = jnp.where(keep, capped, -1e30)
-        top = jnp.max(capped, axis=0, keepdims=True)
-        if diagonal:
-            prob = jnp.exp2(capped - top)
-            m_scr[...] = top
-            l_scr[...] = jnp.sum(prob, axis=0, keepdims=True)
-            acc_scr[...] = dot_f32(v_blk, prob.astype(jnp.bfloat16), 0, 0)
+    def visit(blocks, with_diagonal):
+        rows = [pl.ds(pl.multiple_of(kb * BLK, BLK), BLK) for kb in blocks]
+        scores = [dot_f32(k_ref[r, :], q_all, 1, 1) for r in rows]
+        capped = []
+        for i, r in enumerate(rows):
+            keep = keep_mask(key_pos_ref[r, :], floor_row, wide, with_diagonal and i == 0)
+            capped.append(jnp.where(keep, jnp.tanh(scores[i] * (1.0 / SOFT_CAP)) * (SOFT_CAP * LOG2E), -1e30))
+        top = functools.reduce(jnp.maximum, [jnp.max(c, axis=0, keepdims=True) for c in capped])
+        if not with_diagonal:
+            m_old = m_scr[...]
+            top = jnp.maximum(m_old, top)
+            alpha = jnp.exp2(m_old - top)
+        m_scr[...] = top
+        probs = [jnp.exp2(c - top) for c in capped]
+        total = sum(jnp.sum(p, axis=0, keepdims=True) for p in probs)
+        acc = sum(dot_f32(v_ref[r, :], p.astype(jnp.bfloat16), 0, 0) for r, p in zip(rows, probs))
+        if with_diagonal:
+            l_scr[...] = total
+            acc_scr[...] = acc
         else:
-            m_old = m_scr[...]
-            m_new = jnp.maximum(m_old, top)
-            alpha = jnp.exp2(m_old - m_new)
-            prob = jnp.exp2(capped - m_new)
-            m_scr[...] = m_new
-            l_scr[...] = l_scr[...] * alpha + jnp.sum(prob, axis=0, keepdims=True)
-            acc_scr[...] = acc_scr[...] * alpha + dot_f32(v_blk, prob.astype(jnp.bfloat16), 0, 0)
-
-    visit(blk, True)
-
-    @pl.loop(first_ref[blk], blk)
-    def _(kb):
-        visit(kb, False)
+            l_scr[...] = l_scr[...] * alpha + total
+            acc_scr[...] = acc_scr[...] * alpha + acc
+
+    visit_pairs(visit, first_ref[blk], blk)
 
     total = l_scr[...]
     out = (acc_scr[...] / total).T
@@ -468,7 +502,7 @@
 
 
 def attn_bwd_kernel(groups, head_dim, q_scale, first_ref, q_ref, k_ref, v_ref, o_ref, do_ref, pos_ref, key_pos_ref, lse_ref, cos_ref, sin_ref,
-                    out_ref, dq_scr, dk_scr, dv_scr, dq_out, dk_out, dv_out, dq_sem, kv_sem):
+                    out_ref, delta_scr, dq_scr, dk_scr, dv_scr, dq_out, dk_out, dv_out, dq_sem, kv_sem):
     head, blk = pl.program_id(0), pl.program_id(1)
     n_head, n_blk = pl.num_programs(0), pl.num_programs(1)
     half = head_dim // 2
@@ -478,43 +512,44 @@
 
     @pl.when(blk == 0)
     def _():
-        dk_scr[...] = jnp.zeros_like(dk_scr)
-        dv_scr[...] = jnp.zeros_like(dv_scr)
+        @pl.loop(0, n_blk)
+        def _(i):
+            rows = pl.ds(pl.multiple_of(i * BLK, BLK), BLK)
+            dk_scr[rows, :] = jnp.zeros((BLK, head_dim), jnp.float32)
+            dv_scr[rows, :] = jnp.zeros((BLK, head_dim), jnp.float32)
 
     q_all = stack_heads(q_ref[...], groups, head_dim)
     do_all = stack_heads(do_ref[...], groups, head_dim)
     o_all = stack_heads(o_ref[...], groups, head_dim)
     floor_row = jnp.concatenate([pos_ref[...]] * groups, axis=1) - WINDOW
     lse_row = lse_ref[0, 0]
-    delta = jnp.sum((do_all.astype(jnp.float32) * o_all.astype(jnp.float32)).T, axis=0, keepdims=True)
-
-    def visit(kb, diagonal):
-        start = pl.multiple_of(kb * BLK, BLK)
-        k_blk = k_ref[pl.ds(start, BLK), :]
-        v_blk = v_ref[pl.ds(start, BLK), :]
-        scores = dot_f32(k_blk, q_all, 1, 1)
-        d_prob = dot_f32(v_blk, do_all, 1, 1)
-        tanh_s = jnp.tanh(scores * (1.0 / SOFT_CAP))
-        keep = jnp.concatenate([key_pos_ref[pl.ds(start, BLK), :]] * (wide // LANES), axis=1) > floor_row
-        if diagonal:
-            key_idx = lax.broadcasted_iota(jnp.int32, (BLK, wide), 0)
-            q_idx = lax.broadcasted_iota(jnp.int32, (BLK, wide), 1) % BLK
-            keep = keep & (key_idx <= q_idx)
-        prob = jnp.exp2(jnp.where(keep, tanh_s * (SOFT_CAP * LOG2E) - lse_row, -1e30))
-        d_score = (prob * (d_prob - delta) * (1.0 - tanh_s * tanh_s)).astype(jnp.bfloat16)
-        dv_scr[pl.ds(start, BLK), :] += jnp.dot(prob.astype(jnp.bfloat16), do_all, preferred_element_type=jnp.float32)
-        dk_scr[pl.ds(start, BLK), :] += jnp.dot(d_score, q_all, preferred_element_type=jnp.float32)
-        dq_new = dot_f32(k_blk, d_score, 0, 0)
-        if diagonal:
+
+    def visit(blocks, with_diagonal):
+        if with_diagonal:
+            delta = jnp.sum((do_all.astype(jnp.float32) * o_all.astype(jnp.float32)).T, axis=0, keepdims=True)
+            delta_scr[...] = delta
+        else:
+            delta = delta_scr[...]
+        rows = [pl.ds(pl.multiple_of(kb * BLK, BLK), BLK) for kb in blocks]
+        k_blks = [k_ref[r, :] for r in rows]
+        scores = [dot_f32(k_blk, q_all, 1, 1) for k_blk in k_blks]
+        d_probs = [dot_f32(v_ref[r, :], do_all, 1, 1) for r in rows]
+        dq_new = None
+        for i, r in enumerate(rows):
+            tanh_s = jnp.tanh(scores[i] * (1.0 / SOFT_CAP))
+            keep = keep_mask(key_pos_ref[r, :], floor_row, wide, with_diagonal and i == 0)
+            prob = jnp.exp2(jnp.where(keep, tanh_s * (SOFT_CAP * LOG2E) - lse_row, -1e30))
+            d_score = (prob * (d_probs[i] - delta) * (1.0 - tanh_s * tanh_s)).astype(jnp.bfloat16)
+            dv_scr[r, :] += jnp.dot(prob.astype(jnp.bfloat16), do_all, preferred_element_type=jnp.float32)
+            dk_scr[r, :] += jnp.dot(d_score, q_all, preferred_element_type=jnp.float32)
+            term = dot_f32(k_blks[i], d_score, 0, 0)
+            dq_new = term if dq_new is None else dq_new + term
+        if with_diagonal:
             dq_scr[...] = dq_new
         else:
             dq_scr[...] += dq_new
 
-    visit(blk, True)
-
-    @pl.loop(first_ref[blk], blk)
-    def _(kb):
-        visit(kb, False)
+    visit_pairs(visit, first_ref[blk], blk)
 
     def dq_copy(h, i):
         dst = out_ref.at[pl.ds(pl.multiple_of(i * BLK, BLK), BLK), pl.ds(pl.multiple_of(h * q_width, q_width), q_width)]
@@ -583,6 +618,7 @@
             ],
             out_specs=pl.BlockSpec(memory_space=pl.ANY),
             scratch_shapes=[
+                pltpu.VMEM((1, wide), jnp.float32),
                 pltpu.VMEM((head_dim, wide), jnp.float32),
                 pltpu.VMEM((seq_len, head_dim), jnp.float32),
                 pltpu.VMEM((seq_len, head_dim), jnp.float32),
@@ -600,6 +636,11 @@
     )(first_blk, q_all, k_all, v_all, o_all, d_o, pos, key_pos, lse, cos_t, sin_t)
 
 
+SEQ_ORDER = (1, 2, 0)
+GW_ORDER = (1, 0, 2)
+GWO_ORDER = (2, 1, 0)
+
+
 def solution(mesh):
     act_spec = P('dp', 'tp', None)
     head_spec = P(None, 'tp', None)
@@ -608,7 +649,7 @@
     out_specs = (act_spec, act_spec, grad_spec, grad_spec, grad_spec, P(('dp', 'tp'), None, None), P('dp'), P('dp'))
 
     def local_body(x_in, positions, grad_out, w_query, w_key, w_value, w_out, gain_pre, gain_post):
-        n_rows, _, depth = x_in.shape
+        _, _, depth = x_in.shape
         n_dev = mesh.shape['tp']
         heads_loc, head_dim = w_query.shape[1], w_query.shape[2]
         kv_loc = w_key.shape[1]
@@ -616,12 +657,14 @@
         q_cols, k_cols = heads_loc * head_dim, kv_loc * head_dim
 
         gain_pre_row, gain_post_row = gain_pre[None, :], gain_post[None, :]
-        normed_all = []
-        for b in range(n_rows):
-            normed = pre_norm(x_in, gain_pre_row, b)
-            normed_all.append(lax.all_gather(normed, 'tp', axis=0, tiled=True))
+        rows = x_in.shape[1]
         w_out_loc = w_out.reshape(q_cols, depth)
         w_out_all = lax.all_gather(w_out_loc, 'tp', axis=0, tiled=True)
+        gathered = {}
+        for first_seq, count in ((1, 2), (0, 1)):
+            normed = pre_norm(x_in, gain_pre_row, first_seq, count)
+            whole = lax.all_gather(normed, 'tp', axis=0, tiled=True).reshape(n_dev, count * rows, depth)
+            gathered.update({first_seq + i: (whole, i) for i in range(count)})
 
         pos_all = lax.all_gather(positions, 'tp', axis=1, tiled=True)
         seq_len = pos_all.shape[1]
@@ -630,52 +673,52 @@
         before = pos_all[:, None, :] <= pos_all[:, ::BLK, None] - WINDOW
         first_blk = jnp.sum(before.astype(jnp.int32), axis=-1) // BLK
         w_all = jnp.concatenate([w_query.reshape(depth, q_cols), w_key.reshape(depth, k_cols), w_value.reshape(depth, k_cols)], axis=1)
-
-        saved, d_proj_all = [], []
+        w_t = w_all.T
+        me = lax.axis_index('tp')
+        own_dst, pair_dst = me[None], me[None] ^ 1
+
+        def swap(value, bit):
+            return lax.ppermute(value, 'tp', [(d, d ^ bit) for d in range(n_dev)])
+
+        saved, d_proj_all = {}, {}
         y_out, d_post = None, jnp.zeros((1, depth), jnp.float32)
-        for b in range(n_rows):
+        for b in SEQ_ORDER:
             angles = pos_all[b].astype(jnp.float32)[:, None] * inv_freq
             cos_h, sin_h = jnp.cos(angles), jnp.sin(angles)
             cos_t = jnp.concatenate([cos_h, cos_h], axis=-1)
             sin_t = jnp.concatenate([-sin_h, sin_h], axis=-1)
             pos_b = pos_all[b][None, :]
             key_pos = jnp.broadcast_to(pos_all[b][:, None], (seq_len, LANES))
-            q_b, k_b, v_b = qkv_project(normed_all[b], w_all, cos_t, sin_t, q_cols, k_cols, head_dim)
+            q_b, k_b, v_b = qkv_project(*gathered[b], rows, w_all, cos_t, sin_t, q_cols, k_cols, head_dim)
             o_b, lse_b = attn_fwd(q_b, k_b, v_b, pos_b, key_pos, first_blk[b], groups, head_dim)
-            o_mine = lax.all_to_all(o_b.reshape(-1, seq_len // n_dev, q_cols), 'tp', split_axis=0, concat_axis=0, tiled=True)
+            o_mine = lax.all_to_all(o_b.reshape(n_dev, rows, q_cols), 'tp', split_axis=0, concat_axis=0, tiled=True)
             proj = out_proj(o_mine, w_out_all)
             y_out, d_proj, d_post = post_norm(proj, x_in, grad_out, gain_post_row, d_post, y_out, b)
-            d_proj_all.append(lax.all_gather(d_proj, 'tp', axis=0, tiled=True))
-            saved.append((q_b, k_b, v_b, o_b, pos_b, key_pos, lse_b, cos_t, sin_t))
-
-        me = lax.axis_index('tp')
-        own_dst, pair_dst = me[None], me[None] ^ 1
-        w_t = w_all.T
-
-        def swap(value, bit):
-            return lax.ppermute(value, 'tp', [(d, d ^ bit) for d in range(n_dev)])
+            d_proj_all[b] = lax.all_gather(d_proj, 'tp', axis=0, tiled=True)
+            saved[b] = (q_b, k_b, v_b, o_b, pos_b, key_pos, lse_b, cos_t, sin_t)
 
         grad_x, d_pre = None, jnp.zeros((1, depth), jnp.float32)
-        grad_wo = jnp.zeros((), jnp.float32)
-        d_lin = []
-        for b in range(n_rows):
+        d_lin = {}
+        for b in SEQ_ORDER:
             q_b, k_b, v_b, o_b, pos_b, key_pos, lse_b, cos_t, sin_t = saved[b]
             d_o = dot_f32(d_proj_all[b], w_out_loc, 1, 1).astype(jnp.bfloat16)
-            d_lin.append(attn_bwd(q_b, k_b, v_b, o_b, d_o, pos_b, key_pos, lse_b, first_blk[b], cos_t, sin_t, groups, head_dim))
-            pair = grad_normed_pair(pair_dst, d_lin[b], w_t, seq_len // n_dev)
+            d_lin[b] = attn_bwd(q_b, k_b, v_b, o_b, d_o, pos_b, key_pos, lse_b, first_blk[b], cos_t, sin_t, groups, head_dim)
+            pair = grad_normed_pair(pair_dst, d_lin[b], w_t, rows)
             from_pair = swap(pair, 1)
             send_x, keep_x, send_y, keep_y = grad_normed_own(own_dst, d_lin[b], w_t, from_pair)
             near_x = swap(send_x, 2)
             near_y = swap(send_y, 4)
-            fold_x = (keep_x[1].astype(jnp.float32) + near_x[1].astype(jnp.float32)).astype(jnp.bfloat16)
-            fold_y = (keep_y[1].astype(jnp.float32) + near_y[1].astype(jnp.float32)).astype(jnp.bfloat16)
+            fold_x, fold_y = fold(keep_x, near_x, keep_y, near_y)
             far_x = swap(fold_x, 4)
             far_y = swap(fold_y, 2)
             grad_x, d_pre = pre_grad((keep_x, near_x, far_x, keep_y, near_y, far_y), x_in, grad_out, gain_pre_row, d_pre, grad_x, b)
-            grad_wo = grad_wo + dot_f32(o_b, d_proj_all[b], 0, 0)
-
-        grad_wq, = grad_w(normed_all, d_lin, (heads_loc,), head_dim, 0)
-        grad_wk, grad_wv = grad_w(normed_all, d_lin, (kv_loc, kv_loc), head_dim, 1)
+        grad_wo = jnp.zeros((), jnp.float32)
+        for b in GWO_ORDER:
+            grad_wo = grad_wo + dot_f32(saved[b][3], d_proj_all[b], 0, 0)
+        grads = ()
+        for b in GW_ORDER:
+            grads = grad_w(*gathered[b], rows, d_lin[b], (heads_loc, kv_loc, kv_loc), head_dim, grads)
+        grad_wq, grad_wk, grad_wv = grads
         grad_pre, grad_post = gain_sum(d_pre, d_post, n_dev)
         grad_pre, grad_post = grad_pre[0], grad_post[0]
         return y_out, grad_x, grad_wq, grad_wk, grad_wv, grad_wo.reshape(w_out.shape), grad_pre, grad_post

time: 1990 us -> 1910 us (0.960)
  waiting for transfers between devices: 599 us -> 540 us
  blocking collectives: 166 us -> 136 us
  Pallas kernels: 912 us -> 938 us
    ppermute x15, waiting for transfers between devices: 235 us -> 113 us  [swap(): return lax.ppermute(value, 'tp', [(d, d ^ bit) for d in range(n_dev)])]
    all_gather x1, waiting for transfers between devices: 65.1 us -> 151 us  [local_body(): w_out_all = lax.all_gather(w_out_loc, 'tp', axis=0, tiled=True)]
    all_to_all x1, waiting for transfers between devices: 71.1 us -> 0.01 us  [local_body(): lax.all_to_all(o_b.reshape(n_dev, rows, q_cols), 'tp', split_axis=0, conc...]
    pallas_call x5 -> x8, Pallas kernels: 155 us -> 212 us  [the longest x3 173 us: grad_w(): pl.pallas_call(functools.partial(grad_w_kernel, len(heads), head_dim), gr...]
    all_gather x6 -> x5, waiting for transfers between devices: 227 us -> 274 us  [the longest x2 199 us: local_body(): lax.all_gather(normed, 'tp', axis=0, tiled=True)]
    all_to_all x2, blocking collectives: 151 us -> 121 us  [local_body(): lax.all_to_all(o_b.reshape(n_dev, rows, q_cols), 'tp', split_axis=0, conc...]
    pallas_call x3, Pallas kernels: 128 us -> 104 us  [attn_fwd(): pl.pallas_call(functools.partial(attn_fwd_kernel, groups, head_dim), grid...]
    unnamed x101 -> x91, local copies, waits for them, and re-layouts: 41.8 us -> 43.2 us
  transfers between devices with their start and end apart: 23 -> 22, of which waited for: 12 -> 7; matrix products, arithmetic and copies ran while one was open for 13% -> 12% of each run, Pallas kernels for 45% -> 47%
where the time goes in v3:
time: 1910 us; the launch traced here: 1900 us
  Pallas kernels  938 us (49%)
  waiting for transfers between devices  540 us (28%)
  matrix products  152 us (8%)
  blocking collectives  136 us (7%)
  local copies, waits for them, and re-layouts  61.9 us (3%)
  other arithmetic  43.8 us (2%)
    all_gather x2, waiting for transfers between devices, local_body(): lax.all_gather(normed, 'tp', axis=0, tiled=True)  199 us
    pallas_call x3, Pallas kernels, grad_w(): pl.pallas_call(functools.partial(grad_w_kernel, len(heads), head_dim), gr...  173 us
    pallas_call x3, Pallas kernels, attn_bwd(): pl.pallas_call(functools.partial(attn_bwd_kernel, groups, head_dim, head_...  158 us
    dot_general x6, matrix products, dot_f32(): lax.dot_general(lhs, rhs, (((lhs_dim,), (rhs_dim,)), ((), ())), preferred...  152 us
    all_gather x1, waiting for transfers between devices, local_body(): w_out_all = lax.all_gather(w_out_loc, 'tp', axis=0, tiled=True)  151 us
    pallas_call x3, Pallas kernels, qkv_project(): pl.pallas_call(functools.partial(qkv_kernel, q_cols, k_cols, head_dim, he...  129 us
    all_to_all x2, blocking collectives, local_body(): lax.all_to_all(o_b.reshape(n_dev, rows, q_cols), 'tp', split_axis=0, conc...  121 us
    ppermute x15, waiting for transfers between devices, swap(): return lax.ppermute(value, 'tp', [(d, d ^ bit) for d in range(n_dev)])  113 us
  transfers between devices with their start and end apart: 22, of which 7 were waited for; matrix products, arithmetic and copies ran while one was open for 12% of the time, Pallas kernels for 47%

profile of v3, /device:TPU:0, one launch (start us, length us, event | category | flops | bytes accessed | tf_op | source)
XLA Modules:
  0.0 1901.0 jit_solution(7726706420256890433)
XLA Ops:
  119.1 199.3 %all-gather.11.cloned.1.call-done = bf16[6144,5376]{1,0:T(8,128)(2,1)} async-done(((bf16[768,5376]{1,0:T(8,128)(2,1)}), bf16[6144,5376]{1,0:T(8,128)(2,1)}) %all-gather.11.cloned.1.call-update) | async-done | bytes 66060304 | tf_op jit(solution)/shard_map/all_gather | solution.py:666
  318.5 43.8 %qkv_project.5 = (bf16[3072,512]{1,0:T(8,128)(2,1)}, bf16[3072,256]{1,0:T(8,128)(2,1)}, bf16[3072,256]{1,0:T(8,128)(2,1)}) custom-call(bf16[8,768,5376]{2,1,0:T(8,128)(2,1)} %bitcast.51, bf16[5376,1024]{1,0:T(8,128)(2,1)} %copy.36.w_ref, f32[3072,128]{1,0:T(8,128)} %get-tuple-element.153.cos_ref, f32[3072,128]{1,0:T(8,128)} %get-tuple-element.154.sin_ref), custom_call_target="tpu_custom_call" | custom-call | flops 33822867456 | bytes 50331648 | tf_op jit(solution)/shard_map/qkv_project/pallas_call | solution.py:384
  366.1 32.5 %attn_fwd.5 = (bf16[3072,512]{1,0:T(8,128)(2,1)}, f32[2,12,1,512]{3,2,1,0:T(1,128)S(1)}) custom-call(s32[12]{0:T(128)S(1)} %get-tuple-element.140.first_ref, bf16[3072,512]{1,0:T(8,128)(2,1)} %get-tuple-element.75.q_ref, bf16[3072,256]{1,0:T(8,128)(2,1)S(1)} %copy-done.19, bf16[3072,256]{1,0:T(8,128)(2,1)S(1)} %copy-done.21, ...), custom_call_target="tpu_custom_call" | custom-call | flops 9663676416 | bytes 12582912 | tf_op jit(solution)/shard_map/attn_fwd/pallas_call | solution.py:472
  402.9 151.3 %all-gather.9.cloned.1.call-done.w_ref = bf16[4096,5376]{1,0:T(8,128)(2,1)} async-done(((bf16[512,5376]{1,0:T(8,128)(2,1)}), bf16[4096,5376]{1,0:T(8,128)(2,1)}) %all-gather.9.cloned.1.call-update) | async-done | bytes 44040208 | tf_op jit(solution)/shard_map/all_gather | solution.py:662
  597.9 42.7 %qkv_project.4 = (bf16[3072,512]{1,0:T(8,128)(2,1)}, bf16[3072,256]{1,0:T(8,128)(2,1)}, bf16[3072,256]{1,0:T(8,128)(2,1)}) custom-call(bf16[8,768,5376]{2,1,0:T(8,128)(2,1)} %bitcast.52, bf16[5376,1024]{1,0:T(8,128)(2,1)} %copy.36.w_ref, f32[3072,128]{1,0:T(8,128)} %get-tuple-element.151.cos_ref, f32[3072,128]{1,0:T(8,128)} %get-tuple-element.152.sin_ref), custom_call_target="tpu_custom_call" | custom-call | flops 33822867456 | bytes 50331648 | tf_op jit(solution)/shard_map/qkv_project/pallas_call | solution.py:384
  644.5 32.5 %attn_fwd.4 = (bf16[3072,512]{1,0:T(8,128)(2,1)}, f32[2,12,1,512]{3,2,1,0:T(1,128)S(1)}) custom-call(s32[12]{0:T(128)S(1)} %get-tuple-element.141.first_ref, bf16[3072,512]{1,0:T(8,128)(2,1)} %get-tuple-element.71.q_ref, bf16[3072,256]{1,0:T(8,128)(2,1)S(1)} %copy-done.23, bf16[3072,256]{1,0:T(8,128)(2,1)S(1)} %copy-done.25, ...), custom_call_target="tpu_custom_call" | custom-call | flops 9663676416 | bytes 12582912 | tf_op jit(solution)/shard_map/attn_fwd/pallas_call | solution.py:472
  677.0 63.7 %all_to_all.15.o_ref = bf16[8,384,512]{2,1,0:T(8,128)(2,1)} all-to-all(bf16[8,384,512]{2,1,0:T(8,128)(2,1)} %bitcast.50), channel_id=1, replica_groups=mesh['dp'=1,'tp'=8] {'tp'}, dimensions={0} | all-to-all | bytes 6291456 | tf_op jit(solution)/shard_map/all_to_all | solution.py:694
  785.4 42.9 %qkv_project.3 = (bf16[3072,512]{1,0:T(8,128)(2,1)}, bf16[3072,256]{1,0:T(8,128)(2,1)}, bf16[3072,256]{1,0:T(8,128)(2,1)}) custom-call(bf16[8,384,5376]{2,1,0:T(8,128)(2,1)} %bitcast.55, bf16[5376,1024]{1,0:T(8,128)(2,1)} %copy.36.w_ref, f32[3072,128]{1,0:T(8,128)} %get-tuple-element.149.cos_ref, f32[3072,128]{1,0:T(8,128)} %get-tuple-element.150.sin_ref), custom_call_target="tpu_custom_call" | custom-call | flops 33822867456 | bytes 50331648 | tf_op jit(solution)/shard_map/qkv_project/pallas_call | solution.py:384
  832.4 39.4 %attn_fwd.3 = (bf16[3072,512]{1,0:T(8,128)(2,1)}, f32[2,12,1,512]{3,2,1,0:T(1,128)S(1)}) custom-call(s32[12]{0:T(128)S(1)} %get-tuple-element.142.first_ref, bf16[3072,512]{1,0:T(8,128)(2,1)} %get-tuple-element.67.q_ref, bf16[3072,256]{1,0:T(8,128)(2,1)S(1)} %copy-done.27, bf16[3072,256]{1,0:T(8,128)(2,1)S(1)} %copy-done.29, s32[1,3072]{1,0:T(1,128)S(1)} %copy-done.7, ...), custom_call_target="tpu_custom_call" | custom-call | flops 9663676416 | bytes 12582912 | tf_op jit(solution)/shard_map/attn_fwd/pallas_call | solution.py:472
  871.8 57.7 %all_to_all.16.o_ref = bf16[8,384,512]{2,1,0:T(8,128)(2,1)} all-to-all(bf16[8,384,512]{2,1,0:T(8,128)(2,1)} %bitcast.40), channel_id=1, replica_groups=mesh['dp'=1,'tp'=8] {'tp'}, dimensions={0} | all-to-all | bytes 6291456 | tf_op jit(solution)/shard_map/all_to_all | solution.py:694
  993.6 50.4 %attn_bwd.5.d_ref = bf16[3072,1024]{1,0:T(8,128)(2,1)} custom-call(s32[12]{0:T(128)S(1)} %copy-done.18, bf16[3072,512]{1,0:T(8,128)(2,1)} %get-tuple-element.75.q_ref, bf16[3072,256]{1,0:T(8,128)(2,1)S(1)} %copy-done.20, bf16[3072,256]{1,0:T(8,128)(2,1)S(1)} %copy-done.22, bf16[3072,512]{1,0:T(8,128)(2,1)} %get-tuple-element.78.o_ref, ...), custom_call_target="tpu_custom_call" | custom-call | flops 24159191040 | bytes 25165824 | tf_op jit(solution)/shard_map/attn_bwd/pallas_call | solution.py:607
  1113.6 49.3 %attn_bwd.4.d_ref = bf16[3072,1024]{1,0:T(8,128)(2,1)} custom-call(s32[12]{0:T(128)S(1)} %copy-done.16, bf16[3072,512]{1,0:T(8,128)(2,1)} %get-tuple-element.71.q_ref, bf16[3072,256]{1,0:T(8,128)(2,1)S(1)} %copy-done.24, bf16[3072,256]{1,0:T(8,128)(2,1)S(1)} %copy-done.26, bf16[3072,512]{1,0:T(8,128)(2,1)} %get-tuple-element.74.o_ref, ...), custom_call_target="tpu_custom_call" | custom-call | flops 24159191040 | bytes 25165824 | tf_op jit(solution)/shard_map/attn_bwd/pallas_call | solution.py:607
  1189.1 54.9 %all-gather.13.cloned.1.call-done = bf16[3072,5376]{1,0:T(8,128)(2,1)} async-done(((bf16[384,5376]{1,0:T(8,128)(2,1)}), bf16[3072,5376]{1,0:T(8,128)(2,1)}) %all-gather.13.cloned.1.call-update) | async-done | bytes 33030160 | tf_op jit(solution)/shard_map/all_gather | solution.py:697
  1268.5 58.7 %attn_bwd.3.d_ref = bf16[3072,1024]{1,0:T(8,128)(2,1)} custom-call(s32[12]{0:T(128)S(1)} %copy-done.14, bf16[3072,512]{1,0:T(8,128)(2,1)} %get-tuple-element.67.q_ref, bf16[3072,256]{1,0:T(8,128)(2,1)S(1)} %copy-done.28, bf16[3072,256]{1,0:T(8,128)(2,1)S(1)} %copy-done.30, bf16[3072,512]{1,0:T(8,128)(2,1)} %get-tuple-element.70.o_ref, ...), custom_call_target="tpu_custom_call" | custom-call | flops 24159191040 | bytes 25165824 | tf_op jit(solution)/shard_map/attn_bwd/pallas_call | solution.py:607
  1401.2 29.9 %grad_normed_own.5 = (bf16[2,384,2688]{2,1,0:T(8,128)(2,1)}, bf16[2,384,2688]{2,1,0:T(8,128)(2,1)}, bf16[2,384,2688]{2,1,0:T(8,128)(2,1)}, bf16[2,384,2688]{2,1,0:T(8,128)(2,1)}) custom-call(s32[1]{0:T(128)} %bitcast.15.dst_ref, bf16[3072,1024]{1,0:T(8,128)(2,1)} %attn_bwd.5.d_ref, bf16[1024,5376]{1,0:T(8,128)(2,1)} %get-tuple-element.126.w_ref, ...), custom_call_target="tpu_custom_call" | custom-call | flops 16911433728 | bytes 44040192 | tf_op jit(solution)/shard_map/grad_normed_own/pallas_call | solution.py:238
  1432.5 29.6 %add_add_fusion = f32[512,5376]{1,0:T(8,128)} fusion(f32[512,5376]{1,0:T(8,128)} %fusion.7, f32[512,5376]{1,0:T(8,128)} %fusion.8, bf16[3072,512]{1,0:T(8,128)(2,1)S(1)} %copy-done.31, bf16[3072,5376]{1,0:T(8,128)(2,1)} %all-gather.13.cloned.1.call-done), kind=kOutput, calls=%fused_computation.1 | convolution fusion | flops 16916938752 | bytes 69206016 | tf_op jit(solution)/shard_map/dot_general | solution.py:21
  1462.7 29.6 %grad_normed_own.4 = (bf16[2,384,2688]{2,1,0:T(8,128)(2,1)}, bf16[2,384,2688]{2,1,0:T(8,128)(2,1)}, bf16[2,384,2688]{2,1,0:T(8,128)(2,1)}, bf16[2,384,2688]{2,1,0:T(8,128)(2,1)}) custom-call(s32[1]{0:T(128)} %bitcast.15.dst_ref, bf16[3072,1024]{1,0:T(8,128)(2,1)} %attn_bwd.4.d_ref, bf16[1024,5376]{1,0:T(8,128)(2,1)} %get-tuple-element.126.w_ref, ...), custom_call_target="tpu_custom_call" | custom-call | flops 16911433728 | bytes 44040192 | tf_op jit(solution)/shard_map/grad_normed_own/pallas_call | solution.py:238
  1494.3 29.7 %grad_normed_own.3 = (bf16[2,384,2688]{2,1,0:T(8,128)(2,1)}, bf16[2,384,2688]{2,1,0:T(8,128)(2,1)}, bf16[2,384,2688]{2,1,0:T(8,128)(2,1)}, bf16[2,384,2688]{2,1,0:T(8,128)(2,1)}) custom-call(s32[1]{0:T(128)} %bitcast.15.dst_ref, bf16[3072,1024]{1,0:T(8,128)(2,1)} %attn_bwd.3.d_ref, bf16[1024,5376]{1,0:T(8,128)(2,1)} %get-tuple-element.126.w_ref, ...), custom_call_target="tpu_custom_call" | custom-call | flops 16911433728 | bytes 44040192 | tf_op jit(solution)/shard_map/grad_normed_own/pallas_call | solution.py:238
  1526.1 51.2 %grad_w.3 = (f32[5376,4,128]{2,1,0:T(4,128)}, f32[5376,2,128]{2,1,0:T(2,128)}, f32[5376,2,128]{2,1,0:T(2,128)}) custom-call(bf16[8,768,5376]{2,1,0:T(8,128)(2,1)} %bitcast.53, bf16[3072,1024]{1,0:T(8,128)(2,1)} %attn_bwd.5.d_ref), custom_call_target="tpu_custom_call" | custom-call | flops 33822867456 | bytes 83361792 | tf_op jit(solution)/shard_map/grad_w/pallas_call | solution.py:347
  1584.5 61.5 %grad_w.4 = (f32[5376,4,128]{2,1,0:T(4,128)}, f32[5376,2,128]{2,1,0:T(2,128)}, f32[5376,2,128]{2,1,0:T(2,128)}) custom-call(bf16[8,384,5376]{2,1,0:T(8,128)(2,1)} %bitcast.56, bf16[3072,1024]{1,0:T(8,128)(2,1)} %attn_bwd.3.d_ref, f32[5376,4,128]{2,1,0:T(4,128)} %get-tuple-element.113.refs_0_, ...), custom_call_target="tpu_custom_call", output_to_operand_aliasing={{0}: (2, {}), {1}: (3, {}), {2}: (4, {})} | custom-call | flops 33822867456 | bytes 83361792 | tf_op jit(solution)/shard_map/grad_w/pallas_call | solution.py:347
  1654.4 45.9 %collective-permute-done.1.near_x_ref.refs_1_ = bf16[2,384,2688]{2,1,0:T(8,128)(2,1)S(1)} collective-permute-done((bf16[2,384,2688]{2,1,0:T(8,128)(2,1)}, bf16[2,384,2688]{2,1,0:T(8,128)(2,1)S(1)}, u32[]{:S(2)}, u32[]{:S(2)}) %collective-permute-start.1) | collective-permute-done | bytes 4128800 | tf_op jit(solution)/shard_map/ppermute | solution.py:681
  1701.7 29.7 %collective-permute-done.2.near_y_ref.refs_4_ = bf16[2,384,2688]{2,1,0:T(8,128)(2,1)} collective-permute-done((bf16[2,384,2688]{2,1,0:T(8,128)(2,1)}, bf16[2,384,2688]{2,1,0:T(8,128)(2,1)}, u32[]{:S(2)}, u32[]{:S(2)}) %collective-permute-start.2) | collective-permute-done | bytes 4128800 | tf_op jit(solution)/shard_map/ppermute | solution.py:681
  1737.8 37.9 %collective-permute-done.13.refs_2_ = bf16[384,2688]{1,0:T(8,128)(2,1)} collective-permute-done((bf16[384,2688]{1,0:T(8,128)(2,1)}, bf16[384,2688]{1,0:T(8,128)(2,1)}, u32[]{:S(2)}, u32[]{:S(2)}) %collective-permute-start.13) | collective-permute-done | bytes 2064416 | tf_op jit(solution)/shard_map/ppermute | solution.py:681
  1776.2 60.6 %grad_w.5 = (f32[5376,4,128]{2,1,0:T(4,128)}, f32[5376,2,128]{2,1,0:T(2,128)}, f32[5376,2,128]{2,1,0:T(2,128)}) custom-call(bf16[8,768,5376]{2,1,0:T(8,128)(2,1)} %bitcast.54, bf16[3072,1024]{1,0:T(8,128)(2,1)} %attn_bwd.4.d_ref, f32[5376,4,128]{2,1,0:T(4,128)} %get-tuple-element.116.refs_0_, ...), custom_call_target="tpu_custom_call", output_to_operand_aliasing={{0}: (2, {}), {1}: (3, {}), {2}: (4, {})} | custom-call | flops 33822867456 | bytes 83361792 | tf_op jit(solution)/shard_map/grad_w/pallas_call | solution.py:347
  (183 shorter events, 561.1 us)
Async XLA Ops:
  7.2 311.3 %all-gather.11.cloned.1.call-start = ((), (), s32[]{:S(2)}) async-start(), calls=%async_computation.5 | async-start | bytes 74317824 | tf_op jit(solution)/shard_map/all_gather | solution.py:666
  22.6 531.7 %all-gather.9.cloned.1.call-start = ((), (), s32[]{:S(2)}) async-start(), calls=%async_computation.4 | async-start | bytes 49545216 | tf_op jit(solution)/shard_map/all_gather | solution.py:662
  23.4 762.0 %all-gather.7.cloned.1.call-start = ((), (), s32[]{:S(2)}) async-start(), calls=%async_computation.3 | async-start | bytes 37158912 | tf_op jit(solution)/shard_map/all_gather | solution.py:666
  46.2 594.9 %copy-start.9 = (s32[1,3072]{1,0:T(1,128)}, s32[1,3072]{1,0:T(1,128)S(1)}, u32[]{:S(2)}) copy-start(s32[1,3072]{1,0:T(1,128)S(1)} %get-tuple-element.129.pos_ref) | copy-start | bytes 36868
  97.4 731.3 %copy-start.13 = (s32[12]{0:T(128)}, s32[12]{0:T(128)S(1)}, u32[]{:S(2)}) copy-start(s32[12]{0:T(128)S(1)} %get-tuple-element.142.first_ref) | copy-start | bytes 148
  398.6 155.7 %all-to-all-start.2 = ((bf16[8,384,512]{2,1,0:T(8,128)(2,1)}), bf16[8,384,512]{2,1,0:T(8,128)(2,1)}, u32[]{:S(2)}, u32[]{:S(2)}) async-start(bf16[8,384,512]{2,1,0:T(8,128)(2,1)} %bitcast.49), calls=%async_computation.2 | async-start | bytes 6291456 | tf_op jit(solution)/shard_map/all_to_all | solution.py:694
  402.1 567.0 %all-gather.17.cloned.1.call-start = ((), (), s32[]{:S(2)}) async-start(), calls=%async_computation.8 | async-start | bytes 37158912 | tf_op jit(solution)/shard_map/all_gather | solution.py:697
  594.0 494.9 %all-gather.15.cloned.1.call-start = ((), (), s32[]{:S(2)}) async-start(), calls=%async_computation.7 | async-start | bytes 37158912 | tf_op jit(solution)/shard_map/all_gather | solution.py:697
  779.5 464.5 %all-gather.13.cloned.1.call-start = ((), (), s32[]{:S(2)}) async-start(), calls=%async_computation.6 | async-start | bytes 37158912 | tf_op jit(solution)/shard_map/all_gather | solution.py:697
  1069.0 332.1 %collective-permute-start.10 = (bf16[4,384,5376]{2,1,0:T(8,128)(2,1)}, bf16[4,384,5376]{2,1,0:T(8,128)(2,1)}, u32[]{:S(2)}, u32[]{:S(2)}) collective-permute-start(bf16[4,384,5376]{2,1,0:T(8,128)(2,1)} %grad_normed_pair.5), channel_id=1, source_target_pairs={{0,1},{1,0},{2,3},{3,2},{4,5},{5,4},{6,7},{7,6}} | collective-permute-start | bytes 49545224 | tf_op jit(solution)/shard_map/ppermute | solution.py:681
  1189.1 273.6 %collective-permute-start.5 = (bf16[4,384,5376]{2,1,0:T(8,128)(2,1)}, bf16[4,384,5376]{2,1,0:T(8,128)(2,1)}, u32[]{:S(2)}, u32[]{:S(2)}) collective-permute-start(bf16[4,384,5376]{2,1,0:T(8,128)(2,1)} %grad_normed_pair.4), channel_id=1, source_target_pairs={{0,1},{1,0},{2,3},{3,2},{4,5},{5,4},{6,7},{7,6}} | collective-permute-start | bytes 49545224 | tf_op jit(solution)/shard_map/ppermute | solution.py:681
  1352.4 141.9 %collective-permute-start = (bf16[4,384,5376]{2,1,0:T(8,128)(2,1)}, bf16[4,384,5376]{2,1,0:T(8,128)(2,1)}, u32[]{:S(2)}, u32[]{:S(2)}) collective-permute-start(bf16[4,384,5376]{2,1,0:T(8,128)(2,1)} %grad_normed_pair.3), channel_id=1, source_target_pairs={{0,1},{1,0},{2,3},{3,2},{4,5},{5,4},{6,7},{7,6}} | collective-permute-start | bytes 49545224 | tf_op jit(solution)/shard_map/ppermute | solution.py:681
  1431.1 94.5 %collective-permute-start.11 = (bf16[2,384,2688]{2,1,0:T(8,128)(2,1)}, bf16[2,384,2688]{2,1,0:T(8,128)(2,1)}, u32[]{:S(2)}, u32[]{:S(2)}) collective-permute-start(bf16[2,384,2688]{2,1,0:T(8,128)(2,1)} %get-tuple-element.103), channel_id=1, source_target_pairs={{0,2},{1,3},{2,0},{3,1},{4,6},{5,7},{6,4},{7,5}} | collective-permute-start | bytes 12386312 | tf_op jit(solution)/shard_map/ppermute | solution.py:681
  1462.1 115.2 %collective-permute-start.12 = (bf16[2,384,2688]{2,1,0:T(8,128)(2,1)}, bf16[2,384,2688]{2,1,0:T(8,128)(2,1)}, u32[]{:S(2)}, u32[]{:S(2)}) collective-permute-start(bf16[2,384,2688]{2,1,0:T(8,128)(2,1)} %get-tuple-element.105), channel_id=1, source_target_pairs={{0,4},{1,5},{2,6},{3,7},{4,0},{5,1},{6,2},{7,3}} | collective-permute-start | bytes 12386312 | tf_op jit(solution)/shard_map/ppermute | solution.py:681
  1492.3 153.8 %collective-permute-start.6 = (bf16[2,384,2688]{2,1,0:T(8,128)(2,1)}, bf16[2,384,2688]{2,1,0:T(8,128)(2,1)S(1)}, u32[]{:S(2)}, u32[]{:S(2)}) collective-permute-start(bf16[2,384,2688]{2,1,0:T(8,128)(2,1)} %get-tuple-element.95), channel_id=1, source_target_pairs={{0,2},{1,3},{2,0},{3,1},{4,6},{5,7},{6,4},{7,5}} | collective-permute-start | bytes 12386312 | tf_op jit(solution)/shard_map/ppermute | solution.py:681
  1492.6 154.0 %collective-permute-start.7 = (bf16[2,384,2688]{2,1,0:T(8,128)(2,1)}, bf16[2,384,2688]{2,1,0:T(8,128)(2,1)}, u32[]{:S(2)}, u32[]{:S(2)}) collective-permute-start(bf16[2,384,2688]{2,1,0:T(8,128)(2,1)} %get-tuple-element.97), channel_id=1, source_target_pairs={{0,4},{1,5},{2,6},{3,7},{4,0},{5,1},{6,2},{7,3}} | collective-permute-start | bytes 12386312 | tf_op jit(solution)/shard_map/ppermute | solution.py:681
  1524.0 176.2 %collective-permute-start.1 = (bf16[2,384,2688]{2,1,0:T(8,128)(2,1)}, bf16[2,384,2688]{2,1,0:T(8,128)(2,1)S(1)}, u32[]{:S(2)}, u32[]{:S(2)}) collective-permute-start(bf16[2,384,2688]{2,1,0:T(8,128)(2,1)} %get-tuple-element.87), channel_id=1, source_target_pairs={{0,2},{1,3},{2,0},{3,1},{4,6},{5,7},{6,4},{7,5}} | collective-permute-start | bytes 12386312 | tf_op jit(solution)/shard_map/ppermute | solution.py:681
  1525.5 205.9 %collective-permute-start.2 = (bf16[2,384,2688]{2,1,0:T(8,128)(2,1)}, bf16[2,384,2688]{2,1,0:T(8,128)(2,1)}, u32[]{:S(2)}, u32[]{:S(2)}) collective-permute-start(bf16[2,384,2688]{2,1,0:T(8,128)(2,1)} %get-tuple-element.89), channel_id=1, source_target_pairs={{0,4},{1,5},{2,6},{3,7},{4,0},{5,1},{6,2},{7,3}} | collective-permute-start | bytes 12386312 | tf_op jit(solution)/shard_map/ppermute | solution.py:681
  1583.1 192.6 %collective-permute-start.13 = (bf16[384,2688]{1,0:T(8,128)(2,1)}, bf16[384,2688]{1,0:T(8,128)(2,1)}, u32[]{:S(2)}, u32[]{:S(2)}) collective-permute-start(bf16[384,2688]{1,0:T(8,128)(2,1)} %get-tuple-element.106), channel_id=1, source_target_pairs={{0,4},{1,5},{2,6},{3,7},{4,0},{5,1},{6,2},{7,3}} | collective-permute-start | bytes 6193160 | tf_op jit(solution)/shard_map/ppermute | solution.py:681
  1646.0 190.8 %collective-permute-start.14 = (bf16[384,2688]{1,0:T(8,128)(2,1)}, bf16[384,2688]{1,0:T(8,128)(2,1)}, u32[]{:S(2)}, u32[]{:S(2)}) collective-permute-start(bf16[384,2688]{1,0:T(8,128)(2,1)} %get-tuple-element.107), channel_id=1, source_target_pairs={{0,2},{1,3},{2,0},{3,1},{4,6},{5,7},{6,4},{7,5}} | collective-permute-start | bytes 6193160 | tf_op jit(solution)/shard_map/ppermute | solution.py:681
  1653.8 196.6 %collective-permute-start.8 = (bf16[384,2688]{1,0:T(8,128)(2,1)}, bf16[384,2688]{1,0:T(8,128)(2,1)S(1)}, u32[]{:S(2)}, u32[]{:S(2)}) collective-permute-start(bf16[384,2688]{1,0:T(8,128)(2,1)} %get-tuple-element.98), channel_id=1, source_target_pairs={{0,4},{1,5},{2,6},{3,7},{4,0},{5,1},{6,2},{7,3}} | collective-permute-start | bytes 6193160 | tf_op jit(solution)/shard_map/ppermute | solution.py:681
  1700.3 150.1 %collective-permute-start.9 = (bf16[384,2688]{1,0:T(8,128)(2,1)}, bf16[384,2688]{1,0:T(8,128)(2,1)S(1)}, u32[]{:S(2)}, u32[]{:S(2)}) collective-permute-start(bf16[384,2688]{1,0:T(8,128)(2,1)} %get-tuple-element.99), channel_id=1, source_target_pairs={{0,2},{1,3},{2,0},{3,1},{4,6},{5,7},{6,4},{7,5}} | collective-permute-start | bytes 6193160 | tf_op jit(solution)/shard_map/ppermute | solution.py:681
  1737.2 128.7 %collective-permute-start.3 = (bf16[384,2688]{1,0:T(8,128)(2,1)}, bf16[384,2688]{1,0:T(8,128)(2,1)S(1)}, u32[]{:S(2)}, u32[]{:S(2)}) collective-permute-start(bf16[384,2688]{1,0:T(8,128)(2,1)} %get-tuple-element.90), channel_id=1, source_target_pairs={{0,4},{1,5},{2,6},{3,7},{4,0},{5,1},{6,2},{7,3}} | collective-permute-start | bytes 6193160 | tf_op jit(solution)/shard_map/ppermute | solution.py:681
  1775.7 90.3 %collective-permute-start.4 = (bf16[384,2688]{1,0:T(8,128)(2,1)}, bf16[384,2688]{1,0:T(8,128)(2,1)S(1)}, u32[]{:S(2)}, u32[]{:S(2)}) collective-permute-start(bf16[384,2688]{1,0:T(8,128)(2,1)} %get-tuple-element.91), channel_id=1, source_target_pairs={{0,2},{1,3},{2,0},{3,1},{4,6},{5,7},{6,4},{7,5}} | collective-permute-start | bytes 6193160 | tf_op jit(solution)/shard_map/ppermute | solution.py:681
  (42 other events, 2090.6 us)
Sparse Core Ops, SparseCore 0:
  22.7 295.6 all-gather.10
  320.3 233.9 all-gather.8
  556.7 185.1 all-gather.6
  744.1 186.3 all-gather.16
  932.2 156.6 all-gather.14
  1091.1 152.8 all-gather.12

commit v4 on v3

--- a/solution.py
+++ b/solution.py
@@ -167,32 +167,58 @@
     )(*pieces, x_in, grad_out, gain, dg_in, *([] if first else [gx_prev]))
 
 
-def out_proj_kernel(o_ref, w_ref, r_ref):
-    o_all = jnp.concatenate([o_ref[d] for d in range(o_ref.shape[0])], axis=1)
-    r_ref[...] = jnp.dot(o_all, w_ref[...], preferred_element_type=jnp.float32).astype(r_ref.dtype)
-
-
-def out_proj(o_mine, w_all):
+def out_proj_kernel(me_ref, o_ref, *refs):
+    pieces, r_ref = refs[:-1], refs[-1]
+    o_all = jnp.concatenate([o_ref[me_ref[0] ^ k] for k in PIECE_DEVICES], axis=1)
+    w_all = jnp.concatenate([piece[...] for piece in pieces], axis=0)
+    r_ref[...] = jnp.dot(o_all, w_all, preferred_element_type=jnp.float32).astype(r_ref.dtype)
+
+
+def out_proj(me, o_mine, pieces):
     n_dev, rows, cols = o_mine.shape
-    depth = w_all.shape[1]
+    depth = pieces[0].shape[1]
     tile = 768
     return pl.pallas_call(
         out_proj_kernel,
-        grid=(depth // tile,),
-        in_specs=[
-            pl.BlockSpec((n_dev, rows, cols), lambda i: (0, 0, 0), pipeline_mode=pl.Buffered(1)),
-            pl.BlockSpec((n_dev * cols, tile), lambda i: (0, i)),
-        ],
-        out_specs=pl.BlockSpec((rows, tile), lambda i: (0, i)),
+        grid_spec=pltpu.PrefetchScalarGridSpec(
+            num_scalar_prefetch=1,
+            grid=(depth // tile,),
+            in_specs=[pl.BlockSpec((n_dev, rows, cols), lambda i, me: (0, 0, 0), pipeline_mode=pl.Buffered(1))]
+            + [pl.BlockSpec((piece.shape[0], tile), lambda i, me: (0, i)) for piece in pieces],
+            out_specs=pl.BlockSpec((rows, tile), lambda i, me: (0, i)),
+        ),
         out_shape=jax.ShapeDtypeStruct((rows, depth), jnp.bfloat16),
-        compiler_params=pltpu.CompilerParams(vmem_limit_bytes=54 * 1024 * 1024),
+        compiler_params=pltpu.CompilerParams(vmem_limit_bytes=40 * 1024 * 1024),
         cost_estimate=pl.CostEstimate(flops=2 * n_dev * rows * cols * depth, bytes_accessed=2 * n_dev * cols * depth, transcendentals=0),
         name="out_proj",
-    )(o_mine, w_all)
-
-
-def pair_core_kernel(dst_ref, d_ref, w_ref, out_ref):
-    out_ref[0] = jnp.dot(d_ref[...], w_ref[...], preferred_element_type=jnp.float32).astype(out_ref.dtype)
+    )(me, o_mine, *pieces)
+
+
+PIECE_DEVICES = (0, 1, 2, 4, 3, 5, 6, 7)
+
+
+PIECE = 1024
+
+
+def for_columns(width, visit):
+    @pl.loop(0, width // PIECE)
+    def _(c):
+        visit(pl.ds(pl.multiple_of(c * PIECE, PIECE), PIECE))
+
+    if width % PIECE:
+        visit(pl.ds(width // PIECE * PIECE, width % PIECE))
+
+
+def pair_core_kernel(dst_ref, d0_ref, d1_ref, w_ref, out_ref):
+    rows = d0_ref.shape[0]
+    d_two = jnp.concatenate([d0_ref[...], d1_ref[...]], axis=0)
+
+    def visit(cols):
+        value = jnp.dot(d_two, w_ref[:, cols], preferred_element_type=jnp.float32).astype(out_ref.dtype)
+        out_ref[0, :, cols] = value[:rows]
+        out_ref[1, :, cols] = value[rows:]
+
+    for_columns(w_ref.shape[1], visit)
 
 
 def grad_normed_pair(dst, d_lin, w_t, rows):
@@ -202,56 +228,80 @@
         pair_core_kernel,
         grid_spec=pltpu.PrefetchScalarGridSpec(
             num_scalar_prefetch=1,
-            grid=(2, 4),
+            grid=(2, 2),
             in_specs=[
-                pl.BlockSpec((rows, cols), lambda h, r, dst: (dst[0] ^ (2 * r), 0)),
-                pl.BlockSpec((cols, half), lambda h, r, dst: (0, h)),
+                pl.BlockSpec((rows, cols), lambda h, p, dst: (dst[0] ^ (4 * p), 0)),
+                pl.BlockSpec((rows, cols), lambda h, p, dst: (dst[0] ^ (4 * p + 2), 0)),
+                pl.BlockSpec((cols, half), lambda h, p, dst: (0, h)),
             ],
-            out_specs=pl.BlockSpec((1, rows, half), lambda h, r, dst: (r, 0, h)),
+            out_specs=pl.BlockSpec((2, rows, half), lambda h, p, dst: (p, 0, h)),
         ),
         out_shape=jax.ShapeDtypeStruct((4, rows, depth), jnp.bfloat16),
-        compiler_params=pltpu.CompilerParams(vmem_limit_bytes=48 * 1024 * 1024),
+        compiler_params=pltpu.CompilerParams(vmem_limit_bytes=54 * 1024 * 1024),
         cost_estimate=pl.CostEstimate(flops=8 * rows * cols * depth, bytes_accessed=2 * (4 * rows * depth + cols * depth), transcendentals=0),
         name="grad_normed_pair",
-    )(dst, d_lin, w_t)
+    )(dst, d_lin, d_lin, w_t)
 
 
 def route(h, j):
     return jnp.where(h == 0, (2 * j + 1) % 5, (j + 2) % 4)
 
 
-def own_core_kernel(dst_ref, d_ref, w_ref, add_ref, *outs):
-    step = 4 * pl.program_id(0) + pl.program_id(1)
-    value = jnp.dot(d_ref[...], w_ref[...], preferred_element_type=jnp.float32) + add_ref[0].astype(jnp.float32)
-    value = value.astype(jnp.bfloat16)
+def own_core_kernel(dst_ref, d0_ref, d1_ref, w_ref, add0_ref, add1_ref, *refs):
+    outs, (stage, sem) = refs[:4], refs[4:]
+    rows = d0_ref.shape[0]
+    step = 2 * pl.program_id(0) + pl.program_id(1)
+    slot = step % 2
+    d_two = jnp.concatenate([d0_ref[...], d1_ref[...]], axis=0)
+
+    def copy_out(out):
+        return pltpu.make_async_copy(stage.at[slot], out, sem.at[slot])
+
+    @pl.when(step >= 2)
+    def _():
+        copy_out(outs[0]).wait()
+
+    def visit(cols):
+        value = jnp.dot(d_two, w_ref[:, cols], preferred_element_type=jnp.float32)
+        stage[slot, 0, :, cols] = (value[:rows] + add0_ref[0, :, cols].astype(jnp.float32)).astype(stage.dtype)
+        stage[slot, 1, :, cols] = (value[rows:] + add1_ref[0, :, cols].astype(jnp.float32)).astype(stage.dtype)
+
+    for_columns(w_ref.shape[1], visit)
     for i, out in enumerate(outs):
-        @pl.when((step >= 2 * i) & (step < 2 * i + 2))
+        @pl.when(step == i)
         def _(out=out):
-            out[0] = value
+            copy_out(out).start()
+
+    @pl.when(step == 3)
+    def _():
+        for s in range(2):
+            pltpu.make_async_copy(stage.at[s], outs[0], sem.at[s]).wait()
 
 
 def grad_normed_own(dst, d_lin, w_t, from_pair):
     _, rows, depth = from_pair.shape
     cols = w_t.shape[0]
     half = depth // 2
-    outs = [pl.BlockSpec((1, rows, half), lambda h, j, dst, i=i: (jnp.clip(4 * h + j - 2 * i, 0, 1), 0, 0)) for i in range(4)]
     return pl.pallas_call(
         own_core_kernel,
         grid_spec=pltpu.PrefetchScalarGridSpec(
             num_scalar_prefetch=1,
-            grid=(2, 4),
+            grid=(2, 2),
             in_specs=[
-                pl.BlockSpec((rows, cols), lambda h, j, dst: (dst[0] ^ (2 * route(h, j)), 0)),
-                pl.BlockSpec((cols, half), lambda h, j, dst: (0, h)),
-                pl.BlockSpec((1, rows, half), lambda h, j, dst: (route(h, j), 0, h)),
+                pl.BlockSpec((rows, cols), lambda h, p, dst: (dst[0] ^ (2 * route(h, 2 * p)), 0)),
+                pl.BlockSpec((rows, cols), lambda h, p, dst: (dst[0] ^ (2 * route(h, 2 * p + 1)), 0)),
+                pl.BlockSpec((cols, half), lambda h, p, dst: (0, h)),
+                pl.BlockSpec((1, rows, half), lambda h, p, dst: (route(h, 2 * p), 0, h)),
+                pl.BlockSpec((1, rows, half), lambda h, p, dst: (route(h, 2 * p + 1), 0, h)),
             ],
-            out_specs=outs,
+            out_specs=[pl.BlockSpec(memory_space=pl.ANY)] * 4,
+            scratch_shapes=[pltpu.VMEM((2, 2, rows, half), jnp.bfloat16), pltpu.SemaphoreType.DMA((2,))],
         ),
         out_shape=[jax.ShapeDtypeStruct((2, rows, half), jnp.bfloat16)] * 4,
         compiler_params=pltpu.CompilerParams(vmem_limit_bytes=56 * 1024 * 1024),
         cost_estimate=pl.CostEstimate(flops=8 * rows * cols * depth, bytes_accessed=2 * (8 * rows * depth + cols * depth), transcendentals=0),
         name="grad_normed_own",
-    )(dst, d_lin, w_t, from_pair)
+    )(dst, d_lin, d_lin, w_t, from_pair, from_pair)
 
 
 def fold_kernel(keep_x_ref, near_x_ref, keep_y_ref, near_y_ref, x_ref, y_ref):
@@ -327,37 +377,80 @@
     )(d_pre, d_post)
 
 
-def grad_w_kernel(n_out, head_dim, a_ref, d_ref, *refs):
-    prev, outs = refs[:-n_out], refs[-n_out:]
+def grad_w_kernel(has_prev, split, head_dim, a_ref, d_ref, *refs):
+    outs = refs[1:] if has_prev else refs
     n_dev, rows, tile = a_ref.shape
-    total = dot_f32(a_ref[...].reshape(n_dev * rows, tile), d_ref[...], 0, 0)
-    col = 0
-    for i, out in enumerate(outs):
-        for h in range(out.shape[1]):
-            part = total[:, col:col + head_dim]
-            out[:, h, :] = part + prev[i][:, h, :] if prev else part
-            col += head_dim
-
-
-def grad_w(gathered, slot, rows, d_lin, heads, head_dim, prev):
+    step = 256
+
+    @pl.loop(0, tile // step)
+    def _(m):
+        cols = pl.ds(pl.multiple_of(m * step, step), step)
+        total = dot_f32(a_ref[:, :, cols].reshape(n_dev * rows, step), d_ref[...], 0, 0)
+        if has_prev:
+            total = total + refs[0][cols, :]
+        if not split:
+            outs[0][cols, :] = total
+            return
+        col = 0
+        for out in outs:
+            for h in range(out.shape[1]):
+                out[cols, h, :] = total[:, col:col + head_dim]
+                col += head_dim
+
+
+def grad_w(gathered, slot, rows, d_lin, heads, head_dim, prev, last):
     n_dev, _, depth = gathered.shape
     seq_len, cols = d_lin.shape
-    tile = 384
-    outs = [pl.BlockSpec((tile, h, head_dim), lambda i: (i, 0, 0)) for h in heads]
-    return pl.pallas_call(
-        functools.partial(grad_w_kernel, len(heads), head_dim),
+    tile = 768
+    flat = pl.BlockSpec((tile, cols), lambda i: (i, 0))
+    has_prev = prev is not None
+    if last:
+        out_specs = [pl.BlockSpec((tile, h, head_dim), lambda i: (i, 0, 0)) for h in heads]
+        out_shape = [jax.ShapeDtypeStruct((depth, h, head_dim), jnp.float32) for h in heads]
+    else:
+        out_specs, out_shape = flat, jax.ShapeDtypeStruct((depth, cols), jnp.float32)
+    return pl.pallas_call(
+        functools.partial(grad_w_kernel, has_prev, last, head_dim),
         grid=(depth // tile,),
         in_specs=[
             pl.BlockSpec((n_dev, rows, tile), lambda i: (0, slot, i)),
             pl.BlockSpec((seq_len, cols), lambda i: (0, 0), pipeline_mode=pl.Buffered(1)),
-        ] + (outs if prev else []),
-        out_specs=outs,
-        out_shape=[jax.ShapeDtypeStruct((depth, h, head_dim), jnp.float32) for h in heads],
-        input_output_aliases={2 + i: i for i in range(len(prev))},
-        compiler_params=pltpu.CompilerParams(vmem_limit_bytes=56 * 1024 * 1024),
+        ] + ([flat] if has_prev else []),
+        out_specs=out_specs,
+        out_shape=out_shape,
+        input_output_aliases={2: 0} if has_prev and not last else {},
+        compiler_params=pltpu.CompilerParams(vmem_limit_bytes=58 * 1024 * 1024),
         cost_estimate=pl.CostEstimate(flops=2 * seq_len * depth * cols, bytes_accessed=2 * seq_len * (depth + cols) + 8 * depth * cols, transcendentals=0),
         name="grad_w",
-    )(gathered, d_lin, *prev)
+    )(gathered, d_lin, *([prev] if has_prev else []))
+
+
+def grad_wo_kernel(has_prev, o_ref, d_ref, *refs):
+    out = refs[-1]
+    total = dot_f32(o_ref[...], d_ref[...], 0, 0)
+    out[...] = total + refs[0][...] if has_prev else total
+
+
+def grad_wo_sum(o_all, d_proj, prev):
+    seq_len, cols = o_all.shape
+    depth = d_proj.shape[1]
+    tile = 768
+    has_prev = prev is not None
+    flat = pl.BlockSpec((cols, tile), lambda i: (0, i))
+    return pl.pallas_call(
+        functools.partial(grad_wo_kernel, has_prev),
+        grid=(depth // tile,),
+        in_specs=[
+            pl.BlockSpec((seq_len, cols), lambda i: (0, 0), pipeline_mode=pl.Buffered(1)),
+            pl.BlockSpec((seq_len, tile), lambda i: (0, i)),
+        ] + ([flat] if has_prev else []),
+        out_specs=flat,
+        out_shape=jax.ShapeDtypeStruct((cols, depth), jnp.float32),
+        input_output_aliases={2: 0} if has_prev else {},
+        compiler_params=pltpu.CompilerParams(vmem_limit_bytes=54 * 1024 * 1024),
+        cost_estimate=pl.CostEstimate(flops=2 * seq_len * depth * cols, bytes_accessed=2 * seq_len * (depth + cols) + 8 * depth * cols, transcendentals=0),
+        name="grad_wo",
+    )(o_all, d_proj, *([prev] if has_prev else []))
 
 
 def qkv_kernel(q_cols, k_cols, head_dim, q_scale, a_ref, w_ref, cos_ref, sin_ref, q_ref, k_ref, v_ref):
@@ -638,7 +731,7 @@
 
 SEQ_ORDER = (1, 2, 0)
 GW_ORDER = (1, 0, 2)
-GWO_ORDER = (2, 1, 0)
+GWO_ORDER = (1, 0, 2)
 
 
 def solution(mesh):
@@ -658,13 +751,21 @@
 
         gain_pre_row, gain_post_row = gain_pre[None, :], gain_post[None, :]
         rows = x_in.shape[1]
+        gathered = {}
+        for b in SEQ_ORDER:
+            normed = pre_norm(x_in, gain_pre_row, b, 1)
+            gathered[b] = (lax.all_gather(normed, 'tp', axis=0, tiled=True).reshape(n_dev, rows, depth), 0)
+
+        def swap(value, bit):
+            return lax.ppermute(value, 'tp', [(d, d ^ bit) for d in range(n_dev)])
+
         w_out_loc = w_out.reshape(q_cols, depth)
-        w_out_all = lax.all_gather(w_out_loc, 'tp', axis=0, tiled=True)
-        gathered = {}
-        for first_seq, count in ((1, 2), (0, 1)):
-            normed = pre_norm(x_in, gain_pre_row, first_seq, count)
-            whole = lax.all_gather(normed, 'tp', axis=0, tiled=True).reshape(n_dev, count * rows, depth)
-            gathered.update({first_seq + i: (whole, i) for i in range(count)})
+        mid = q_cols // 2
+        near_w = {bit: swap(w_out_loc, bit) for bit in (1, 2, 4)}
+        far_w = (swap(near_w[2][:mid], 4), swap(near_w[4][mid:], 2))
+        other_core = [swap(near_w[2], 1), swap(near_w[4], 1)]
+        far_other = [swap(part, 1) for part in far_w]
+        w_out_pieces = (w_out_loc, near_w[1], near_w[2], near_w[4], *other_core, *far_w, *far_other)
 
         pos_all = lax.all_gather(positions, 'tp', axis=1, tiled=True)
         seq_len = pos_all.shape[1]
@@ -674,11 +775,7 @@
         first_blk = jnp.sum(before.astype(jnp.int32), axis=-1) // BLK
         w_all = jnp.concatenate([w_query.reshape(depth, q_cols), w_key.reshape(depth, k_cols), w_value.reshape(depth, k_cols)], axis=1)
         w_t = w_all.T
-        me = lax.axis_index('tp')
-        own_dst, pair_dst = me[None], me[None] ^ 1
-
-        def swap(value, bit):
-            return lax.ppermute(value, 'tp', [(d, d ^ bit) for d in range(n_dev)])
+        me = lax.axis_index('tp')[None]
 
         saved, d_proj_all = {}, {}
         y_out, d_post = None, jnp.zeros((1, depth), jnp.float32)
@@ -692,7 +789,7 @@
             q_b, k_b, v_b = qkv_project(*gathered[b], rows, w_all, cos_t, sin_t, q_cols, k_cols, head_dim)
             o_b, lse_b = attn_fwd(q_b, k_b, v_b, pos_b, key_pos, first_blk[b], groups, head_dim)
             o_mine = lax.all_to_all(o_b.reshape(n_dev, rows, q_cols), 'tp', split_axis=0, concat_axis=0, tiled=True)
-            proj = out_proj(o_mine, w_out_all)
+            proj = out_proj(me, o_mine, w_out_pieces)
             y_out, d_proj, d_post = post_norm(proj, x_in, grad_out, gain_post_row, d_post, y_out, b)
             d_proj_all[b] = lax.all_gather(d_proj, 'tp', axis=0, tiled=True)
             saved[b] = (q_b, k_b, v_b, o_b, pos_b, key_pos, lse_b, cos_t, sin_t)
@@ -703,21 +800,21 @@
             q_b, k_b, v_b, o_b, pos_b, key_pos, lse_b, cos_t, sin_t = saved[b]
             d_o = dot_f32(d_proj_all[b], w_out_loc, 1, 1).astype(jnp.bfloat16)
             d_lin[b] = attn_bwd(q_b, k_b, v_b, o_b, d_o, pos_b, key_pos, lse_b, first_blk[b], cos_t, sin_t, groups, head_dim)
-            pair = grad_normed_pair(pair_dst, d_lin[b], w_t, rows)
+            pair = grad_normed_pair(me ^ 1, d_lin[b], w_t, rows)
             from_pair = swap(pair, 1)
-            send_x, keep_x, send_y, keep_y = grad_normed_own(own_dst, d_lin[b], w_t, from_pair)
+            send_x, keep_x, send_y, keep_y = grad_normed_own(me, d_lin[b], w_t, from_pair)
             near_x = swap(send_x, 2)
             near_y = swap(send_y, 4)
             fold_x, fold_y = fold(keep_x, near_x, keep_y, near_y)
             far_x = swap(fold_x, 4)
             far_y = swap(fold_y, 2)
             grad_x, d_pre = pre_grad((keep_x, near_x, far_x, keep_y, near_y, far_y), x_in, grad_out, gain_pre_row, d_pre, grad_x, b)
-        grad_wo = jnp.zeros((), jnp.float32)
+        grad_wo = None
         for b in GWO_ORDER:
-            grad_wo = grad_wo + dot_f32(saved[b][3], d_proj_all[b], 0, 0)
-        grads = ()
+            grad_wo = grad_wo_sum(saved[b][3], d_proj_all[b], grad_wo)
+        grads = None
         for b in GW_ORDER:
-            grads = grad_w(*gathered[b], rows, d_lin[b], (heads_loc, kv_loc, kv_loc), head_dim, grads)
+            grads = grad_w(*gathered[b], rows, d_lin[b], (heads_loc, kv_loc, kv_loc), head_dim, grads, b == GW_ORDER[-1])
         grad_wq, grad_wk, grad_wv = grads
         grad_pre, grad_post = gain_sum(d_pre, d_post, n_dev)
         grad_pre, grad_post = grad_pre[0], grad_post[0]

time: 1910 us -> 1860 us (0.974)
  waiting for transfers between devices: 540 us -> 398 us
  blocking collectives: 136 us -> 238 us
  matrix products: 152 us -> 75.6 us
  Pallas kernels: 938 us -> 979 us
    all_gather x3, waiting for transfers between devices: 351 us -> 0.02 us  [local_body(): lax.all_gather(normed, 'tp', axis=0, tiled=True).reshape(n_dev, rows, depth)]
    all_gather x1, blocking collectives: 14.1 us -> 238 us  [local_body(): pos_all = lax.all_gather(positions, 'tp', axis=1, tiled=True)]
    all_to_all x2 -> x0, blocking collectives: 121 us -> none  [local_body(): lax.all_to_all(o_b.reshape(n_dev, rows, q_cols), 'tp', split_axis=0, conc...]
    all_to_all x1 -> x3, waiting for transfers between devices: 0.01 us -> 107 us  [local_body(): lax.all_to_all(o_b.reshape(n_dev, rows, q_cols), 'tp', split_axis=0, conc...]
    ppermute x15 -> x24, waiting for transfers between devices: 113 us -> 199 us  [swap(): return lax.ppermute(value, 'tp', [(d, d ^ bit) for d in range(n_dev)])]
    dot_general x6 -> x3, matrix products: 152 us -> 75.6 us  [dot_f32(): lax.dot_general(lhs, rhs, (((lhs_dim,), (rhs_dim,)), ((), ())), preferred...]
    pallas_call x6 -> x9, Pallas kernels: 252 us -> 297 us  [the longest x3 147 us: grad_w(): pl.pallas_call(functools.partial(grad_w_kernel, has_prev, last, head_dim)...]
    unnamed x91 -> x77, local copies, waits for them, and re-layouts: 43.2 us -> 46.7 us
  transfers between devices with their start and end apart: 22 -> 33, of which waited for: 7 -> 9; matrix products, arithmetic and copies ran while one was open for 12% -> 9% of each run, Pallas kernels for 47% -> 51%
where the time goes in v4:
time: 1860 us; the launch traced here: 1850 us
  Pallas kernels  979 us (53%)
  waiting for transfers between devices  398 us (21%)
  blocking collectives  238 us (13%)
  matrix products  75.6 us (4%)
  local copies, waits for them, and re-layouts  70.8 us (4%)
  other arithmetic  43 us (2%)
  starting transfers between devices  28.3 us (2%)
    all_gather x1, blocking collectives, local_body(): pos_all = lax.all_gather(positions, 'tp', axis=1, tiled=True)  238 us
    ppermute x24, waiting for transfers between devices, swap(): return lax.ppermute(value, 'tp', [(d, d ^ bit) for d in range(n_dev)])  199 us
    pallas_call x3, Pallas kernels, attn_bwd(): pl.pallas_call(functools.partial(attn_bwd_kernel, groups, head_dim, head_...  160 us
    pallas_call x3, Pallas kernels, grad_w(): pl.pallas_call(functools.partial(grad_w_kernel, has_prev, last, head_dim)...  147 us
    pallas_call x3, Pallas kernels, qkv_project(): pl.pallas_call(functools.partial(qkv_kernel, q_cols, k_cols, head_dim, he...  129 us
    all_to_all x3, waiting for transfers between devices, local_body(): lax.all_to_all(o_b.reshape(n_dev, rows, q_cols), 'tp', split_axis=0, conc...  107 us
    pallas_call x3, Pallas kernels, attn_fwd(): pl.pallas_call(functools.partial(attn_fwd_kernel, groups, head_dim), grid...  105 us
    all_gather x3, waiting for transfers between devices, local_body(): d_proj_all[b] = lax.all_gather(d_proj, 'tp', axis=0, tiled=True)  91.2 us
  transfers between devices with their start and end apart: 33, of which 9 were waited for; matrix products, arithmetic and copies ran while one was open for 9% of the time, Pallas kernels for 51%

profile of v4, /device:TPU:0, one launch (start us, length us, event | category | flops | bytes accessed | tf_op | source)
XLA Modules:
  0.0 1846.6 jit_solution(9085459976590183180)
XLA Ops:
  37.0 237.6 %all_gather.21 = s32[3,3072]{1,0:T(4,128)S(1)} all-gather(s32[3,384]{1,0:T(4,128)S(1)} %copy-done.36), channel_id=1, replica_groups=mesh['dp'=1,'tp'=8] {'tp'}, dimensions={1}, use_global_device_ids=true | all-gather | bytes 41472 | tf_op jit(solution)/shard_map/all_gather | solution.py:770
  356.4 71.9 %collective-permute-done.6.refs_7_ = bf16[256,5376]{1,0:T(8,128)(2,1)} collective-permute-done((bf16[256,5376]{1,0:T(8,128)(2,1)S(1)}, bf16[256,5376]{1,0:T(8,128)(2,1)}, u32[]{:S(2)}, u32[]{:S(2)}) %collective-permute-start.6) | collective-permute-done | bytes 2752544 | tf_op jit(solution)/shard_map/ppermute | solution.py:760
  429.3 42.9 %qkv_project.5 = (bf16[3072,512]{1,0:T(8,128)(2,1)}, bf16[3072,256]{1,0:T(8,128)(2,1)}, bf16[3072,256]{1,0:T(8,128)(2,1)}) custom-call(bf16[8,384,5376]{2,1,0:T(8,128)(2,1)} %bitcast.43, bf16[5376,1024]{1,0:T(8,128)(2,1)} %copy.33.w_ref, f32[3072,128]{1,0:T(8,128)} %get-tuple-element.141.cos_ref, f32[3072,128]{1,0:T(8,128)} %get-tuple-element.142.sin_ref), custom_call_target="tpu_custom_call" | custom-call | flops 33822867456 | bytes 50331648 | tf_op jit(solution)/shard_map/qkv_project/pallas_call | solution.py:477
  476.0 32.6 %attn_fwd.5 = (bf16[3072,512]{1,0:T(8,128)(2,1)}, f32[2,12,1,512]{3,2,1,0:T(1,128)S(1)}) custom-call(s32[12]{0:T(128)S(1)} %get-tuple-element.128.first_ref, bf16[3072,512]{1,0:T(8,128)(2,1)} %get-tuple-element.69.q_ref, bf16[3072,256]{1,0:T(8,128)(2,1)S(1)} %copy-done.13, bf16[3072,256]{1,0:T(8,128)(2,1)S(1)} %copy-done.15, ...), custom_call_target="tpu_custom_call" | custom-call | flops 9663676416 | bytes 12582912 | tf_op jit(solution)/shard_map/attn_fwd/pallas_call | solution.py:565
  512.4 70.7 %all-to-all-done.2.o_ref = bf16[8,384,512]{2,1,0:T(8,128)(2,1)S(1)} async-done(((bf16[8,384,512]{2,1,0:T(8,128)(2,1)}), bf16[8,384,512]{2,1,0:T(8,128)(2,1)S(1)}, u32[]{:S(2)}, u32[]{:S(2)}) %all-to-all-start.2) | async-done | bytes 3145760 | tf_op jit(solution)/shard_map/all_to_all | solution.py:791
  632.5 43.3 %qkv_project.4 = (bf16[3072,512]{1,0:T(8,128)(2,1)}, bf16[3072,256]{1,0:T(8,128)(2,1)}, bf16[3072,256]{1,0:T(8,128)(2,1)}) custom-call(bf16[8,384,5376]{2,1,0:T(8,128)(2,1)} %bitcast.41, bf16[5376,1024]{1,0:T(8,128)(2,1)} %copy.33.w_ref, f32[3072,128]{1,0:T(8,128)} %get-tuple-element.139.cos_ref, f32[3072,128]{1,0:T(8,128)} %get-tuple-element.140.sin_ref), custom_call_target="tpu_custom_call" | custom-call | flops 33822867456 | bytes 50331648 | tf_op jit(solution)/shard_map/qkv_project/pallas_call | solution.py:477
  679.7 32.6 %attn_fwd.4 = (bf16[3072,512]{1,0:T(8,128)(2,1)}, f32[2,12,1,512]{3,2,1,0:T(1,128)S(1)}) custom-call(s32[12]{0:T(128)S(1)} %get-tuple-element.129.first_ref, bf16[3072,512]{1,0:T(8,128)(2,1)} %get-tuple-element.65.q_ref, bf16[3072,256]{1,0:T(8,128)(2,1)S(1)} %copy-done.17, bf16[3072,256]{1,0:T(8,128)(2,1)S(1)} %copy-done.19, ...), custom_call_target="tpu_custom_call" | custom-call | flops 9663676416 | bytes 12582912 | tf_op jit(solution)/shard_map/attn_fwd/pallas_call | solution.py:565
  714.9 42.8 %qkv_project.3 = (bf16[3072,512]{1,0:T(8,128)(2,1)}, bf16[3072,256]{1,0:T(8,128)(2,1)}, bf16[3072,256]{1,0:T(8,128)(2,1)}) custom-call(bf16[8,384,5376]{2,1,0:T(8,128)(2,1)} %bitcast.45, bf16[5376,1024]{1,0:T(8,128)(2,1)} %copy.33.w_ref, f32[3072,128]{1,0:T(8,128)} %get-tuple-element.137.cos_ref, f32[3072,128]{1,0:T(8,128)} %get-tuple-element.138.sin_ref), custom_call_target="tpu_custom_call" | custom-call | flops 33822867456 | bytes 50331648 | tf_op jit(solution)/shard_map/qkv_project/pallas_call | solution.py:477
  761.1 39.4 %attn_fwd.3 = (bf16[3072,512]{1,0:T(8,128)(2,1)}, f32[2,12,1,512]{3,2,1,0:T(1,128)S(1)}) custom-call(s32[12]{0:T(128)S(1)} %get-tuple-element.130.first_ref, bf16[3072,512]{1,0:T(8,128)(2,1)} %get-tuple-element.61.q_ref, bf16[3072,256]{1,0:T(8,128)(2,1)S(1)} %copy-done.21, bf16[3072,256]{1,0:T(8,128)(2,1)S(1)} %copy-done.23, s32[1,3072]{1,0:T(1,128)S(1)} %copy-done.7, ...), custom_call_target="tpu_custom_call" | custom-call | flops 9663676416 | bytes 12582912 | tf_op jit(solution)/shard_map/attn_fwd/pallas_call | solution.py:565
  840.8 36.1 %all-to-all-done.o_ref = bf16[8,384,512]{2,1,0:T(8,128)(2,1)} async-done(((bf16[8,384,512]{2,1,0:T(8,128)(2,1)}), bf16[8,384,512]{2,1,0:T(8,128)(2,1)}, u32[]{:S(2)}, u32[]{:S(2)}) %all-to-all-start) | async-done | bytes 3145760 | tf_op jit(solution)/shard_map/all_to_all | solution.py:791
  915.4 26.9 %convolution_convert_fusion.do_ref = bf16[3072,512]{1,0:T(8,128)(2,1)} fusion(bf16[3072,5376]{1,0:T(8,128)(2,1)} %all-gather.17.cloned.1.call-done.d_ref, bf16[512,5376]{1,0:T(8,128)(2,1)} %bitcast.53), kind=kOutput, calls=%fused_computation.1 | convolution fusion | flops 16913006592 | bytes 41680896 | tf_op jit(solution)/shard_map/dot_general | solution.py:21
  942.4 50.3 %attn_bwd.5.d0_ref.d1_ref.d_ref = bf16[3072,1024]{1,0:T(8,128)(2,1)} custom-call(s32[12]{0:T(128)S(1)} %copy-done.12, bf16[3072,512]{1,0:T(8,128)(2,1)} %get-tuple-element.69.q_ref, bf16[3072,256]{1,0:T(8,128)(2,1)S(1)} %copy-done.14, bf16[3072,256]{1,0:T(8,128)(2,1)S(1)} %copy-done.16, bf16[3072,512]{1,0:T(8,128)(2,1)} %get-tuple-element.72.o_ref, ...), custom_call_target="tpu_custom_call" | custom-call | flops 24159191040 | bytes 25165824 | tf_op jit(solution)/shard_map/attn_bwd/pallas_call | solution.py:700
  1018.3 48.9 %all-gather.13.cloned.1.call-done.d_ref = bf16[3072,5376]{1,0:T(8,128)(2,1)} async-done(((bf16[384,5376]{1,0:T(8,128)(2,1)}), bf16[3072,5376]{1,0:T(8,128)(2,1)}) %all-gather.13.cloned.1.call-update) | async-done | bytes 33030160 | tf_op jit(solution)/shard_map/all_gather | solution.py:794
  1094.3 59.9 %attn_bwd.3.d0_ref.d1_ref.d_ref = bf16[3072,1024]{1,0:T(8,128)(2,1)} custom-call(s32[12]{0:T(128)S(1)} %get-tuple-element.130.first_ref, bf16[3072,512]{1,0:T(8,128)(2,1)} %get-tuple-element.61.q_ref, bf16[3072,256]{1,0:T(8,128)(2,1)S(1)} %copy-done.22, bf16[3072,256]{1,0:T(8,128)(2,1)S(1)} %copy-done.24, bf16[3072,512]{1,0:T(8,128)(2,1)} %get-tuple-element.64.o_ref, ...), custom_call_target="tpu_custom_call" | custom-call | flops 24159191040 | bytes 25165824 | tf_op jit(solution)/shard_map/attn_bwd/pallas_call | solution.py:700
  1180.0 42.3 %all-gather.15.cloned.1.call-done.d_ref = bf16[3072,5376]{1,0:T(8,128)(2,1)} async-done(((bf16[384,5376]{1,0:T(8,128)(2,1)}), bf16[3072,5376]{1,0:T(8,128)(2,1)}) %all-gather.15.cloned.1.call-update) | async-done | bytes 33030160 | tf_op jit(solution)/shard_map/all_gather | solution.py:794
  1246.7 50.1 %attn_bwd.4.d0_ref.d1_ref.d_ref = bf16[3072,1024]{1,0:T(8,128)(2,1)} custom-call(s32[12]{0:T(128)S(1)} %get-tuple-element.129.first_ref, bf16[3072,512]{1,0:T(8,128)(2,1)} %get-tuple-element.65.q_ref, bf16[3072,256]{1,0:T(8,128)(2,1)S(1)} %copy-done.18, bf16[3072,256]{1,0:T(8,128)(2,1)S(1)} %copy-done.20, bf16[3072,512]{1,0:T(8,128)(2,1)} %get-tuple-element.68.o_ref, ...), custom_call_target="tpu_custom_call" | custom-call | flops 24159191040 | bytes 25165824 | tf_op jit(solution)/shard_map/attn_bwd/pallas_call | solution.py:700
  1322.9 44.4 %grad_w.3.refs_0_ = f32[5376,1024]{1,0:T(8,128)} custom-call(bf16[8,384,5376]{2,1,0:T(8,128)(2,1)} %bitcast.44, bf16[3072,1024]{1,0:T(8,128)(2,1)} %attn_bwd.5.d0_ref.d1_ref.d_ref), custom_call_target="tpu_custom_call" | custom-call | flops 33822867456 | bytes 83361792 | tf_op jit(solution)/shard_map/grad_w/pallas_call | solution.py:412
  1367.3 27.5 %grad_normed_own.5 = (bf16[2,384,2688]{2,1,0:T(8,128)(2,1)}, bf16[2,384,2688]{2,1,0:T(8,128)(2,1)}, bf16[2,384,2688]{2,1,0:T(8,128)(2,1)}, bf16[2,384,2688]{2,1,0:T(8,128)(2,1)}) custom-call(s32[1]{0:T(128)} %bitcast.me_ref.dst_ref, bf16[3072,1024]{1,0:T(8,128)(2,1)} %attn_bwd.5.d0_ref.d1_ref.d_ref, bf16[3072,1024]{1,0:T(8,128)(2,1)} %attn_bwd.5.d0_ref.d1_ref.d_ref, ...), custom_call_target="tpu_custom_call" | custom-call | flops 16911433728 | bytes 44040192 | tf_op jit(solution)/shard_map/grad_normed_own/pallas_call | solution.py:285
  1396.9 45.6 %grad_w.4.refs_0_ = f32[5376,1024]{1,0:T(8,128)} custom-call(bf16[8,384,5376]{2,1,0:T(8,128)(2,1)} %bitcast.46, bf16[3072,1024]{1,0:T(8,128)(2,1)} %attn_bwd.3.d0_ref.d1_ref.d_ref, f32[5376,1024]{1,0:T(8,128)} %grad_w.3.refs_0_), custom_call_target="tpu_custom_call", output_to_operand_aliasing={{}: (2, {})} | custom-call | flops 33822867456 | bytes 83361792 | tf_op jit(solution)/shard_map/grad_w/pallas_call | solution.py:412
  1442.5 27.5 %grad_normed_own.3 = (bf16[2,384,2688]{2,1,0:T(8,128)(2,1)}, bf16[2,384,2688]{2,1,0:T(8,128)(2,1)}, bf16[2,384,2688]{2,1,0:T(8,128)(2,1)}, bf16[2,384,2688]{2,1,0:T(8,128)(2,1)}) custom-call(s32[1]{0:T(128)} %bitcast.me_ref.dst_ref, bf16[3072,1024]{1,0:T(8,128)(2,1)} %attn_bwd.3.d0_ref.d1_ref.d_ref, bf16[3072,1024]{1,0:T(8,128)(2,1)} %attn_bwd.3.d0_ref.d1_ref.d_ref, ...), custom_call_target="tpu_custom_call" | custom-call | flops 16911433728 | bytes 44040192 | tf_op jit(solution)/shard_map/grad_normed_own/pallas_call | solution.py:285
  1472.0 27.5 %grad_normed_own.4 = (bf16[2,384,2688]{2,1,0:T(8,128)(2,1)}, bf16[2,384,2688]{2,1,0:T(8,128)(2,1)}, bf16[2,384,2688]{2,1,0:T(8,128)(2,1)}, bf16[2,384,2688]{2,1,0:T(8,128)(2,1)}) custom-call(s32[1]{0:T(128)} %bitcast.me_ref.dst_ref, bf16[3072,1024]{1,0:T(8,128)(2,1)} %attn_bwd.4.d0_ref.d1_ref.d_ref, bf16[3072,1024]{1,0:T(8,128)(2,1)} %attn_bwd.4.d0_ref.d1_ref.d_ref, ...), custom_call_target="tpu_custom_call" | custom-call | flops 16911433728 | bytes 44040192 | tf_op jit(solution)/shard_map/grad_normed_own/pallas_call | solution.py:285
  1508.8 56.6 %grad_w.5 = (f32[5376,4,128]{2,1,0:T(4,128)}, f32[5376,2,128]{2,1,0:T(2,128)}, f32[5376,2,128]{2,1,0:T(2,128)}) custom-call(bf16[8,384,5376]{2,1,0:T(8,128)(2,1)} %bitcast.42, bf16[3072,1024]{1,0:T(8,128)(2,1)} %attn_bwd.4.d0_ref.d1_ref.d_ref, f32[5376,1024]{1,0:T(8,128)} %grad_w.4.refs_0_), custom_call_target="tpu_custom_call" | custom-call | flops 33822867456 | bytes 83361792 | tf_op jit(solution)/shard_map/grad_w/pallas_call | solution.py:412
  1597.6 66.5 %collective-permute-done.15.near_x_ref.refs_1_ = bf16[2,384,2688]{2,1,0:T(8,128)(2,1)} collective-permute-done((bf16[2,384,2688]{2,1,0:T(8,128)(2,1)}, bf16[2,384,2688]{2,1,0:T(8,128)(2,1)}, u32[]{:S(2)}, u32[]{:S(2)}) %collective-permute-start.15) | collective-permute-done | bytes 4128800 | tf_op jit(solution)/shard_map/ppermute | solution.py:760
  1672.0 37.9 %collective-permute-done.22.refs_2_ = bf16[384,2688]{1,0:T(8,128)(2,1)} collective-permute-done((bf16[384,2688]{1,0:T(8,128)(2,1)}, bf16[384,2688]{1,0:T(8,128)(2,1)}, u32[]{:S(2)}, u32[]{:S(2)}) %collective-permute-start.22) | collective-permute-done | bytes 2064416 | tf_op jit(solution)/shard_map/ppermute | solution.py:760
  (192 shorter events, 569.9 us)
Async XLA Ops:
  7.2 422.1 %all-gather.11.cloned.1.call-start = ((), (), s32[]{:S(2)}) async-start(), calls=%async_computation.5 | async-start | bytes 37158912 | tf_op jit(solution)/shard_map/all_gather | solution.py:757
  16.2 616.3 %all-gather.9.cloned.1.call-start = ((), (), s32[]{:S(2)}) async-start(), calls=%async_computation.4 | async-start | bytes 37158912 | tf_op jit(solution)/shard_map/all_gather | solution.py:757
  24.0 690.9 %all-gather.7.cloned.1.call-start = ((), (), s32[]{:S(2)}) async-start(), calls=%async_computation.3 | async-start | bytes 37158912 | tf_op jit(solution)/shard_map/all_gather | solution.py:757
  32.1 279.1 %collective-permute-start.2 = (bf16[512,5376]{1,0:T(8,128)(2,1)}, bf16[512,5376]{1,0:T(8,128)(2,1)}, u32[]{:S(2)}, u32[]{:S(2)}) collective-permute-start(bf16[512,5376]{1,0:T(8,128)(2,1)} %bitcast.47), channel_id=1, source_target_pairs={{0,4},{1,5},{2,6},{3,7},{4,0},{5,1},{6,2},{7,3}} | collective-permute-start | bytes 16515080 | tf_op jit(solution)/shard_map/ppermute | solution.py:760
  35.5 278.0 %collective-permute-start.1 = (bf16[512,5376]{1,0:T(8,128)(2,1)}, bf16[512,5376]{1,0:T(8,128)(2,1)}, u32[]{:S(2)}, u32[]{:S(2)}) collective-permute-start(bf16[512,5376]{1,0:T(8,128)(2,1)} %bitcast.48), channel_id=1, source_target_pairs={{0,2},{1,3},{2,0},{3,1},{4,6},{5,7},{6,4},{7,5}} | collective-permute-start | bytes 16515080 | tf_op jit(solution)/shard_map/ppermute | solution.py:760
  37.0 475.4 %collective-permute-start = (bf16[512,5376]{1,0:T(8,128)(2,1)}, bf16[512,5376]{1,0:T(8,128)(2,1)}, u32[]{:S(2)}, u32[]{:S(2)}) collective-permute-start(bf16[512,5376]{1,0:T(8,128)(2,1)} %bitcast.49), channel_id=1, source_target_pairs={{0,1},{1,0},{2,3},{3,2},{4,5},{5,4},{6,7},{7,6}} | collective-permute-start | bytes 16515080 | tf_op jit(solution)/shard_map/ppermute | solution.py:760
  313.2 115.1 %collective-permute-start.6 = (bf16[256,5376]{1,0:T(8,128)(2,1)S(1)}, bf16[256,5376]{1,0:T(8,128)(2,1)}, u32[]{:S(2)}, u32[]{:S(2)}) collective-permute-start(bf16[256,5376]{1,0:T(8,128)(2,1)S(1)} %slice.47), channel_id=1, source_target_pairs={{0,2},{1,3},{2,0},{3,1},{4,6},{5,7},{6,4},{7,5}} | collective-permute-start | bytes 8257544 | tf_op jit(solution)/shard_map/ppermute | solution.py:760
  355.9 156.5 %collective-permute-start.4 = (bf16[512,5376]{1,0:T(8,128)(2,1)}, bf16[512,5376]{1,0:T(8,128)(2,1)}, u32[]{:S(2)}, u32[]{:S(2)}) collective-permute-start(bf16[512,5376]{1,0:T(8,128)(2,1)} %collective-permute-done.2.refs_3_), channel_id=1, source_target_pairs={{0,1},{1,0},{2,3},{3,2},{4,5},{5,4},{6,7},{7,6}} | collective-permute-start | bytes 16515080 | tf_op jit(solution)/shard_map/ppermute | solution.py:760
  355.9 156.6 %collective-permute-start.3 = (bf16[512,5376]{1,0:T(8,128)(2,1)}, bf16[512,5376]{1,0:T(8,128)(2,1)}, u32[]{:S(2)}, u32[]{:S(2)}) collective-permute-start(bf16[512,5376]{1,0:T(8,128)(2,1)} %collective-permute-done.1.refs_2_), channel_id=1, source_target_pairs={{0,1},{1,0},{2,3},{3,2},{4,5},{5,4},{6,7},{7,6}} | collective-permute-start | bytes 16515080 | tf_op jit(solution)/shard_map/ppermute | solution.py:760
  511.2 404.1 %all-gather.17.cloned.1.call-start = ((), (), s32[]{:S(2)}) async-start(), calls=%async_computation.8 | async-start | bytes 37158912 | tf_op jit(solution)/shard_map/all_gather | solution.py:794
  804.9 262.2 %all-gather.13.cloned.1.call-start = ((), (), s32[]{:S(2)}) async-start(), calls=%async_computation.6 | async-start | bytes 37158912 | tf_op jit(solution)/shard_map/all_gather | solution.py:794
  914.7 307.6 %all-gather.15.cloned.1.call-start = ((), (), s32[]{:S(2)}) async-start(), calls=%async_computation.7 | async-start | bytes 37158912 | tf_op jit(solution)/shard_map/all_gather | solution.py:794
  1018.3 349.1 %collective-permute-start.19 = (bf16[4,384,5376]{2,1,0:T(8,128)(2,1)}, bf16[4,384,5376]{2,1,0:T(8,128)(2,1)}, u32[]{:S(2)}, u32[]{:S(2)}) collective-permute-start(bf16[4,384,5376]{2,1,0:T(8,128)(2,1)} %grad_normed_pair.5), channel_id=1, source_target_pairs={{0,1},{1,0},{2,3},{3,2},{4,5},{5,4},{6,7},{7,6}} | collective-permute-start | bytes 49545224 | tf_op jit(solution)/shard_map/ppermute | solution.py:760
  1179.7 262.7 %collective-permute-start.9 = (bf16[4,384,5376]{2,1,0:T(8,128)(2,1)}, bf16[4,384,5376]{2,1,0:T(8,128)(2,1)}, u32[]{:S(2)}, u32[]{:S(2)}) collective-permute-start(bf16[4,384,5376]{2,1,0:T(8,128)(2,1)} %grad_normed_pair.3), channel_id=1, source_target_pairs={{0,1},{1,0},{2,3},{3,2},{4,5},{5,4},{6,7},{7,6}} | collective-permute-start | bytes 49545224 | tf_op jit(solution)/shard_map/ppermute | solution.py:760
  1322.6 149.3 %collective-permute-start.14 = (bf16[4,384,5376]{2,1,0:T(8,128)(2,1)}, bf16[4,384,5376]{2,1,0:T(8,128)(2,1)}, u32[]{:S(2)}, u32[]{:S(2)}) collective-permute-start(bf16[4,384,5376]{2,1,0:T(8,128)(2,1)} %grad_normed_pair.4), channel_id=1, source_target_pairs={{0,1},{1,0},{2,3},{3,2},{4,5},{5,4},{6,7},{7,6}} | collective-permute-start | bytes 49545224 | tf_op jit(solution)/shard_map/ppermute | solution.py:760
  1469.9 119.4 %collective-permute-start.10 = (bf16[2,384,2688]{2,1,0:T(8,128)(2,1)}, bf16[2,384,2688]{2,1,0:T(8,128)(2,1)S(1)}, u32[]{:S(2)}, u32[]{:S(2)}) collective-permute-start(bf16[2,384,2688]{2,1,0:T(8,128)(2,1)} %get-tuple-element.81), channel_id=1, source_target_pairs={{0,2},{1,3},{2,0},{3,1},{4,6},{5,7},{6,4},{7,5}} | collective-permute-start | bytes 12386312 | tf_op jit(solution)/shard_map/ppermute | solution.py:760
  1470.3 119.6 %collective-permute-start.11 = (bf16[2,384,2688]{2,1,0:T(8,128)(2,1)}, bf16[2,384,2688]{2,1,0:T(8,128)(2,1)}, u32[]{:S(2)}, u32[]{:S(2)}) collective-permute-start(bf16[2,384,2688]{2,1,0:T(8,128)(2,1)} %get-tuple-element.83), channel_id=1, source_target_pairs={{0,4},{1,5},{2,6},{3,7},{4,0},{5,1},{6,2},{7,3}} | collective-permute-start | bytes 12386312 | tf_op jit(solution)/shard_map/ppermute | solution.py:760
  1499.5 164.7 %collective-permute-start.15 = (bf16[2,384,2688]{2,1,0:T(8,128)(2,1)}, bf16[2,384,2688]{2,1,0:T(8,128)(2,1)}, u32[]{:S(2)}, u32[]{:S(2)}) collective-permute-start(bf16[2,384,2688]{2,1,0:T(8,128)(2,1)} %get-tuple-element.89), channel_id=1, source_target_pairs={{0,2},{1,3},{2,0},{3,1},{4,6},{5,7},{6,4},{7,5}} | collective-permute-start | bytes 12386312 | tf_op jit(solution)/shard_map/ppermute | solution.py:760
  1500.9 164.7 %collective-permute-start.16 = (bf16[2,384,2688]{2,1,0:T(8,128)(2,1)}, bf16[2,384,2688]{2,1,0:T(8,128)(2,1)}, u32[]{:S(2)}, u32[]{:S(2)}) collective-permute-start(bf16[2,384,2688]{2,1,0:T(8,128)(2,1)} %get-tuple-element.91), channel_id=1, source_target_pairs={{0,4},{1,5},{2,6},{3,7},{4,0},{5,1},{6,2},{7,3}} | collective-permute-start | bytes 12386312 | tf_op jit(solution)/shard_map/ppermute | solution.py:760
  1507.3 202.5 %collective-permute-start.22 = (bf16[384,2688]{1,0:T(8,128)(2,1)}, bf16[384,2688]{1,0:T(8,128)(2,1)}, u32[]{:S(2)}, u32[]{:S(2)}) collective-permute-start(bf16[384,2688]{1,0:T(8,128)(2,1)} %get-tuple-element.100), channel_id=1, source_target_pairs={{0,4},{1,5},{2,6},{3,7},{4,0},{5,1},{6,2},{7,3}} | collective-permute-start | bytes 6193160 | tf_op jit(solution)/shard_map/ppermute | solution.py:760
  1589.3 172.7 %collective-permute-start.23 = (bf16[384,2688]{1,0:T(8,128)(2,1)}, bf16[384,2688]{1,0:T(8,128)(2,1)}, u32[]{:S(2)}, u32[]{:S(2)}) collective-permute-start(bf16[384,2688]{1,0:T(8,128)(2,1)} %get-tuple-element.101), channel_id=1, source_target_pairs={{0,2},{1,3},{2,0},{3,1},{4,6},{5,7},{6,4},{7,5}} | collective-permute-start | bytes 6193160 | tf_op jit(solution)/shard_map/ppermute | solution.py:760
  1597.0 215.7 %collective-permute-start.12 = (bf16[384,2688]{1,0:T(8,128)(2,1)}, bf16[384,2688]{1,0:T(8,128)(2,1)S(1)}, u32[]{:S(2)}, u32[]{:S(2)}) collective-permute-start(bf16[384,2688]{1,0:T(8,128)(2,1)} %get-tuple-element.84), channel_id=1, source_target_pairs={{0,4},{1,5},{2,6},{3,7},{4,0},{5,1},{6,2},{7,3}} | collective-permute-start | bytes 6193160 | tf_op jit(solution)/shard_map/ppermute | solution.py:760
  1664.2 148.6 %collective-permute-start.13 = (bf16[384,2688]{1,0:T(8,128)(2,1)}, bf16[384,2688]{1,0:T(8,128)(2,1)S(1)}, u32[]{:S(2)}, u32[]{:S(2)}) collective-permute-start(bf16[384,2688]{1,0:T(8,128)(2,1)} %get-tuple-element.85), channel_id=1, source_target_pairs={{0,2},{1,3},{2,0},{3,1},{4,6},{5,7},{6,4},{7,5}} | collective-permute-start | bytes 6193160 | tf_op jit(solution)/shard_map/ppermute | solution.py:760
  1671.4 125.8 %collective-permute-start.17 = (bf16[384,2688]{1,0:T(8,128)(2,1)}, bf16[384,2688]{1,0:T(8,128)(2,1)S(1)}, u32[]{:S(2)}, u32[]{:S(2)}) collective-permute-start(bf16[384,2688]{1,0:T(8,128)(2,1)} %get-tuple-element.92), channel_id=1, source_target_pairs={{0,4},{1,5},{2,6},{3,7},{4,0},{5,1},{6,2},{7,3}} | collective-permute-start | bytes 6193160 | tf_op jit(solution)/shard_map/ppermute | solution.py:760
  (46 other events, 1711.6 us)
Sparse Core Ops, SparseCore 0:
  16.4 269.1 all-gather.10
  287.4 207.1 all-gather.8
  497.0 186.5 all-gather.6
  685.8 220.3 all-gather.16
  914.8 152.2 all-gather.12
  1069.4 152.8 all-gather.14

commit v5 on v4

--- a/solution.py
+++ b/solution.py
@@ -731,7 +731,7 @@
 
 SEQ_ORDER = (1, 2, 0)
 GW_ORDER = (1, 0, 2)
-GWO_ORDER = (1, 0, 2)
+GWO_ORDER = (1, 2, 0)
 
 
 def solution(mesh):
@@ -751,15 +751,19 @@
 
         gain_pre_row, gain_post_row = gain_pre[None, :], gain_post[None, :]
         rows = x_in.shape[1]
+        normed = {SEQ_ORDER[0]: pre_norm(x_in, gain_pre_row, SEQ_ORDER[0], 1)}
+        normed[SEQ_ORDER[0]], positions = lax.optimization_barrier((normed[SEQ_ORDER[0]], positions))
+        pos_all = lax.all_gather(positions, 'tp', axis=1, tiled=True)
+        w_out_loc, pos_all = lax.optimization_barrier((w_out.reshape(q_cols, depth), pos_all))
         gathered = {}
         for b in SEQ_ORDER:
-            normed = pre_norm(x_in, gain_pre_row, b, 1)
-            gathered[b] = (lax.all_gather(normed, 'tp', axis=0, tiled=True).reshape(n_dev, rows, depth), 0)
+            if b not in normed:
+                normed[b] = pre_norm(x_in, gain_pre_row, b, 1)
+            gathered[b] = (lax.all_gather(normed[b], 'tp', axis=0, tiled=True).reshape(n_dev, rows, depth), 0)
 
         def swap(value, bit):
             return lax.ppermute(value, 'tp', [(d, d ^ bit) for d in range(n_dev)])
 
-        w_out_loc = w_out.reshape(q_cols, depth)
         mid = q_cols // 2
         near_w = {bit: swap(w_out_loc, bit) for bit in (1, 2, 4)}
         far_w = (swap(near_w[2][:mid], 4), swap(near_w[4][mid:], 2))
@@ -767,7 +771,6 @@
         far_other = [swap(part, 1) for part in far_w]
         w_out_pieces = (w_out_loc, near_w[1], near_w[2], near_w[4], *other_core, *far_w, *far_other)
 
-        pos_all = lax.all_gather(positions, 'tp', axis=1, tiled=True)
         seq_len = pos_all.shape[1]
         half = head_dim // 2
         inv_freq = ROPE_THETA ** (-2.0 * jnp.arange(half, dtype=jnp.float32) / head_dim)

time: 1860 us -> 1800 us (0.968)
  blocking collectives: 238 us -> 146 us
  waiting for transfers between devices: 398 us -> 438 us
    all_gather x1, blocking collectives: 238 us -> 14.7 us  [local_body(): pos_all = lax.all_gather(positions, 'tp', axis=1, tiled=True)]
    ppermute x24, waiting for transfers between devices: 199 us -> 370 us  [swap(): return lax.ppermute(value, 'tp', [(d, d ^ bit) for d in range(n_dev)])]
    all_to_all x0 -> x2, blocking collectives: none -> 131 us  [local_body(): lax.all_to_all(o_b.reshape(n_dev, rows, q_cols), 'tp', split_axis=0, conc...]
    all_gather x3, waiting for transfers between devices: 91.2 us -> 23.4 us  [local_body(): d_proj_all[b] = lax.all_gather(d_proj, 'tp', axis=0, tiled=True)]
    all_to_all x3 -> x1, waiting for transfers between devices: 107 us -> 44.9 us  [local_body(): lax.all_to_all(o_b.reshape(n_dev, rows, q_cols), 'tp', split_axis=0, conc...]
  transfers between devices with their start and end apart: 33 -> 31, of which waited for: 9 -> 8; matrix products, arithmetic and copies ran while one was open for 9% -> 9% of each run, Pallas kernels for 51% -> 53%
where the time goes in v5:
time: 1800 us; the launch traced here: 1790 us
  Pallas kernels  982 us (55%)
  waiting for transfers between devices  438 us (24%)
  blocking collectives  146 us (8%)
  matrix products  73.4 us (4%)
  local copies, waits for them, and re-layouts  70.2 us (4%)
  other arithmetic  44.8 us (2%)
  starting transfers between devices  19.8 us (1%)
    ppermute x24, waiting for transfers between devices, swap(): return lax.ppermute(value, 'tp', [(d, d ^ bit) for d in range(n_dev)])  370 us
    pallas_call x3, Pallas kernels, attn_bwd(): pl.pallas_call(functools.partial(attn_bwd_kernel, groups, head_dim, head_...  159 us
    pallas_call x3, Pallas kernels, grad_w(): pl.pallas_call(functools.partial(grad_w_kernel, has_prev, last, head_dim)...  147 us
    pallas_call x3, Pallas kernels, qkv_project(): pl.pallas_call(functools.partial(qkv_kernel, q_cols, k_cols, head_dim, he...  134 us
    all_to_all x2, blocking collectives, local_body(): lax.all_to_all(o_b.reshape(n_dev, rows, q_cols), 'tp', split_axis=0, conc...  131 us
    pallas_call x3, Pallas kernels, attn_fwd(): pl.pallas_call(functools.partial(attn_fwd_kernel, groups, head_dim), grid...  104 us
    pallas_call x3, Pallas kernels, grad_normed_own(): pl.pallas_call(own_core_kernel, grid_spec=pltpu.PrefetchScalarGridSpec(nu...  82.3 us
    pallas_call x3, Pallas kernels, grad_normed_pair(): pl.pallas_call(pair_core_kernel, grid_spec=pltpu.PrefetchScalarGridSpec(n...  78.5 us
  transfers between devices with their start and end apart: 31, of which 8 were waited for; matrix products, arithmetic and copies ran while one was open for 9% of the time, Pallas kernels for 53%

profile of v5, /device:TPU:0, one launch (start us, length us, event | category | flops | bytes accessed | tf_op | source)
XLA Modules:
  0.0 1788.4 jit_solution(15569049610362529656)
XLA Ops:
  85.3 195.3 %collective-permute-done.2.refs_3_ = bf16[512,5376]{1,0:T(8,128)(2,1)} collective-permute-done((bf16[512,5376]{1,0:T(8,128)(2,1)}, bf16[512,5376]{1,0:T(8,128)(2,1)}, u32[]{:S(2)}, u32[]{:S(2)}) %collective-permute-start.2) | collective-permute-done | bytes 5505056 | tf_op jit(solution)/shard_map/ppermute | solution.py:765
  326.6 59.4 %collective-permute-done.6.refs_7_ = bf16[256,5376]{1,0:T(8,128)(2,1)} collective-permute-done((bf16[256,5376]{1,0:T(8,128)(2,1)S(1)}, bf16[256,5376]{1,0:T(8,128)(2,1)}, u32[]{:S(2)}, u32[]{:S(2)}) %collective-permute-start.6) | collective-permute-done | bytes 2752544 | tf_op jit(solution)/shard_map/ppermute | solution.py:765
  391.3 46.0 %qkv_project.5 = (bf16[3072,512]{1,0:T(8,128)(2,1)}, bf16[3072,256]{1,0:T(8,128)(2,1)}, bf16[3072,256]{1,0:T(8,128)(2,1)}) custom-call(bf16[8,384,5376]{2,1,0:T(8,128)(2,1)} %bitcast.43, bf16[5376,1024]{1,0:T(8,128)(2,1)} %copy.33.w_ref, f32[3072,128]{1,0:T(8,128)} %get-tuple-element.149.cos_ref, f32[3072,128]{1,0:T(8,128)} %get-tuple-element.150.sin_ref), custom_call_target="tpu_custom_call" | custom-call | flops 33822867456 | bytes 50331648 | tf_op jit(solution)/shard_map/qkv_project/pallas_call | solution.py:477
  441.1 32.5 %attn_fwd.5 = (bf16[3072,512]{1,0:T(8,128)(2,1)}, f32[2,12,1,512]{3,2,1,0:T(1,128)S(1)}) custom-call(s32[12]{0:T(128)S(1)} %get-tuple-element.136.first_ref, bf16[3072,512]{1,0:T(8,128)(2,1)} %get-tuple-element.77.q_ref, bf16[3072,256]{1,0:T(8,128)(2,1)S(1)} %copy-done.13, bf16[3072,256]{1,0:T(8,128)(2,1)S(1)} %copy-done.15, ...), custom_call_target="tpu_custom_call" | custom-call | flops 9663676416 | bytes 12582912 | tf_op jit(solution)/shard_map/attn_fwd/pallas_call | solution.py:565
  477.2 44.9 %all-to-all-done.2.o_ref = bf16[8,384,512]{2,1,0:T(8,128)(2,1)S(1)} async-done(((bf16[8,384,512]{2,1,0:T(8,128)(2,1)}), bf16[8,384,512]{2,1,0:T(8,128)(2,1)S(1)}, u32[]{:S(2)}, u32[]{:S(2)}) %all-to-all-start.2) | async-done | bytes 3145760 | tf_op jit(solution)/shard_map/all_to_all | solution.py:794
  565.4 44.7 %qkv_project.4 = (bf16[3072,512]{1,0:T(8,128)(2,1)}, bf16[3072,256]{1,0:T(8,128)(2,1)}, bf16[3072,256]{1,0:T(8,128)(2,1)}) custom-call(bf16[8,384,5376]{2,1,0:T(8,128)(2,1)} %bitcast.41, bf16[5376,1024]{1,0:T(8,128)(2,1)} %copy.33.w_ref, f32[3072,128]{1,0:T(8,128)} %get-tuple-element.147.cos_ref, f32[3072,128]{1,0:T(8,128)} %get-tuple-element.148.sin_ref), custom_call_target="tpu_custom_call" | custom-call | flops 33822867456 | bytes 50331648 | tf_op jit(solution)/shard_map/qkv_project/pallas_call | solution.py:477
  613.9 32.6 %attn_fwd.4 = (bf16[3072,512]{1,0:T(8,128)(2,1)}, f32[2,12,1,512]{3,2,1,0:T(1,128)S(1)}) custom-call(s32[12]{0:T(128)S(1)} %get-tuple-element.137.first_ref, bf16[3072,512]{1,0:T(8,128)(2,1)} %get-tuple-element.72.q_ref, bf16[3072,256]{1,0:T(8,128)(2,1)S(1)} %copy-done.17, bf16[3072,256]{1,0:T(8,128)(2,1)S(1)} %copy-done.19, ...), custom_call_target="tpu_custom_call" | custom-call | flops 9663676416 | bytes 12582912 | tf_op jit(solution)/shard_map/attn_fwd/pallas_call | solution.py:565
  646.5 57.4 %all_to_all.15.o_ref = bf16[8,384,512]{2,1,0:T(8,128)(2,1)S(1)} all-to-all(bf16[8,384,512]{2,1,0:T(8,128)(2,1)} %bitcast.39), channel_id=1, replica_groups=mesh['dp'=1,'tp'=8] {'tp'}, dimensions={0} | all-to-all | bytes 6291456 | tf_op jit(solution)/shard_map/all_to_all | solution.py:794
  746.5 43.0 %qkv_project.3 = (bf16[3072,512]{1,0:T(8,128)(2,1)}, bf16[3072,256]{1,0:T(8,128)(2,1)}, bf16[3072,256]{1,0:T(8,128)(2,1)}) custom-call(bf16[8,384,5376]{2,1,0:T(8,128)(2,1)} %bitcast.45, bf16[5376,1024]{1,0:T(8,128)(2,1)} %copy.33.w_ref, f32[3072,128]{1,0:T(8,128)} %get-tuple-element.145.cos_ref, f32[3072,128]{1,0:T(8,128)} %get-tuple-element.146.sin_ref), custom_call_target="tpu_custom_call" | custom-call | flops 33822867456 | bytes 50331648 | tf_op jit(solution)/shard_map/qkv_project/pallas_call | solution.py:477
  793.4 39.5 %attn_fwd.3 = (bf16[3072,512]{1,0:T(8,128)(2,1)}, f32[2,12,1,512]{3,2,1,0:T(1,128)S(1)}) custom-call(s32[12]{0:T(128)S(1)} %get-tuple-element.138.first_ref, bf16[3072,512]{1,0:T(8,128)(2,1)} %get-tuple-element.67.q_ref, bf16[3072,256]{1,0:T(8,128)(2,1)S(1)} %copy-done.21, bf16[3072,256]{1,0:T(8,128)(2,1)S(1)} %copy-done.23, s32[1,3072]{1,0:T(1,128)S(1)} %copy-done.7, ...), custom_call_target="tpu_custom_call" | custom-call | flops 9663676416 | bytes 12582912 | tf_op jit(solution)/shard_map/attn_fwd/pallas_call | solution.py:565
  832.8 73.8 %all_to_all.16.o_ref = bf16[8,384,512]{2,1,0:T(8,128)(2,1)S(1)} all-to-all(bf16[8,384,512]{2,1,0:T(8,128)(2,1)} %bitcast.40), channel_id=1, replica_groups=mesh['dp'=1,'tp'=8] {'tp'}, dimensions={0} | all-to-all | bytes 6291456 | tf_op jit(solution)/shard_map/all_to_all | solution.py:794
  906.6 26.5 %out_proj.3.proj_ref = bf16[384,5376]{1,0:T(8,128)(2,1)} custom-call(s32[1]{0:T(128)} %bitcast.me_ref.dst_ref, bf16[8,384,512]{2,1,0:T(8,128)(2,1)S(1)} %all_to_all.16.o_ref, bf16[512,5376]{1,0:T(8,128)(2,1)} %bitcast.52, bf16[512,5376]{1,0:T(8,128)(2,1)} %collective-permute-done.refs_1_, bf16[512,5376]{1,0:T(8,128)(2,1)} %collective-permute-done.1.refs_2_, ...), custom_call_target="tpu_custom_call" | custom-call | flops 16911433728 | bytes 44040192 | tf_op jit(solution)/shard_map/out_proj/pallas_call | solution.py:181
  970.5 49.8 %attn_bwd.5.d0_ref.d1_ref.d_ref = bf16[3072,1024]{1,0:T(8,128)(2,1)} custom-call(s32[12]{0:T(128)S(1)} %copy-done.12, bf16[3072,512]{1,0:T(8,128)(2,1)} %get-tuple-element.77.q_ref, bf16[3072,256]{1,0:T(8,128)(2,1)S(1)} %copy-done.14, bf16[3072,256]{1,0:T(8,128)(2,1)S(1)} %copy-done.16, bf16[3072,512]{1,0:T(8,128)(2,1)} %get-tuple-element.80.o_ref, ...), custom_call_target="tpu_custom_call" | custom-call | flops 24159191040 | bytes 25165824 | tf_op jit(solution)/shard_map/attn_bwd/pallas_call | solution.py:700
  1020.3 27.1 %grad_normed_pair.5 = bf16[4,384,5376]{2,1,0:T(8,128)(2,1)} custom-call(s32[1]{0:T(128)S(6)} %xor.2.dst_ref, bf16[3072,1024]{1,0:T(8,128)(2,1)} %attn_bwd.5.d0_ref.d1_ref.d_ref, bf16[3072,1024]{1,0:T(8,128)(2,1)} %attn_bwd.5.d0_ref.d1_ref.d_ref, bf16[1024,5376]{1,0:T(8,128)(2,1)} %get-tuple-element.122.w_ref), custom_call_target="tpu_custom_call" | custom-call | flops 16911433728 | bytes 27525120 | tf_op jit(solution)/shard_map/grad_normed_pair/pallas_call | solution.py:227
  1072.1 49.8 %attn_bwd.4.d0_ref.d1_ref.d_ref = bf16[3072,1024]{1,0:T(8,128)(2,1)} custom-call(s32[12]{0:T(128)S(1)} %get-tuple-element.137.first_ref, bf16[3072,512]{1,0:T(8,128)(2,1)} %get-tuple-element.72.q_ref, bf16[3072,256]{1,0:T(8,128)(2,1)S(1)} %copy-done.18, bf16[3072,256]{1,0:T(8,128)(2,1)S(1)} %copy-done.20, bf16[3072,512]{1,0:T(8,128)(2,1)} %get-tuple-element.75.o_ref, ...), custom_call_target="tpu_custom_call" | custom-call | flops 24159191040 | bytes 25165824 | tf_op jit(solution)/shard_map/attn_bwd/pallas_call | solution.py:700
  1195.6 59.3 %attn_bwd.3.d0_ref.d1_ref.d_ref = bf16[3072,1024]{1,0:T(8,128)(2,1)} custom-call(s32[12]{0:T(128)S(1)} %get-tuple-element.138.first_ref, bf16[3072,512]{1,0:T(8,128)(2,1)} %get-tuple-element.67.q_ref, bf16[3072,256]{1,0:T(8,128)(2,1)S(1)} %copy-done.22, bf16[3072,256]{1,0:T(8,128)(2,1)S(1)} %copy-done.24, bf16[3072,512]{1,0:T(8,128)(2,1)} %get-tuple-element.70.o_ref, ...), custom_call_target="tpu_custom_call" | custom-call | flops 24159191040 | bytes 25165824 | tf_op jit(solution)/shard_map/attn_bwd/pallas_call | solution.py:700
  1280.6 44.7 %grad_w.3.refs_0_ = f32[5376,1024]{1,0:T(8,128)} custom-call(bf16[8,384,5376]{2,1,0:T(8,128)(2,1)} %bitcast.44, bf16[3072,1024]{1,0:T(8,128)(2,1)} %attn_bwd.5.d0_ref.d1_ref.d_ref), custom_call_target="tpu_custom_call" | custom-call | flops 33822867456 | bytes 83361792 | tf_op jit(solution)/shard_map/grad_w/pallas_call | solution.py:412
  1325.3 27.5 %grad_normed_own.5 = (bf16[2,384,2688]{2,1,0:T(8,128)(2,1)}, bf16[2,384,2688]{2,1,0:T(8,128)(2,1)}, bf16[2,384,2688]{2,1,0:T(8,128)(2,1)}, bf16[2,384,2688]{2,1,0:T(8,128)(2,1)}) custom-call(s32[1]{0:T(128)} %bitcast.me_ref.dst_ref, bf16[3072,1024]{1,0:T(8,128)(2,1)} %attn_bwd.5.d0_ref.d1_ref.d_ref, bf16[3072,1024]{1,0:T(8,128)(2,1)} %attn_bwd.5.d0_ref.d1_ref.d_ref, ...), custom_call_target="tpu_custom_call" | custom-call | flops 16911433728 | bytes 44040192 | tf_op jit(solution)/shard_map/grad_normed_own/pallas_call | solution.py:285
  1354.8 45.4 %grad_w.4.refs_0_ = f32[5376,1024]{1,0:T(8,128)} custom-call(bf16[8,384,5376]{2,1,0:T(8,128)(2,1)} %bitcast.46, bf16[3072,1024]{1,0:T(8,128)(2,1)} %attn_bwd.3.d0_ref.d1_ref.d_ref, f32[5376,1024]{1,0:T(8,128)} %grad_w.3.refs_0_), custom_call_target="tpu_custom_call", output_to_operand_aliasing={{}: (2, {})} | custom-call | flops 33822867456 | bytes 83361792 | tf_op jit(solution)/shard_map/grad_w/pallas_call | solution.py:412
  1400.2 27.5 %grad_normed_own.4 = (bf16[2,384,2688]{2,1,0:T(8,128)(2,1)}, bf16[2,384,2688]{2,1,0:T(8,128)(2,1)}, bf16[2,384,2688]{2,1,0:T(8,128)(2,1)}, bf16[2,384,2688]{2,1,0:T(8,128)(2,1)}) custom-call(s32[1]{0:T(128)} %bitcast.me_ref.dst_ref, bf16[3072,1024]{1,0:T(8,128)(2,1)} %attn_bwd.4.d0_ref.d1_ref.d_ref, bf16[3072,1024]{1,0:T(8,128)(2,1)} %attn_bwd.4.d0_ref.d1_ref.d_ref, ...), custom_call_target="tpu_custom_call" | custom-call | flops 16911433728 | bytes 44040192 | tf_op jit(solution)/shard_map/grad_normed_own/pallas_call | solution.py:285
  1430.0 27.3 %grad_normed_own.3 = (bf16[2,384,2688]{2,1,0:T(8,128)(2,1)}, bf16[2,384,2688]{2,1,0:T(8,128)(2,1)}, bf16[2,384,2688]{2,1,0:T(8,128)(2,1)}, bf16[2,384,2688]{2,1,0:T(8,128)(2,1)}) custom-call(s32[1]{0:T(128)} %bitcast.me_ref.dst_ref, bf16[3072,1024]{1,0:T(8,128)(2,1)} %attn_bwd.3.d0_ref.d1_ref.d_ref, bf16[3072,1024]{1,0:T(8,128)(2,1)} %attn_bwd.3.d0_ref.d1_ref.d_ref, ...), custom_call_target="tpu_custom_call" | custom-call | flops 16911433728 | bytes 44040192 | tf_op jit(solution)/shard_map/grad_normed_own/pallas_call | solution.py:285
  1466.9 56.4 %grad_w.5 = (f32[5376,4,128]{2,1,0:T(4,128)}, f32[5376,2,128]{2,1,0:T(2,128)}, f32[5376,2,128]{2,1,0:T(2,128)}) custom-call(bf16[8,384,5376]{2,1,0:T(8,128)(2,1)} %bitcast.42, bf16[3072,1024]{1,0:T(8,128)(2,1)} %attn_bwd.4.d0_ref.d1_ref.d_ref, f32[5376,1024]{1,0:T(8,128)} %grad_w.4.refs_0_), custom_call_target="tpu_custom_call" | custom-call | flops 33822867456 | bytes 83361792 | tf_op jit(solution)/shard_map/grad_w/pallas_call | solution.py:412
  1555.3 66.8 %collective-permute-done.10.near_x_ref.refs_1_ = bf16[2,384,2688]{2,1,0:T(8,128)(2,1)} collective-permute-done((bf16[2,384,2688]{2,1,0:T(8,128)(2,1)}, bf16[2,384,2688]{2,1,0:T(8,128)(2,1)}, u32[]{:S(2)}, u32[]{:S(2)}) %collective-permute-start.10) | collective-permute-done | bytes 4128800 | tf_op jit(solution)/shard_map/ppermute | solution.py:765
  1629.9 37.8 %collective-permute-done.22.refs_2_ = bf16[384,2688]{1,0:T(8,128)(2,1)S(1)} collective-permute-done((bf16[384,2688]{1,0:T(8,128)(2,1)}, bf16[384,2688]{1,0:T(8,128)(2,1)S(1)}, u32[]{:S(2)}, u32[]{:S(2)}) %collective-permute-start.22) | collective-permute-done | bytes 2064416 | tf_op jit(solution)/shard_map/ppermute | solution.py:765
  (190 shorter events, 558.7 us)
Async XLA Ops:
  7.2 384.1 %all-gather.11.cloned.1.call-start = ((), (), s32[]{:S(2)}) async-start(), calls=%async_computation.5 | async-start | bytes 37158912 | tf_op jit(solution)/shard_map/all_gather | solution.py:762
  16.2 549.1 %all-gather.9.cloned.1.call-start = ((), (), s32[]{:S(2)}) async-start(), calls=%async_computation.4 | async-start | bytes 37158912 | tf_op jit(solution)/shard_map/all_gather | solution.py:762
  23.9 722.5 %all-gather.7.cloned.1.call-start = ((), (), s32[]{:S(2)}) async-start(), calls=%async_computation.3 | async-start | bytes 37158912 | tf_op jit(solution)/shard_map/all_gather | solution.py:762
  47.4 233.2 %collective-permute-start.2 = (bf16[512,5376]{1,0:T(8,128)(2,1)}, bf16[512,5376]{1,0:T(8,128)(2,1)}, u32[]{:S(2)}, u32[]{:S(2)}) collective-permute-start(bf16[512,5376]{1,0:T(8,128)(2,1)} %bitcast.47), channel_id=1, source_target_pairs={{0,4},{1,5},{2,6},{3,7},{4,0},{5,1},{6,2},{7,3}} | collective-permute-start | bytes 16515080 | tf_op jit(solution)/shard_map/ppermute | solution.py:765
  47.9 235.9 %collective-permute-start.1 = (bf16[512,5376]{1,0:T(8,128)(2,1)}, bf16[512,5376]{1,0:T(8,128)(2,1)}, u32[]{:S(2)}, u32[]{:S(2)}) collective-permute-start(bf16[512,5376]{1,0:T(8,128)(2,1)} %bitcast.48), channel_id=1, source_target_pairs={{0,2},{1,3},{2,0},{3,1},{4,6},{5,7},{6,4},{7,5}} | collective-permute-start | bytes 16515080 | tf_op jit(solution)/shard_map/ppermute | solution.py:765
  49.4 427.7 %collective-permute-start = (bf16[512,5376]{1,0:T(8,128)(2,1)}, bf16[512,5376]{1,0:T(8,128)(2,1)}, u32[]{:S(2)}, u32[]{:S(2)}) collective-permute-start(bf16[512,5376]{1,0:T(8,128)(2,1)} %bitcast.49), channel_id=1, source_target_pairs={{0,1},{1,0},{2,3},{3,2},{4,5},{5,4},{6,7},{7,6}} | collective-permute-start | bytes 16515080 | tf_op jit(solution)/shard_map/ppermute | solution.py:765
  326.1 151.1 %collective-permute-start.4 = (bf16[512,5376]{1,0:T(8,128)(2,1)}, bf16[512,5376]{1,0:T(8,128)(2,1)}, u32[]{:S(2)}, u32[]{:S(2)}) collective-permute-start(bf16[512,5376]{1,0:T(8,128)(2,1)} %collective-permute-done.2.refs_3_), channel_id=1, source_target_pairs={{0,1},{1,0},{2,3},{3,2},{4,5},{5,4},{6,7},{7,6}} | collective-permute-start | bytes 16515080 | tf_op jit(solution)/shard_map/ppermute | solution.py:765
  326.1 151.1 %collective-permute-start.3 = (bf16[512,5376]{1,0:T(8,128)(2,1)}, bf16[512,5376]{1,0:T(8,128)(2,1)}, u32[]{:S(2)}, u32[]{:S(2)}) collective-permute-start(bf16[512,5376]{1,0:T(8,128)(2,1)} %collective-permute-done.1.refs_2_), channel_id=1, source_target_pairs={{0,1},{1,0},{2,3},{3,2},{4,5},{5,4},{6,7},{7,6}} | collective-permute-start | bytes 16515080 | tf_op jit(solution)/shard_map/ppermute | solution.py:765
  476.3 469.7 %all-gather.17.cloned.1.call-start = ((), (), s32[]{:S(2)}) async-start(), calls=%async_computation.8 | async-start | bytes 37158912 | tf_op jit(solution)/shard_map/all_gather | solution.py:797
  558.6 488.8 %all-gather.15.cloned.1.call-start = ((), (), s32[]{:S(2)}) async-start(), calls=%async_computation.7 | async-start | bytes 37158912 | tf_op jit(solution)/shard_map/all_gather | solution.py:797
  740.6 430.5 %all-gather.13.cloned.1.call-start = ((), (), s32[]{:S(2)}) async-start(), calls=%async_computation.6 | async-start | bytes 37158912 | tf_op jit(solution)/shard_map/all_gather | solution.py:797
  1047.4 277.9 %collective-permute-start.19 = (bf16[4,384,5376]{2,1,0:T(8,128)(2,1)}, bf16[4,384,5376]{2,1,0:T(8,128)(2,1)}, u32[]{:S(2)}, u32[]{:S(2)}) collective-permute-start(bf16[4,384,5376]{2,1,0:T(8,128)(2,1)} %grad_normed_pair.5), channel_id=1, source_target_pairs={{0,1},{1,0},{2,3},{3,2},{4,5},{5,4},{6,7},{7,6}} | collective-permute-start | bytes 49545224 | tf_op jit(solution)/shard_map/ppermute | solution.py:765
  1147.8 252.5 %collective-permute-start.14 = (bf16[4,384,5376]{2,1,0:T(8,128)(2,1)}, bf16[4,384,5376]{2,1,0:T(8,128)(2,1)}, u32[]{:S(2)}, u32[]{:S(2)}) collective-permute-start(bf16[4,384,5376]{2,1,0:T(8,128)(2,1)} %grad_normed_pair.4), channel_id=1, source_target_pairs={{0,1},{1,0},{2,3},{3,2},{4,5},{5,4},{6,7},{7,6}} | collective-permute-start | bytes 49545224 | tf_op jit(solution)/shard_map/ppermute | solution.py:765
  1280.3 149.7 %collective-permute-start.9 = (bf16[4,384,5376]{2,1,0:T(8,128)(2,1)}, bf16[4,384,5376]{2,1,0:T(8,128)(2,1)}, u32[]{:S(2)}, u32[]{:S(2)}) collective-permute-start(bf16[4,384,5376]{2,1,0:T(8,128)(2,1)} %grad_normed_pair.3), channel_id=1, source_target_pairs={{0,1},{1,0},{2,3},{3,2},{4,5},{5,4},{6,7},{7,6}} | collective-permute-start | bytes 49545224 | tf_op jit(solution)/shard_map/ppermute | solution.py:765
  1352.7 105.9 %collective-permute-start.20 = (bf16[2,384,2688]{2,1,0:T(8,128)(2,1)}, bf16[2,384,2688]{2,1,0:T(8,128)(2,1)S(1)}, u32[]{:S(2)}, u32[]{:S(2)}) collective-permute-start(bf16[2,384,2688]{2,1,0:T(8,128)(2,1)} %get-tuple-element.105), channel_id=1, source_target_pairs={{0,2},{1,3},{2,0},{3,1},{4,6},{5,7},{6,4},{7,5}} | collective-permute-start | bytes 12386312 | tf_op jit(solution)/shard_map/ppermute | solution.py:765
  1427.8 119.5 %collective-permute-start.15 = (bf16[2,384,2688]{2,1,0:T(8,128)(2,1)}, bf16[2,384,2688]{2,1,0:T(8,128)(2,1)}, u32[]{:S(2)}, u32[]{:S(2)}) collective-permute-start(bf16[2,384,2688]{2,1,0:T(8,128)(2,1)} %get-tuple-element.97), channel_id=1, source_target_pairs={{0,2},{1,3},{2,0},{3,1},{4,6},{5,7},{6,4},{7,5}} | collective-permute-start | bytes 12386312 | tf_op jit(solution)/shard_map/ppermute | solution.py:765
  1428.3 119.5 %collective-permute-start.16 = (bf16[2,384,2688]{2,1,0:T(8,128)(2,1)}, bf16[2,384,2688]{2,1,0:T(8,128)(2,1)}, u32[]{:S(2)}, u32[]{:S(2)}) collective-permute-start(bf16[2,384,2688]{2,1,0:T(8,128)(2,1)} %get-tuple-element.99), channel_id=1, source_target_pairs={{0,4},{1,5},{2,6},{3,7},{4,0},{5,1},{6,2},{7,3}} | collective-permute-start | bytes 12386312 | tf_op jit(solution)/shard_map/ppermute | solution.py:765
  1457.4 164.7 %collective-permute-start.10 = (bf16[2,384,2688]{2,1,0:T(8,128)(2,1)}, bf16[2,384,2688]{2,1,0:T(8,128)(2,1)}, u32[]{:S(2)}, u32[]{:S(2)}) collective-permute-start(bf16[2,384,2688]{2,1,0:T(8,128)(2,1)} %get-tuple-element.89), channel_id=1, source_target_pairs={{0,2},{1,3},{2,0},{3,1},{4,6},{5,7},{6,4},{7,5}} | collective-permute-start | bytes 12386312 | tf_op jit(solution)/shard_map/ppermute | solution.py:765
  1458.6 164.9 %collective-permute-start.11 = (bf16[2,384,2688]{2,1,0:T(8,128)(2,1)}, bf16[2,384,2688]{2,1,0:T(8,128)(2,1)}, u32[]{:S(2)}, u32[]{:S(2)}) collective-permute-start(bf16[2,384,2688]{2,1,0:T(8,128)(2,1)} %get-tuple-element.91), channel_id=1, source_target_pairs={{0,4},{1,5},{2,6},{3,7},{4,0},{5,1},{6,2},{7,3}} | collective-permute-start | bytes 12386312 | tf_op jit(solution)/shard_map/ppermute | solution.py:765
  1466.4 201.3 %collective-permute-start.22 = (bf16[384,2688]{1,0:T(8,128)(2,1)}, bf16[384,2688]{1,0:T(8,128)(2,1)S(1)}, u32[]{:S(2)}, u32[]{:S(2)}) collective-permute-start(bf16[384,2688]{1,0:T(8,128)(2,1)} %get-tuple-element.108), channel_id=1, source_target_pairs={{0,4},{1,5},{2,6},{3,7},{4,0},{5,1},{6,2},{7,3}} | collective-permute-start | bytes 6193160 | tf_op jit(solution)/shard_map/ppermute | solution.py:765
  1547.2 172.7 %collective-permute-start.23 = (bf16[384,2688]{1,0:T(8,128)(2,1)}, bf16[384,2688]{1,0:T(8,128)(2,1)S(1)}, u32[]{:S(2)}, u32[]{:S(2)}) collective-permute-start(bf16[384,2688]{1,0:T(8,128)(2,1)} %get-tuple-element.109), channel_id=1, source_target_pairs={{0,2},{1,3},{2,0},{3,1},{4,6},{5,7},{6,4},{7,5}} | collective-permute-start | bytes 6193160 | tf_op jit(solution)/shard_map/ppermute | solution.py:765
  1553.6 181.1 %collective-permute-start.17 = (bf16[384,2688]{1,0:T(8,128)(2,1)}, bf16[384,2688]{1,0:T(8,128)(2,1)S(1)}, u32[]{:S(2)}, u32[]{:S(2)}) collective-permute-start(bf16[384,2688]{1,0:T(8,128)(2,1)} %get-tuple-element.100), channel_id=1, source_target_pairs={{0,4},{1,5},{2,6},{3,7},{4,0},{5,1},{6,2},{7,3}} | collective-permute-start | bytes 6193160 | tf_op jit(solution)/shard_map/ppermute | solution.py:765
  1622.1 112.7 %collective-permute-start.18 = (bf16[384,2688]{1,0:T(8,128)(2,1)}, bf16[384,2688]{1,0:T(8,128)(2,1)S(1)}, u32[]{:S(2)}, u32[]{:S(2)}) collective-permute-start(bf16[384,2688]{1,0:T(8,128)(2,1)} %get-tuple-element.101), channel_id=1, source_target_pairs={{0,2},{1,3},{2,0},{3,1},{4,6},{5,7},{6,4},{7,5}} | collective-permute-start | bytes 6193160 | tf_op jit(solution)/shard_map/ppermute | solution.py:765
  1629.3 125.8 %collective-permute-start.12 = (bf16[384,2688]{1,0:T(8,128)(2,1)}, bf16[384,2688]{1,0:T(8,128)(2,1)S(1)}, u32[]{:S(2)}, u32[]{:S(2)}) collective-permute-start(bf16[384,2688]{1,0:T(8,128)(2,1)} %get-tuple-element.92), channel_id=1, source_target_pairs={{0,4},{1,5},{2,6},{3,7},{4,0},{5,1},{6,2},{7,3}} | collective-permute-start | bytes 6193160 | tf_op jit(solution)/shard_map/ppermute | solution.py:765
  (44 other events, 1485.6 us)
Sparse Core Ops, SparseCore 0:
  16.3 269.1 all-gather.10
  287.4 197.5 all-gather.8
  487.4 167.9 all-gather.6
  657.6 169.2 all-gather.16
  828.5 185.1 all-gather.14
  1016.0 155.0 all-gather.12

commit v6 on v4

--- a/solution.py
+++ b/solution.py
@@ -453,40 +453,93 @@
     )(o_all, d_proj, *([prev] if has_prev else []))
 
 
-def qkv_kernel(q_cols, k_cols, head_dim, q_scale, a_ref, w_ref, cos_ref, sin_ref, q_ref, k_ref, v_ref):
-    n_dev, rows, depth = a_ref.shape
-    lin = jnp.dot(a_ref[...].reshape(n_dev * rows, depth), w_ref[...], preferred_element_type=jnp.float32)
-    cos_t, sin_t = cos_ref[...], sin_ref[...]
-    for h in range((q_cols + k_cols) // head_dim):
-        col = h * head_dim
-        part = lin[:, col:col + head_dim]
-        part = part * cos_t + pltpu.roll(part, head_dim // 2, 1) * sin_t
-        if col < q_cols:
-            q_ref[:, col:col + head_dim] = (part * q_scale).astype(q_ref.dtype)
-        else:
-            k_ref[:, col - q_cols:col - q_cols + head_dim] = part.astype(k_ref.dtype)
-    v_ref[...] = lin[:, q_cols + k_cols:].astype(v_ref.dtype)
-
-
-def qkv_project(gathered, slot, rows, w_all, cos_t, sin_t, q_cols, k_cols, head_dim):
-    n_dev, _, depth = gathered.shape
+def qkv_kernel(q_cols, k_cols, head_dim, q_scale, dev_ref, *refs):
+    pieces, (w_hbm, cos_ref, sin_ref, q_ref, k_ref, v_ref, whole_ref, buf, w_ref, in_sem, out_sem, w_sem) = refs[:-12], refs[-12:]
+    n_slot, rows, _ = buf.shape
+    groups, taken = [], []
+    for piece in pieces:
+        taken.append(piece)
+        if sum(part.shape[0] for part in taken) == rows:
+            groups.append(taken)
+            taken = []
+
+    def start_in(p):
+        slot = p % n_slot
+        for i, group in enumerate(groups):
+            @pl.when(p == i)
+            def _(group=group):
+                row = 0
+                for part in group:
+                    pltpu.make_async_copy(part, buf.at[slot, pl.ds(row, part.shape[0])], in_sem.at[slot]).start()
+                    row += part.shape[0]
+
+    def out_copy(p):
+        slot = p % n_slot
+        return pltpu.make_async_copy(buf.at[slot], whole_ref.at[dev_ref[p]], out_sem.at[slot])
+
+    w_copy = pltpu.make_async_copy(w_hbm, w_ref, w_sem)
+    start_in(0)
+    w_copy.start()
+
+    @pl.loop(0, len(groups))
+    def _(p):
+        slot = p % n_slot
+        pltpu.make_async_copy(pieces[0], buf.at[slot], in_sem.at[slot]).wait()
+        out_copy(p).start()
+
+        @pl.when(p + 1 < len(groups))
+        def _():
+            @pl.when(p + 1 >= n_slot)
+            def _():
+                out_copy(p + 1 - n_slot).wait()
+
+            start_in(p + 1)
+
+        @pl.when(p == 0)
+        def _():
+            w_copy.wait()
+
+        here = pl.ds(pl.multiple_of(dev_ref[p] * rows, rows), rows)
+        lin = jnp.dot(buf[slot], w_ref[...], preferred_element_type=jnp.float32)
+        cos_t, sin_t = cos_ref[here, :], sin_ref[here, :]
+        for h in range((q_cols + k_cols) // head_dim):
+            col = h * head_dim
+            part = lin[:, col:col + head_dim]
+            part = part * cos_t + pltpu.roll(part, head_dim // 2, 1) * sin_t
+            if col < q_cols:
+                q_ref[here, col:col + head_dim] = (part * q_scale).astype(q_ref.dtype)
+            else:
+                k_ref[here, col - q_cols:col - q_cols + head_dim] = part.astype(k_ref.dtype)
+        v_ref[here, :] = lin[:, q_cols + k_cols:].astype(v_ref.dtype)
+
+    for p in range(len(groups) - n_slot, len(groups)):
+        out_copy(p).wait()
+
+
+def qkv_project(devices, pieces, w_all, cos_t, sin_t, q_cols, k_cols, head_dim):
+    rows, depth = pieces[0].shape
     cols = w_all.shape[1]
-    v_cols = cols - q_cols - k_cols
-    seq_len, tile = n_dev * rows, 2 * rows
-    by_row = [pl.BlockSpec((tile, width), lambda i: (i, 0)) for width in (head_dim, head_dim, q_cols, k_cols, v_cols)]
+    seq_len = cos_t.shape[0]
+    n_dev = seq_len // rows
+    widths = (q_cols, k_cols, cols - q_cols - k_cols)
+    hbm, vmem = pl.BlockSpec(memory_space=pl.ANY), pl.BlockSpec(memory_space=pltpu.VMEM)
     return pl.pallas_call(
         functools.partial(qkv_kernel, q_cols, k_cols, head_dim, head_dim ** -0.5),
-        grid=(n_dev // 2,),
-        in_specs=[
-            pl.BlockSpec((2, rows, depth), lambda i: (i, slot, 0)),
-            pl.BlockSpec((depth, cols), lambda i: (0, 0), pipeline_mode=pl.Buffered(1)),
-        ] + by_row[:2],
-        out_specs=by_row[2:],
-        out_shape=[jax.ShapeDtypeStruct((seq_len, width), jnp.bfloat16) for width in (q_cols, k_cols, v_cols)],
-        compiler_params=pltpu.CompilerParams(vmem_limit_bytes=58 * 1024 * 1024),
-        cost_estimate=pl.CostEstimate(flops=2 * seq_len * depth * cols, bytes_accessed=2 * (seq_len * depth + depth * cols + seq_len * cols), transcendentals=0),
+        in_specs=[pl.BlockSpec(memory_space=pltpu.SMEM)] + [hbm] * (len(pieces) + 1) + [vmem] * 2,
+        out_specs=[vmem] * 3 + [hbm],
+        out_shape=[jax.ShapeDtypeStruct((seq_len, width), jnp.bfloat16) for width in widths]
+        + [jax.ShapeDtypeStruct((n_dev, rows, depth), jnp.bfloat16)],
+        scratch_shapes=[
+            pltpu.VMEM((3, rows, depth), jnp.bfloat16),
+            pltpu.VMEM((depth, cols), jnp.bfloat16),
+            pltpu.SemaphoreType.DMA((3,)),
+            pltpu.SemaphoreType.DMA((3,)),
+            pltpu.SemaphoreType.DMA,
+        ],
+        compiler_params=pltpu.CompilerParams(vmem_limit_bytes=56 * 1024 * 1024),
+        cost_estimate=pl.CostEstimate(flops=2 * seq_len * depth * cols, bytes_accessed=2 * (2 * seq_len * depth + depth * cols + seq_len * cols), transcendentals=0),
         name="qkv_project",
-    )(gathered, w_all, cos_t, sin_t)
+    )(devices, *pieces, w_all, cos_t, sin_t)
 
 
 def stack_heads(block, groups, head_dim):
@@ -731,7 +784,7 @@
 
 SEQ_ORDER = (1, 2, 0)
 GW_ORDER = (1, 0, 2)
-GWO_ORDER = (1, 0, 2)
+GWO_ORDER = (2, 1, 0)
 
 
 def solution(mesh):
@@ -751,23 +804,27 @@
 
         gain_pre_row, gain_post_row = gain_pre[None, :], gain_post[None, :]
         rows = x_in.shape[1]
-        gathered = {}
-        for b in SEQ_ORDER:
-            normed = pre_norm(x_in, gain_pre_row, b, 1)
-            gathered[b] = (lax.all_gather(normed, 'tp', axis=0, tiled=True).reshape(n_dev, rows, depth), 0)
 
         def swap(value, bit):
             return lax.ppermute(value, 'tp', [(d, d ^ bit) for d in range(n_dev)])
 
-        w_out_loc = w_out.reshape(q_cols, depth)
-        mid = q_cols // 2
-        near_w = {bit: swap(w_out_loc, bit) for bit in (1, 2, 4)}
-        far_w = (swap(near_w[2][:mid], 4), swap(near_w[4][mid:], 2))
-        other_core = [swap(near_w[2], 1), swap(near_w[4], 1)]
-        far_other = [swap(part, 1) for part in far_w]
-        w_out_pieces = (w_out_loc, near_w[1], near_w[2], near_w[4], *other_core, *far_w, *far_other)
+        def near_of(value):
+            return {bit: swap(value, bit) for bit in (1, 2, 4)}
+
+        def pieces_of(value, near):
+            mid = value.shape[0] // 2
+            far = (swap(near[2][:mid], 4), swap(near[4][mid:], 2))
+            other_core = [swap(near[2], 1), swap(near[4], 1)]
+            far_other = [swap(part, 1) for part in far]
+            return (value, near[1], near[2], near[4], *other_core, *far, *far_other)
 
         pos_all = lax.all_gather(positions, 'tp', axis=1, tiled=True)
+        w_out_loc, x_held, pos_all = lax.optimization_barrier((w_out.reshape(q_cols, depth), x_in, pos_all))
+        own, near = {'wo': w_out_loc}, {'wo': near_of(w_out_loc)}
+        for b in SEQ_ORDER:
+            own[b] = pre_norm(x_held, gain_pre_row, b, 1)
+            near[b] = near_of(own[b])
+
         seq_len = pos_all.shape[1]
         half = head_dim // 2
         inv_freq = ROPE_THETA ** (-2.0 * jnp.arange(half, dtype=jnp.float32) / head_dim)
@@ -775,18 +832,27 @@
         first_blk = jnp.sum(before.astype(jnp.int32), axis=-1) // BLK
         w_all = jnp.concatenate([w_query.reshape(depth, q_cols), w_key.reshape(depth, k_cols), w_value.reshape(depth, k_cols)], axis=1)
         w_t = w_all.T
+        tables = {}
+        for b in SEQ_ORDER:
+            angles = pos_all[b].astype(jnp.float32)[:, None] * inv_freq
+            cos_h, sin_h = jnp.cos(angles), jnp.sin(angles)
+            tables[b] = (jnp.concatenate([cos_h, cos_h], axis=-1), jnp.concatenate([-sin_h, sin_h], axis=-1))
+        near[SEQ_ORDER[0]], w_all, w_t, tables, first_blk = lax.optimization_barrier((near[SEQ_ORDER[0]], w_all, w_t, tables, first_blk))
+        w_out_pieces = pieces_of(own['wo'], near['wo'])
+        normed = {b: pieces_of(own[b], near[b]) for b in SEQ_ORDER}
+
         me = lax.axis_index('tp')[None]
+        devices = me ^ jnp.array(PIECE_DEVICES, jnp.int32)
+        gathered = {}
 
         saved, d_proj_all = {}, {}
         y_out, d_post = None, jnp.zeros((1, depth), jnp.float32)
         for b in SEQ_ORDER:
-            angles = pos_all[b].astype(jnp.float32)[:, None] * inv_freq
-            cos_h, sin_h = jnp.cos(angles), jnp.sin(angles)
-            cos_t = jnp.concatenate([cos_h, cos_h], axis=-1)
-            sin_t = jnp.concatenate([-sin_h, sin_h], axis=-1)
+            cos_t, sin_t = tables[b]
             pos_b = pos_all[b][None, :]
             key_pos = jnp.broadcast_to(pos_all[b][:, None], (seq_len, LANES))
-            q_b, k_b, v_b = qkv_project(*gathered[b], rows, w_all, cos_t, sin_t, q_cols, k_cols, head_dim)
+            q_b, k_b, v_b, whole = qkv_project(devices, normed[b], w_all, cos_t, sin_t, q_cols, k_cols, head_dim)
+            gathered[b] = (whole, 0)
             o_b, lse_b = attn_fwd(q_b, k_b, v_b, pos_b, key_pos, first_blk[b], groups, head_dim)
             o_mine = lax.all_to_all(o_b.reshape(n_dev, rows, q_cols), 'tp', split_axis=0, concat_axis=0, tiled=True)
             proj = out_proj(me, o_mine, w_out_pieces)

time: 1860 us -> 2200 us (1.18)
  waiting for transfers between devices: 398 us -> 865 us
  blocking collectives: 238 us -> 95.1 us
    ppermute x24 -> x51, waiting for transfers between devices: 199 us -> 834 us  [swap(): return lax.ppermute(value, 'tp', [(d, d ^ bit) for d in range(n_dev)])]
    all_gather x1, blocking collectives: 238 us -> 13.8 us  [local_body(): pos_all = lax.all_gather(positions, 'tp', axis=1, tiled=True)]
    all_gather x3, waiting for transfers between devices: 91.2 us -> 0.04 us  [local_body(): d_proj_all[b] = lax.all_gather(d_proj, 'tp', axis=0, tiled=True)]
    all_to_all x0 -> x2, blocking collectives: none -> 81.3 us  [local_body(): lax.all_to_all(o_b.reshape(n_dev, rows, q_cols), 'tp', split_axis=0, conc...]
    all_to_all x3 -> x1, waiting for transfers between devices: 107 us -> 31.4 us  [local_body(): lax.all_to_all(o_b.reshape(n_dev, rows, q_cols), 'tp', split_axis=0, conc...]
    unnamed x77 -> x107, local copies, waits for them, and re-layouts: 46.7 us -> 50 us
  transfers between devices with their start and end apart: 33 -> 55, of which waited for: 9 -> 20; matrix products, arithmetic and copies ran while one was open for 9% -> 8% of each run, Pallas kernels for 51% -> 42%
where the time goes in v6:
time: 2200 us; the launch traced here: 2190 us
  Pallas kernels  987 us (45%)
  waiting for transfers between devices  865 us (39%)
  blocking collectives  95.1 us (4%)
  local copies, waits for them, and re-layouts  78.1 us (4%)
  matrix products  76.3 us (3%)
  other arithmetic  39.1 us (2%)
  starting transfers between devices  32.3 us (1%)
    ppermute x51, waiting for transfers between devices, swap(): return lax.ppermute(value, 'tp', [(d, d ^ bit) for d in range(n_dev)])  834 us
    pallas_call x3, Pallas kernels, attn_bwd(): pl.pallas_call(functools.partial(attn_bwd_kernel, groups, head_dim, head_...  161 us
    pallas_call x3, Pallas kernels, grad_w(): pl.pallas_call(functools.partial(grad_w_kernel, has_prev, last, head_dim)...  147 us
    pallas_call x3, Pallas kernels, qkv_project(): pl.pallas_call(functools.partial(qkv_kernel, q_cols, k_cols, head_dim, he...  141 us
    pallas_call x3, Pallas kernels, attn_fwd(): pl.pallas_call(functools.partial(attn_fwd_kernel, groups, head_dim), grid...  104 us
    pallas_call x3, Pallas kernels, grad_normed_own(): pl.pallas_call(own_core_kernel, grid_spec=pltpu.PrefetchScalarGridSpec(nu...  82.5 us
    all_to_all x2, blocking collectives, local_body(): lax.all_to_all(o_b.reshape(n_dev, rows, q_cols), 'tp', split_axis=0, conc...  81.3 us
    pallas_call x3, Pallas kernels, grad_normed_pair(): pl.pallas_call(pair_core_kernel, grid_spec=pltpu.PrefetchScalarGridSpec(n...  76.6 us
  transfers between devices with their start and end apart: 55, of which 20 were waited for; matrix products, arithmetic and copies ran while one was open for 8% of the time, Pallas kernels for 42%

profile of v6, /device:TPU:0, one launch (start us, length us, event | category | flops | bytes accessed | tf_op | source)
XLA Modules:
  0.0 2188.0 jit_solution(15633558246254222192)
XLA Ops:
  95.3 133.3 %collective-permute-done.2.refs_3_ = bf16[384,5376]{1,0:T(8,128)(2,1)} collective-permute-done((bf16[384,5376]{1,0:T(8,128)(2,1)}, bf16[384,5376]{1,0:T(8,128)(2,1)}, u32[]{:S(2)}, u32[]{:S(2)}) %collective-permute-start.2) | collective-permute-done | bytes 4128800 | tf_op jit(solution)/shard_map/ppermute | solution.py:809
  234.6 48.7 %collective-permute-done.33.refs_7_ = bf16[192,5376]{1,0:T(8,128)(2,1)} collective-permute-done((bf16[192,5376]{1,0:T(8,128)(2,1)S(1)}, bf16[192,5376]{1,0:T(8,128)(2,1)}, u32[]{:S(2)}, u32[]{:S(2)}) %collective-permute-start.33) | collective-permute-done | bytes 2064416 | tf_op jit(solution)/shard_map/ppermute | solution.py:809
  307.0 46.9 %qkv_project.5 = (bf16[3072,512]{1,0:T(8,128)(2,1)}, bf16[3072,256]{1,0:T(8,128)(2,1)}, bf16[3072,256]{1,0:T(8,128)(2,1)}, bf16[8,384,5376]{2,1,0:T(8,128)(2,1)}) custom-call(s32[8]{0:T(128)} %broadcast_xor_fusion.dev_ref, bf16[384,5376]{1,0:T(8,128)(2,1)} %pre_norm.3.refs_0_, bf16[384,5376]{1,0:T(8,128)(2,1)} %collective-permute-done.refs_1_, ...), custom_call_target="tpu_custom_call" | custom-call | flops 33822867456 | bytes 83361792 | tf_op jit(solution)/shard_map/qkv_project/pallas_call | solution.py:526
  357.8 32.5 %attn_fwd.5 = (bf16[3072,512]{1,0:T(8,128)(2,1)}, f32[2,12,1,512]{3,2,1,0:T(1,128)S(1)}) custom-call(s32[12]{0:T(128)S(1)} %get-tuple-element.164.first_ref, bf16[3072,512]{1,0:T(8,128)(2,1)} %get-tuple-element.101.q_ref, bf16[3072,256]{1,0:T(8,128)(2,1)S(1)} %copy-done.16, bf16[3072,256]{1,0:T(8,128)(2,1)S(1)} %copy-done.18, ...), custom_call_target="tpu_custom_call" | custom-call | flops 9663676416 | bytes 12582912 | tf_op jit(solution)/shard_map/attn_fwd/pallas_call | solution.py:618
  399.7 31.4 %all-to-all-done.2.o_ref = bf16[8,384,512]{2,1,0:T(8,128)(2,1)S(1)} async-done(((bf16[8,384,512]{2,1,0:T(8,128)(2,1)}), bf16[8,384,512]{2,1,0:T(8,128)(2,1)S(1)}, u32[]{:S(2)}, u32[]{:S(2)}) %all-to-all-start.2) | async-done | bytes 3145760 | tf_op jit(solution)/shard_map/all_to_all | solution.py:857
  477.0 170.8 %collective-permute-done.23.refs_3_ = bf16[384,5376]{1,0:T(8,128)(2,1)S(1)} collective-permute-done((bf16[384,5376]{1,0:T(8,128)(2,1)}, bf16[384,5376]{1,0:T(8,128)(2,1)S(1)}, u32[]{:S(2)}, u32[]{:S(2)}) %collective-permute-start.23) | collective-permute-done | bytes 4128800 | tf_op jit(solution)/shard_map/ppermute | solution.py:809
  652.5 87.6 %collective-permute-done.27.refs_7_ = bf16[192,5376]{1,0:T(8,128)(2,1)S(1)} collective-permute-done((bf16[192,5376]{1,0:T(8,128)(2,1)S(1)}, bf16[192,5376]{1,0:T(8,128)(2,1)S(1)}, u32[]{:S(2)}, u32[]{:S(2)}) %collective-permute-start.27) | collective-permute-done | bytes 2064416 | tf_op jit(solution)/shard_map/ppermute | solution.py:809
  749.5 47.0 %qkv_project.4 = (bf16[3072,512]{1,0:T(8,128)(2,1)}, bf16[3072,256]{1,0:T(8,128)(2,1)}, bf16[3072,256]{1,0:T(8,128)(2,1)}, bf16[8,384,5376]{2,1,0:T(8,128)(2,1)}) custom-call(s32[8]{0:T(128)} %broadcast_xor_fusion.dev_ref, bf16[384,5376]{1,0:T(8,128)(2,1)} %pre_norm.5.refs_0_, bf16[384,5376]{1,0:T(8,128)(2,1)} %copy-done.40, bf16[384,5376]{1,0:T(8,128)(2,1)} %copy-done.37, ...), custom_call_target="tpu_custom_call" | custom-call | flops 33822867456 | bytes 83361792 | tf_op jit(solution)/shard_map/qkv_project/pallas_call | solution.py:526
  800.4 32.5 %attn_fwd.4 = (bf16[3072,512]{1,0:T(8,128)(2,1)}, f32[2,12,1,512]{3,2,1,0:T(1,128)S(1)}) custom-call(s32[12]{0:T(128)S(1)} %get-tuple-element.165.first_ref, bf16[3072,512]{1,0:T(8,128)(2,1)} %get-tuple-element.92.q_ref, bf16[3072,256]{1,0:T(8,128)(2,1)S(1)} %copy-done.20, bf16[3072,256]{1,0:T(8,128)(2,1)S(1)} %copy-done.22, s32[1,3072]{1,0:T(1,128)S(1)} %copy-done.10, ...), custom_call_target="tpu_custom_call" | custom-call | flops 9663676416 | bytes 12582912 | tf_op jit(solution)/shard_map/attn_fwd/pallas_call | solution.py:618
  832.9 40.9 %all_to_all.15.o_ref = bf16[8,384,512]{2,1,0:T(8,128)(2,1)S(1)} all-to-all(bf16[8,384,512]{2,1,0:T(8,128)(2,1)} %bitcast.36), channel_id=1, replica_groups=mesh['dp'=1,'tp'=8] {'tp'}, dimensions={0} | all-to-all | bytes 6291456 | tf_op jit(solution)/shard_map/all_to_all | solution.py:857
  918.9 173.2 %collective-permute-done.5.refs_3_ = bf16[384,5376]{1,0:T(8,128)(2,1)S(1)} collective-permute-done((bf16[384,5376]{1,0:T(8,128)(2,1)}, bf16[384,5376]{1,0:T(8,128)(2,1)S(1)}, u32[]{:S(2)}, u32[]{:S(2)}) %collective-permute-start.5) | collective-permute-done | bytes 4128800 | tf_op jit(solution)/shard_map/ppermute | solution.py:809
  1094.9 88.1 %collective-permute-done.9.refs_7_ = bf16[192,5376]{1,0:T(8,128)(2,1)S(1)} collective-permute-done((bf16[192,5376]{1,0:T(8,128)(2,1)S(1)}, bf16[192,5376]{1,0:T(8,128)(2,1)S(1)}, u32[]{:S(2)}, u32[]{:S(2)}) %collective-permute-start.9) | collective-permute-done | bytes 2064416 | tf_op jit(solution)/shard_map/ppermute | solution.py:809
  1193.5 46.8 %qkv_project.3 = (bf16[3072,512]{1,0:T(8,128)(2,1)}, bf16[3072,256]{1,0:T(8,128)(2,1)}, bf16[3072,256]{1,0:T(8,128)(2,1)}, bf16[8,384,5376]{2,1,0:T(8,128)(2,1)}) custom-call(s32[8]{0:T(128)} %broadcast_xor_fusion.dev_ref, bf16[384,5376]{1,0:T(8,128)(2,1)} %pre_norm.4.refs_0_, bf16[384,5376]{1,0:T(8,128)(2,1)} %copy-done.39, bf16[384,5376]{1,0:T(8,128)(2,1)} %copy-done.36, ...), custom_call_target="tpu_custom_call" | custom-call | flops 33822867456 | bytes 83361792 | tf_op jit(solution)/shard_map/qkv_project/pallas_call | solution.py:526
  1244.2 39.4 %attn_fwd.3 = (bf16[3072,512]{1,0:T(8,128)(2,1)}, f32[2,12,1,512]{3,2,1,0:T(1,128)S(1)}) custom-call(s32[12]{0:T(128)S(1)} %get-tuple-element.166.first_ref, bf16[3072,512]{1,0:T(8,128)(2,1)} %get-tuple-element.85.q_ref, bf16[3072,256]{1,0:T(8,128)(2,1)S(1)} %copy-done.24, bf16[3072,256]{1,0:T(8,128)(2,1)S(1)} %copy-done.26, s32[1,3072]{1,0:T(1,128)S(1)} %copy-done.7, ...), custom_call_target="tpu_custom_call" | custom-call | flops 9663676416 | bytes 12582912 | tf_op jit(solution)/shard_map/attn_fwd/pallas_call | solution.py:618
  1283.6 40.4 %all_to_all.16.o_ref = bf16[8,384,512]{2,1,0:T(8,128)(2,1)S(1)} all-to-all(bf16[8,384,512]{2,1,0:T(8,128)(2,1)} %bitcast.37), channel_id=1, replica_groups=mesh['dp'=1,'tp'=8] {'tp'}, dimensions={0} | all-to-all | bytes 6291456 | tf_op jit(solution)/shard_map/all_to_all | solution.py:857
  1386.8 50.7 %attn_bwd.5.d0_ref.d1_ref.d_ref = bf16[3072,1024]{1,0:T(8,128)(2,1)} custom-call(s32[12]{0:T(128)S(1)} %copy-done.15, bf16[3072,512]{1,0:T(8,128)(2,1)} %get-tuple-element.101.q_ref, bf16[3072,256]{1,0:T(8,128)(2,1)S(1)} %copy-done.17, bf16[3072,256]{1,0:T(8,128)(2,1)S(1)} %copy-done.19, bf16[3072,512]{1,0:T(8,128)(2,1)} %get-tuple-element.104.o_ref, ...), custom_call_target="tpu_custom_call" | custom-call | flops 24159191040 | bytes 25165824 | tf_op jit(solution)/shard_map/attn_bwd/pallas_call | solution.py:753
  1491.1 50.4 %attn_bwd.4.d0_ref.d1_ref.d_ref = bf16[3072,1024]{1,0:T(8,128)(2,1)} custom-call(s32[12]{0:T(128)S(1)} %get-tuple-element.165.first_ref, bf16[3072,512]{1,0:T(8,128)(2,1)} %get-tuple-element.92.q_ref, bf16[3072,256]{1,0:T(8,128)(2,1)S(1)} %copy-done.21, bf16[3072,256]{1,0:T(8,128)(2,1)S(1)} %copy-done.23, bf16[3072,512]{1,0:T(8,128)(2,1)} %get-tuple-element.95.o_ref, ...), custom_call_target="tpu_custom_call" | custom-call | flops 24159191040 | bytes 25165824 | tf_op jit(solution)/shard_map/attn_bwd/pallas_call | solution.py:753
  1594.7 60.0 %attn_bwd.3.d0_ref.d1_ref.d_ref = bf16[3072,1024]{1,0:T(8,128)(2,1)} custom-call(s32[12]{0:T(128)S(1)} %get-tuple-element.166.first_ref, bf16[3072,512]{1,0:T(8,128)(2,1)} %get-tuple-element.85.q_ref, bf16[3072,256]{1,0:T(8,128)(2,1)S(1)} %copy-done.25, bf16[3072,256]{1,0:T(8,128)(2,1)S(1)} %copy-done.27, bf16[3072,512]{1,0:T(8,128)(2,1)} %get-tuple-element.88.o_ref, ...), custom_call_target="tpu_custom_call" | custom-call | flops 24159191040 | bytes 25165824 | tf_op jit(solution)/shard_map/attn_bwd/pallas_call | solution.py:753
  1680.4 44.6 %grad_w.3.refs_0_ = f32[5376,1024]{1,0:T(8,128)} custom-call(bf16[8,384,5376]{2,1,0:T(8,128)(2,1)} %get-tuple-element.142.a_ref, bf16[3072,1024]{1,0:T(8,128)(2,1)} %attn_bwd.5.d0_ref.d1_ref.d_ref), custom_call_target="tpu_custom_call" | custom-call | flops 33822867456 | bytes 83361792 | tf_op jit(solution)/shard_map/grad_w/pallas_call | solution.py:412
  1752.5 45.7 %grad_w.4.refs_0_ = f32[5376,1024]{1,0:T(8,128)} custom-call(bf16[8,384,5376]{2,1,0:T(8,128)(2,1)} %get-tuple-element.141.a_ref, bf16[3072,1024]{1,0:T(8,128)(2,1)} %attn_bwd.3.d0_ref.d1_ref.d_ref, f32[5376,1024]{1,0:T(8,128)} %grad_w.3.refs_0_), custom_call_target="tpu_custom_call", output_to_operand_aliasing={{}: (2, {})} | custom-call | flops 33822867456 | bytes 83361792 | tf_op jit(solution)/shard_map/grad_w/pallas_call | solution.py:412
  1798.1 27.6 %grad_normed_own.4 = (bf16[2,384,2688]{2,1,0:T(8,128)(2,1)}, bf16[2,384,2688]{2,1,0:T(8,128)(2,1)}, bf16[2,384,2688]{2,1,0:T(8,128)(2,1)}, bf16[2,384,2688]{2,1,0:T(8,128)(2,1)}) custom-call(s32[1]{0:T(128)} %bitcast.me_ref.dst_ref, bf16[3072,1024]{1,0:T(8,128)(2,1)} %attn_bwd.4.d0_ref.d1_ref.d_ref, bf16[3072,1024]{1,0:T(8,128)(2,1)} %attn_bwd.4.d0_ref.d1_ref.d_ref, ...), custom_call_target="tpu_custom_call" | custom-call | flops 16911433728 | bytes 44040192 | tf_op jit(solution)/shard_map/grad_normed_own/pallas_call | solution.py:285
  1865.1 56.4 %grad_w.5 = (f32[5376,4,128]{2,1,0:T(4,128)}, f32[5376,2,128]{2,1,0:T(2,128)}, f32[5376,2,128]{2,1,0:T(2,128)}) custom-call(bf16[8,384,5376]{2,1,0:T(8,128)(2,1)} %get-tuple-element.140.a_ref, bf16[3072,1024]{1,0:T(8,128)(2,1)} %attn_bwd.4.d0_ref.d1_ref.d_ref, f32[5376,1024]{1,0:T(8,128)} %grad_w.4.refs_0_), custom_call_target="tpu_custom_call" | custom-call | flops 33822867456 | bytes 83361792 | tf_op jit(solution)/shard_map/grad_w/pallas_call | solution.py:412
  1955.1 66.6 %collective-permute-done.37.near_x_ref.refs_1_ = bf16[2,384,2688]{2,1,0:T(8,128)(2,1)} collective-permute-done((bf16[2,384,2688]{2,1,0:T(8,128)(2,1)}, bf16[2,384,2688]{2,1,0:T(8,128)(2,1)}, u32[]{:S(2)}, u32[]{:S(2)}) %collective-permute-start.37) | collective-permute-done | bytes 4128800 | tf_op jit(solution)/shard_map/ppermute | solution.py:809
  2027.5 38.4 %collective-permute-done.49.refs_2_ = bf16[384,2688]{1,0:T(8,128)(2,1)S(1)} collective-permute-done((bf16[384,2688]{1,0:T(8,128)(2,1)}, bf16[384,2688]{1,0:T(8,128)(2,1)S(1)}, u32[]{:S(2)}, u32[]{:S(2)}) %collective-permute-start.49) | collective-permute-done | bytes 2064416 | tf_op jit(solution)/shard_map/ppermute | solution.py:809
  (272 shorter events, 673.4 us)
Async XLA Ops:
  21.0 213.1 %collective-permute-start.14 = (bf16[512,5376]{1,0:T(8,128)(2,1)}, bf16[512,5376]{1,0:T(8,128)(2,1)}, u32[]{:S(2)}, u32[]{:S(2)}) collective-permute-start(bf16[512,5376]{1,0:T(8,128)(2,1)} %bitcast.1.refs_0_), channel_id=1, source_target_pairs={{0,4},{1,5},{2,6},{3,7},{4,0},{5,1},{6,2},{7,3}} | collective-permute-start | bytes 16515080 | tf_op jit(solution)/shard_map/ppermute | solution.py:809
  30.7 197.9 %collective-permute-start.2 = (bf16[384,5376]{1,0:T(8,128)(2,1)}, bf16[384,5376]{1,0:T(8,128)(2,1)}, u32[]{:S(2)}, u32[]{:S(2)}) collective-permute-start(bf16[384,5376]{1,0:T(8,128)(2,1)} %pre_norm.3.refs_0_), channel_id=1, source_target_pairs={{0,4},{1,5},{2,6},{3,7},{4,0},{5,1},{6,2},{7,3}} | collective-permute-start | bytes 12386312 | tf_op jit(solution)/shard_map/ppermute | solution.py:809
  32.0 196.5 %collective-permute-start.1 = (bf16[384,5376]{1,0:T(8,128)(2,1)}, bf16[384,5376]{1,0:T(8,128)(2,1)}, u32[]{:S(2)}, u32[]{:S(2)}) collective-permute-start(bf16[384,5376]{1,0:T(8,128)(2,1)} %pre_norm.3.refs_0_), channel_id=1, source_target_pairs={{0,2},{1,3},{2,0},{3,1},{4,6},{5,7},{6,4},{7,5}} | collective-permute-start | bytes 12386312 | tf_op jit(solution)/shard_map/ppermute | solution.py:809
  32.7 195.8 %collective-permute-start = (bf16[384,5376]{1,0:T(8,128)(2,1)}, bf16[384,5376]{1,0:T(8,128)(2,1)}, u32[]{:S(2)}, u32[]{:S(2)}) collective-permute-start(bf16[384,5376]{1,0:T(8,128)(2,1)} %pre_norm.3.refs_0_), channel_id=1, source_target_pairs={{0,1},{1,0},{2,3},{3,2},{4,5},{5,4},{6,7},{7,6}} | collective-permute-start | bytes 12386312 | tf_op jit(solution)/shard_map/ppermute | solution.py:809
  32.7 268.2 %collective-permute-start.13 = (bf16[512,5376]{1,0:T(8,128)(2,1)}, bf16[512,5376]{1,0:T(8,128)(2,1)}, u32[]{:S(2)}, u32[]{:S(2)}) collective-permute-start(bf16[512,5376]{1,0:T(8,128)(2,1)} %bitcast.1.refs_0_), channel_id=1, source_target_pairs={{0,2},{1,3},{2,0},{3,1},{4,6},{5,7},{6,4},{7,5}} | collective-permute-start | bytes 16515080 | tf_op jit(solution)/shard_map/ppermute | solution.py:809
  393.3 966.6 %all-gather.8.cloned.1.call-start = ((), (), s32[]{:S(2)}) async-start(), calls=%async_computation.5 | async-start | bytes 37158912 | tf_op jit(solution)/shard_map/all_gather | solution.py:860
  467.9 995.2 %all-gather.6.cloned.1.call-start = ((), (), s32[]{:S(2)}) async-start(), calls=%async_computation.4 | async-start | bytes 37158912 | tf_op jit(solution)/shard_map/all_gather | solution.py:860
  476.0 171.8 %collective-permute-start.23 = (bf16[384,5376]{1,0:T(8,128)(2,1)}, bf16[384,5376]{1,0:T(8,128)(2,1)S(1)}, u32[]{:S(2)}, u32[]{:S(2)}) collective-permute-start(bf16[384,5376]{1,0:T(8,128)(2,1)} %pre_norm.5.refs_0_), channel_id=1, source_target_pairs={{0,4},{1,5},{2,6},{3,7},{4,0},{5,1},{6,2},{7,3}} | collective-permute-start | bytes 12386312 | tf_op jit(solution)/shard_map/ppermute | solution.py:809
  476.4 174.7 %collective-permute-start.22 = (bf16[384,5376]{1,0:T(8,128)(2,1)}, bf16[384,5376]{1,0:T(8,128)(2,1)S(1)}, u32[]{:S(2)}, u32[]{:S(2)}) collective-permute-start(bf16[384,5376]{1,0:T(8,128)(2,1)} %pre_norm.5.refs_0_), channel_id=1, source_target_pairs={{0,2},{1,3},{2,0},{3,1},{4,6},{5,7},{6,4},{7,5}} | collective-permute-start | bytes 12386312 | tf_op jit(solution)/shard_map/ppermute | solution.py:809
  477.0 264.1 %collective-permute-start.21 = (bf16[384,5376]{1,0:T(8,128)(2,1)}, bf16[384,5376]{1,0:T(8,128)(2,1)S(1)}, u32[]{:S(2)}, u32[]{:S(2)}) collective-permute-start(bf16[384,5376]{1,0:T(8,128)(2,1)} %pre_norm.5.refs_0_), channel_id=1, source_target_pairs={{0,1},{1,0},{2,3},{3,2},{4,5},{5,4},{6,7},{7,6}} | collective-permute-start | bytes 12386312 | tf_op jit(solution)/shard_map/ppermute | solution.py:809
  909.7 657.8 %all-gather.4.cloned.1.call-start = ((), (), s32[]{:S(2)}) async-start(), calls=%async_computation.3 | async-start | bytes 37158912 | tf_op jit(solution)/shard_map/all_gather | solution.py:860
  918.0 174.1 %collective-permute-start.5 = (bf16[384,5376]{1,0:T(8,128)(2,1)}, bf16[384,5376]{1,0:T(8,128)(2,1)S(1)}, u32[]{:S(2)}, u32[]{:S(2)}) collective-permute-start(bf16[384,5376]{1,0:T(8,128)(2,1)} %pre_norm.4.refs_0_), channel_id=1, source_target_pairs={{0,4},{1,5},{2,6},{3,7},{4,0},{5,1},{6,2},{7,3}} | collective-permute-start | bytes 12386312 | tf_op jit(solution)/shard_map/ppermute | solution.py:809
  918.7 174.4 %collective-permute-start.4 = (bf16[384,5376]{1,0:T(8,128)(2,1)}, bf16[384,5376]{1,0:T(8,128)(2,1)S(1)}, u32[]{:S(2)}, u32[]{:S(2)}) collective-permute-start(bf16[384,5376]{1,0:T(8,128)(2,1)} %pre_norm.4.refs_0_), channel_id=1, source_target_pairs={{0,2},{1,3},{2,0},{3,1},{4,6},{5,7},{6,4},{7,5}} | collective-permute-start | bytes 12386312 | tf_op jit(solution)/shard_map/ppermute | solution.py:809
  918.9 265.1 %collective-permute-start.3 = (bf16[384,5376]{1,0:T(8,128)(2,1)}, bf16[384,5376]{1,0:T(8,128)(2,1)S(1)}, u32[]{:S(2)}, u32[]{:S(2)}) collective-permute-start(bf16[384,5376]{1,0:T(8,128)(2,1)} %pre_norm.4.refs_0_), channel_id=1, source_target_pairs={{0,1},{1,0},{2,3},{3,2},{4,5},{5,4},{6,7},{7,6}} | collective-permute-start | bytes 12386312 | tf_op jit(solution)/shard_map/ppermute | solution.py:809
  1463.0 262.0 %collective-permute-start.46 = (bf16[4,384,5376]{2,1,0:T(8,128)(2,1)}, bf16[4,384,5376]{2,1,0:T(8,128)(2,1)}, u32[]{:S(2)}, u32[]{:S(2)}) collective-permute-start(bf16[4,384,5376]{2,1,0:T(8,128)(2,1)} %grad_normed_pair.5), channel_id=1, source_target_pairs={{0,1},{1,0},{2,3},{3,2},{4,5},{5,4},{6,7},{7,6}} | collective-permute-start | bytes 49545224 | tf_op jit(solution)/shard_map/ppermute | solution.py:809
  1567.1 231.0 %collective-permute-start.41 = (bf16[4,384,5376]{2,1,0:T(8,128)(2,1)}, bf16[4,384,5376]{2,1,0:T(8,128)(2,1)}, u32[]{:S(2)}, u32[]{:S(2)}) collective-permute-start(bf16[4,384,5376]{2,1,0:T(8,128)(2,1)} %grad_normed_pair.4), channel_id=1, source_target_pairs={{0,1},{1,0},{2,3},{3,2},{4,5},{5,4},{6,7},{7,6}} | collective-permute-start | bytes 49545224 | tf_op jit(solution)/shard_map/ppermute | solution.py:809
  1680.2 149.5 %collective-permute-start.36 = (bf16[4,384,5376]{2,1,0:T(8,128)(2,1)}, bf16[4,384,5376]{2,1,0:T(8,128)(2,1)}, u32[]{:S(2)}, u32[]{:S(2)}) collective-permute-start(bf16[4,384,5376]{2,1,0:T(8,128)(2,1)} %grad_normed_pair.3), channel_id=1, source_target_pairs={{0,1},{1,0},{2,3},{3,2},{4,5},{5,4},{6,7},{7,6}} | collective-permute-start | bytes 49545224 | tf_op jit(solution)/shard_map/ppermute | solution.py:809
  1825.7 119.6 %collective-permute-start.42 = (bf16[2,384,2688]{2,1,0:T(8,128)(2,1)}, bf16[2,384,2688]{2,1,0:T(8,128)(2,1)}, u32[]{:S(2)}, u32[]{:S(2)}) collective-permute-start(bf16[2,384,2688]{2,1,0:T(8,128)(2,1)} %get-tuple-element.122), channel_id=1, source_target_pairs={{0,2},{1,3},{2,0},{3,1},{4,6},{5,7},{6,4},{7,5}} | collective-permute-start | bytes 12386312 | tf_op jit(solution)/shard_map/ppermute | solution.py:809
  1857.2 164.6 %collective-permute-start.37 = (bf16[2,384,2688]{2,1,0:T(8,128)(2,1)}, bf16[2,384,2688]{2,1,0:T(8,128)(2,1)}, u32[]{:S(2)}, u32[]{:S(2)}) collective-permute-start(bf16[2,384,2688]{2,1,0:T(8,128)(2,1)} %get-tuple-element.114), channel_id=1, source_target_pairs={{0,2},{1,3},{2,0},{3,1},{4,6},{5,7},{6,4},{7,5}} | collective-permute-start | bytes 12386312 | tf_op jit(solution)/shard_map/ppermute | solution.py:809
  1857.2 164.5 %collective-permute-start.38 = (bf16[2,384,2688]{2,1,0:T(8,128)(2,1)}, bf16[2,384,2688]{2,1,0:T(8,128)(2,1)}, u32[]{:S(2)}, u32[]{:S(2)}) collective-permute-start(bf16[2,384,2688]{2,1,0:T(8,128)(2,1)} %get-tuple-element.116), channel_id=1, source_target_pairs={{0,4},{1,5},{2,6},{3,7},{4,0},{5,1},{6,2},{7,3}} | collective-permute-start | bytes 12386312 | tf_op jit(solution)/shard_map/ppermute | solution.py:809
  1865.0 200.9 %collective-permute-start.49 = (bf16[384,2688]{1,0:T(8,128)(2,1)}, bf16[384,2688]{1,0:T(8,128)(2,1)S(1)}, u32[]{:S(2)}, u32[]{:S(2)}) collective-permute-start(bf16[384,2688]{1,0:T(8,128)(2,1)} %get-tuple-element.133), channel_id=1, source_target_pairs={{0,4},{1,5},{2,6},{3,7},{4,0},{5,1},{6,2},{7,3}} | collective-permute-start | bytes 6193160 | tf_op jit(solution)/shard_map/ppermute | solution.py:809
  1945.3 174.1 %collective-permute-start.50 = (bf16[384,2688]{1,0:T(8,128)(2,1)}, bf16[384,2688]{1,0:T(8,128)(2,1)S(1)}, u32[]{:S(2)}, u32[]{:S(2)}) collective-permute-start(bf16[384,2688]{1,0:T(8,128)(2,1)} %get-tuple-element.134), channel_id=1, source_target_pairs={{0,2},{1,3},{2,0},{3,1},{4,6},{5,7},{6,4},{7,5}} | collective-permute-start | bytes 6193160 | tf_op jit(solution)/shard_map/ppermute | solution.py:809
  1953.1 181.2 %collective-permute-start.44 = (bf16[384,2688]{1,0:T(8,128)(2,1)}, bf16[384,2688]{1,0:T(8,128)(2,1)S(1)}, u32[]{:S(2)}, u32[]{:S(2)}) collective-permute-start(bf16[384,2688]{1,0:T(8,128)(2,1)} %get-tuple-element.125), channel_id=1, source_target_pairs={{0,4},{1,5},{2,6},{3,7},{4,0},{5,1},{6,2},{7,3}} | collective-permute-start | bytes 6193160 | tf_op jit(solution)/shard_map/ppermute | solution.py:809
  2027.5 126.3 %collective-permute-start.39 = (bf16[384,2688]{1,0:T(8,128)(2,1)}, bf16[384,2688]{1,0:T(8,128)(2,1)S(1)}, u32[]{:S(2)}, u32[]{:S(2)}) collective-permute-start(bf16[384,2688]{1,0:T(8,128)(2,1)} %get-tuple-element.117), channel_id=1, source_target_pairs={{0,4},{1,5},{2,6},{3,7},{4,0},{5,1},{6,2},{7,3}} | collective-permute-start | bytes 6193160 | tf_op jit(solution)/shard_map/ppermute | solution.py:809
  (83 other events, 3478.9 us)
Sparse Core Ops, SparseCore 0:
  468.0 277.9 all-gather.7
  909.9 281.3 all-gather.5
  1360.0 151.9 all-gather.3

commit v7 on v6

--- a/solution.py
+++ b/solution.py
@@ -393,9 +393,9 @@
             return
         col = 0
         for out in outs:
-            for h in range(out.shape[1]):
-                out[cols, h, :] = total[:, col:col + head_dim]
-                col += head_dim
+            heads = out.shape[1]
+            out[cols] = total[:, col:col + heads * head_dim].reshape(step, heads, head_dim)
+            col += heads * head_dim
 
 
 def grad_w(gathered, slot, rows, d_lin, heads, head_dim, prev, last):
@@ -818,11 +818,16 @@
             far_other = [swap(part, 1) for part in far]
             return (value, near[1], near[2], near[4], *other_core, *far, *far_other)
 
+        w_out_loc = w_out.reshape(q_cols, depth)
+        own, near = {}, {'wo': near_of(w_out_loc)}
+        for b in SEQ_ORDER[:2]:
+            own[b] = pre_norm(x_in, gain_pre_row, b, 1)
+        positions, own = lax.optimization_barrier((positions, own))
         pos_all = lax.all_gather(positions, 'tp', axis=1, tiled=True)
-        w_out_loc, x_held, pos_all = lax.optimization_barrier((w_out.reshape(q_cols, depth), x_in, pos_all))
-        own, near = {'wo': w_out_loc}, {'wo': near_of(w_out_loc)}
+        own, x_held, pos_all = lax.optimization_barrier((own, x_in, pos_all))
         for b in SEQ_ORDER:
-            own[b] = pre_norm(x_held, gain_pre_row, b, 1)
+            if b not in own:
+                own[b] = pre_norm(x_held, gain_pre_row, b, 1)
             near[b] = near_of(own[b])
 
         seq_len = pos_all.shape[1]
@@ -838,7 +843,7 @@
             cos_h, sin_h = jnp.cos(angles), jnp.sin(angles)
             tables[b] = (jnp.concatenate([cos_h, cos_h], axis=-1), jnp.concatenate([-sin_h, sin_h], axis=-1))
         near[SEQ_ORDER[0]], w_all, w_t, tables, first_blk = lax.optimization_barrier((near[SEQ_ORDER[0]], w_all, w_t, tables, first_blk))
-        w_out_pieces = pieces_of(own['wo'], near['wo'])
+        w_out_pieces = pieces_of(w_out_loc, near['wo'])
         normed = {b: pieces_of(own[b], near[b]) for b in SEQ_ORDER}
 
         me = lax.axis_index('tp')[None]

time: 2200 us -> 2280 us (1.036)
  blocking collectives: 95.1 us -> 190 us
    all_gather x1, blocking collectives: 13.8 us -> 109 us  [local_body(): pos_all = lax.all_gather(positions, 'tp', axis=1, tiled=True)]
    unnamed x107 -> x103, local copies, waits for them, and re-layouts: 50 us -> 44.9 us
  transfers between devices with their start and end apart: 55 -> 55, of which waited for: 20 -> 21; matrix products, arithmetic and copies ran while one was open for 8% -> 7% of each run, Pallas kernels for 42% -> 40%
where the time goes in v7:
time: 2280 us; the launch traced here: 2270 us
  Pallas kernels  971 us (43%)
  waiting for transfers between devices  869 us (38%)
  blocking collectives  190 us (8%)
  matrix products  76.7 us (3%)
  local copies, waits for them, and re-layouts  73 us (3%)
  other arithmetic  39.2 us (2%)
  starting transfers between devices  34.4 us (2%)
    ppermute x51, waiting for transfers between devices, swap(): return lax.ppermute(value, 'tp', [(d, d ^ bit) for d in range(n_dev)])  837 us
    pallas_call x3, Pallas kernels, attn_bwd(): pl.pallas_call(functools.partial(attn_bwd_kernel, groups, head_dim, head_...  159 us
    pallas_call x3, Pallas kernels, qkv_project(): pl.pallas_call(functools.partial(qkv_kernel, q_cols, k_cols, head_dim, he...  139 us
    pallas_call x3, Pallas kernels, grad_w(): pl.pallas_call(functools.partial(grad_w_kernel, has_prev, last, head_dim)...  136 us
    all_gather x1, blocking collectives, local_body(): pos_all = lax.all_gather(positions, 'tp', axis=1, tiled=True)  109 us
    pallas_call x3, Pallas kernels, attn_fwd(): pl.pallas_call(functools.partial(attn_fwd_kernel, groups, head_dim), grid...  104 us
    pallas_call x3, Pallas kernels, grad_normed_own(): pl.pallas_call(own_core_kernel, grid_spec=pltpu.PrefetchScalarGridSpec(nu...  82.3 us
    all_to_all x2, blocking collectives, local_body(): lax.all_to_all(o_b.reshape(n_dev, rows, q_cols), 'tp', split_axis=0, conc...  80.5 us
  transfers between devices with their start and end apart: 55, of which 21 were waited for; matrix products, arithmetic and copies ran while one was open for 7% of the time, Pallas kernels for 40%

profile of v7, /device:TPU:0, one launch (start us, length us, event | category | flops | bytes accessed | tf_op | source)
XLA Modules:
  0.0 2267.2 jit_solution(3241400573315064400)
XLA Ops:
  27.1 109.0 %all_gather.12 = s32[3,3072]{1,0:T(4,128)S(1)} all-gather(s32[3,384]{1,0:T(4,128)S(1)} %copy-done.36), channel_id=1, replica_groups=mesh['dp'=1,'tp'=8] {'tp'}, dimensions={1}, use_global_device_ids=true | all-gather | bytes 41472 | tf_op jit(solution)/shard_map/all_gather | solution.py:826
  235.1 153.9 %collective-permute-done.33.refs_7_ = bf16[192,5376]{1,0:T(8,128)(2,1)} collective-permute-done((bf16[192,5376]{1,0:T(8,128)(2,1)S(1)}, bf16[192,5376]{1,0:T(8,128)(2,1)}, u32[]{:S(2)}, u32[]{:S(2)}) %collective-permute-start.33) | collective-permute-done | bytes 2064416 | tf_op jit(solution)/shard_map/ppermute | solution.py:809
  411.9 46.1 %qkv_project.5 = (bf16[3072,512]{1,0:T(8,128)(2,1)}, bf16[3072,256]{1,0:T(8,128)(2,1)}, bf16[3072,256]{1,0:T(8,128)(2,1)}, bf16[8,384,5376]{2,1,0:T(8,128)(2,1)}) custom-call(s32[8]{0:T(128)} %broadcast_xor_fusion.dev_ref, bf16[384,5376]{1,0:T(8,128)(2,1)} %pre_norm.3.refs_0_, bf16[384,5376]{1,0:T(8,128)(2,1)} %collective-permute-done.refs_1_, ...), custom_call_target="tpu_custom_call" | custom-call | flops 33822867456 | bytes 83361792 | tf_op jit(solution)/shard_map/qkv_project/pallas_call | solution.py:526
  461.8 32.5 %attn_fwd.5 = (bf16[3072,512]{1,0:T(8,128)(2,1)}, f32[2,12,1,512]{3,2,1,0:T(1,128)S(1)}) custom-call(s32[12]{0:T(128)S(1)} %get-tuple-element.172.first_ref, bf16[3072,512]{1,0:T(8,128)(2,1)} %get-tuple-element.109.q_ref, bf16[3072,256]{1,0:T(8,128)(2,1)S(1)} %copy-done.13, bf16[3072,256]{1,0:T(8,128)(2,1)S(1)} %copy-done.15, ...), custom_call_target="tpu_custom_call" | custom-call | flops 9663676416 | bytes 12582912 | tf_op jit(solution)/shard_map/attn_fwd/pallas_call | solution.py:618
  503.8 31.4 %all-to-all-done.2.o_ref = bf16[8,384,512]{2,1,0:T(8,128)(2,1)S(1)} async-done(((bf16[8,384,512]{2,1,0:T(8,128)(2,1)}), bf16[8,384,512]{2,1,0:T(8,128)(2,1)S(1)}, u32[]{:S(2)}, u32[]{:S(2)}) %all-to-all-start.2) | async-done | bytes 3145760 | tf_op jit(solution)/shard_map/all_to_all | solution.py:862
  573.3 163.5 %collective-permute-done.23.refs_3_ = bf16[384,5376]{1,0:T(8,128)(2,1)S(1)} collective-permute-done((bf16[384,5376]{1,0:T(8,128)(2,1)}, bf16[384,5376]{1,0:T(8,128)(2,1)S(1)}, u32[]{:S(2)}, u32[]{:S(2)}) %collective-permute-start.23) | collective-permute-done | bytes 4128800 | tf_op jit(solution)/shard_map/ppermute | solution.py:809
  742.3 86.4 %collective-permute-done.27.refs_7_ = bf16[192,5376]{1,0:T(8,128)(2,1)S(1)} collective-permute-done((bf16[192,5376]{1,0:T(8,128)(2,1)S(1)}, bf16[192,5376]{1,0:T(8,128)(2,1)S(1)}, u32[]{:S(2)}, u32[]{:S(2)}) %collective-permute-start.27) | collective-permute-done | bytes 2064416 | tf_op jit(solution)/shard_map/ppermute | solution.py:809
  837.9 46.6 %qkv_project.4 = (bf16[3072,512]{1,0:T(8,128)(2,1)}, bf16[3072,256]{1,0:T(8,128)(2,1)}, bf16[3072,256]{1,0:T(8,128)(2,1)}, bf16[8,384,5376]{2,1,0:T(8,128)(2,1)}) custom-call(s32[8]{0:T(128)} %broadcast_xor_fusion.dev_ref, bf16[384,5376]{1,0:T(8,128)(2,1)} %pre_norm.4.refs_0_, bf16[384,5376]{1,0:T(8,128)(2,1)} %copy-done.38, bf16[384,5376]{1,0:T(8,128)(2,1)} %copy-done.34, ...), custom_call_target="tpu_custom_call" | custom-call | flops 33822867456 | bytes 83361792 | tf_op jit(solution)/shard_map/qkv_project/pallas_call | solution.py:526
  888.4 32.5 %attn_fwd.4 = (bf16[3072,512]{1,0:T(8,128)(2,1)}, f32[2,12,1,512]{3,2,1,0:T(1,128)S(1)}) custom-call(s32[12]{0:T(128)S(1)} %get-tuple-element.173.first_ref, bf16[3072,512]{1,0:T(8,128)(2,1)} %get-tuple-element.100.q_ref, bf16[3072,256]{1,0:T(8,128)(2,1)S(1)} %copy-done.17, bf16[3072,256]{1,0:T(8,128)(2,1)S(1)} %copy-done.19, ...), custom_call_target="tpu_custom_call" | custom-call | flops 9663676416 | bytes 12582912 | tf_op jit(solution)/shard_map/attn_fwd/pallas_call | solution.py:618
  920.8 40.1 %all_to_all.15.o_ref = bf16[8,384,512]{2,1,0:T(8,128)(2,1)S(1)} all-to-all(bf16[8,384,512]{2,1,0:T(8,128)(2,1)} %bitcast.36), channel_id=1, replica_groups=mesh['dp'=1,'tp'=8] {'tp'}, dimensions={0} | all-to-all | bytes 6291456 | tf_op jit(solution)/shard_map/all_to_all | solution.py:862
  1006.2 173.4 %collective-permute-done.5.refs_3_ = bf16[384,5376]{1,0:T(8,128)(2,1)S(1)} collective-permute-done((bf16[384,5376]{1,0:T(8,128)(2,1)}, bf16[384,5376]{1,0:T(8,128)(2,1)S(1)}, u32[]{:S(2)}, u32[]{:S(2)}) %collective-permute-start.5) | collective-permute-done | bytes 4128800 | tf_op jit(solution)/shard_map/ppermute | solution.py:809
  1182.5 88.1 %collective-permute-done.9.refs_7_ = bf16[192,5376]{1,0:T(8,128)(2,1)S(1)} collective-permute-done((bf16[192,5376]{1,0:T(8,128)(2,1)S(1)}, bf16[192,5376]{1,0:T(8,128)(2,1)S(1)}, u32[]{:S(2)}, u32[]{:S(2)}) %collective-permute-start.9) | collective-permute-done | bytes 2064416 | tf_op jit(solution)/shard_map/ppermute | solution.py:809
  1281.2 46.1 %qkv_project.3 = (bf16[3072,512]{1,0:T(8,128)(2,1)}, bf16[3072,256]{1,0:T(8,128)(2,1)}, bf16[3072,256]{1,0:T(8,128)(2,1)}, bf16[8,384,5376]{2,1,0:T(8,128)(2,1)}) custom-call(s32[8]{0:T(128)} %broadcast_xor_fusion.dev_ref, bf16[384,5376]{1,0:T(8,128)(2,1)} %pre_norm.5.refs_0_, bf16[384,5376]{1,0:T(8,128)(2,1)} %copy-done.37, bf16[384,5376]{1,0:T(8,128)(2,1)} %copy-done.33, ...), custom_call_target="tpu_custom_call" | custom-call | flops 33822867456 | bytes 83361792 | tf_op jit(solution)/shard_map/qkv_project/pallas_call | solution.py:526
  1331.1 39.4 %attn_fwd.3 = (bf16[3072,512]{1,0:T(8,128)(2,1)}, f32[2,12,1,512]{3,2,1,0:T(1,128)S(1)}) custom-call(s32[12]{0:T(128)S(1)} %get-tuple-element.174.first_ref, bf16[3072,512]{1,0:T(8,128)(2,1)} %get-tuple-element.93.q_ref, bf16[3072,256]{1,0:T(8,128)(2,1)S(1)} %copy-done.21, bf16[3072,256]{1,0:T(8,128)(2,1)S(1)} %copy-done.23, s32[1,3072]{1,0:T(1,128)S(1)} %copy-done.7, ...), custom_call_target="tpu_custom_call" | custom-call | flops 9663676416 | bytes 12582912 | tf_op jit(solution)/shard_map/attn_fwd/pallas_call | solution.py:618
  1370.6 40.4 %all_to_all.16.o_ref = bf16[8,384,512]{2,1,0:T(8,128)(2,1)S(1)} all-to-all(bf16[8,384,512]{2,1,0:T(8,128)(2,1)} %bitcast.37), channel_id=1, replica_groups=mesh['dp'=1,'tp'=8] {'tp'}, dimensions={0} | all-to-all | bytes 6291456 | tf_op jit(solution)/shard_map/all_to_all | solution.py:862
  1473.9 49.9 %attn_bwd.5.d0_ref.d1_ref.d_ref = bf16[3072,1024]{1,0:T(8,128)(2,1)} custom-call(s32[12]{0:T(128)S(1)} %copy-done.12, bf16[3072,512]{1,0:T(8,128)(2,1)} %get-tuple-element.109.q_ref, bf16[3072,256]{1,0:T(8,128)(2,1)S(1)} %copy-done.14, bf16[3072,256]{1,0:T(8,128)(2,1)S(1)} %copy-done.16, bf16[3072,512]{1,0:T(8,128)(2,1)} %get-tuple-element.112.o_ref, ...), custom_call_target="tpu_custom_call" | custom-call | flops 24159191040 | bytes 25165824 | tf_op jit(solution)/shard_map/attn_bwd/pallas_call | solution.py:753
  1574.9 49.7 %attn_bwd.4.d0_ref.d1_ref.d_ref = bf16[3072,1024]{1,0:T(8,128)(2,1)} custom-call(s32[12]{0:T(128)S(1)} %get-tuple-element.173.first_ref, bf16[3072,512]{1,0:T(8,128)(2,1)} %get-tuple-element.100.q_ref, bf16[3072,256]{1,0:T(8,128)(2,1)S(1)} %copy-done.18, bf16[3072,256]{1,0:T(8,128)(2,1)S(1)} %copy-done.20, bf16[3072,512]{1,0:T(8,128)(2,1)} %get-tuple-element.103.o_ref, ...), custom_call_target="tpu_custom_call" | custom-call | flops 24159191040 | bytes 25165824 | tf_op jit(solution)/shard_map/attn_bwd/pallas_call | solution.py:753
  1674.9 59.1 %attn_bwd.3.d0_ref.d1_ref.d_ref = bf16[3072,1024]{1,0:T(8,128)(2,1)} custom-call(s32[12]{0:T(128)S(1)} %get-tuple-element.174.first_ref, bf16[3072,512]{1,0:T(8,128)(2,1)} %get-tuple-element.93.q_ref, bf16[3072,256]{1,0:T(8,128)(2,1)S(1)} %copy-done.22, bf16[3072,256]{1,0:T(8,128)(2,1)S(1)} %copy-done.24, bf16[3072,512]{1,0:T(8,128)(2,1)} %get-tuple-element.96.o_ref, ...), custom_call_target="tpu_custom_call" | custom-call | flops 24159191040 | bytes 25165824 | tf_op jit(solution)/shard_map/attn_bwd/pallas_call | solution.py:753
  1759.9 44.5 %grad_w.3.refs_0_ = f32[5376,1024]{1,0:T(8,128)} custom-call(bf16[8,384,5376]{2,1,0:T(8,128)(2,1)} %get-tuple-element.150.a_ref, bf16[3072,1024]{1,0:T(8,128)(2,1)} %attn_bwd.5.d0_ref.d1_ref.d_ref), custom_call_target="tpu_custom_call" | custom-call | flops 33822867456 | bytes 83361792 | tf_op jit(solution)/shard_map/grad_w/pallas_call | solution.py:412
  1832.0 45.6 %grad_w.4.refs_0_ = f32[5376,1024]{1,0:T(8,128)} custom-call(bf16[8,384,5376]{2,1,0:T(8,128)(2,1)} %get-tuple-element.149.a_ref, bf16[3072,1024]{1,0:T(8,128)(2,1)} %attn_bwd.3.d0_ref.d1_ref.d_ref, f32[5376,1024]{1,0:T(8,128)} %grad_w.3.refs_0_), custom_call_target="tpu_custom_call", output_to_operand_aliasing={{}: (2, {})} | custom-call | flops 33822867456 | bytes 83361792 | tf_op jit(solution)/shard_map/grad_w/pallas_call | solution.py:412
  1877.7 27.5 %grad_normed_own.4 = (bf16[2,384,2688]{2,1,0:T(8,128)(2,1)}, bf16[2,384,2688]{2,1,0:T(8,128)(2,1)}, bf16[2,384,2688]{2,1,0:T(8,128)(2,1)}, bf16[2,384,2688]{2,1,0:T(8,128)(2,1)}) custom-call(s32[1]{0:T(128)} %bitcast.me_ref.dst_ref, bf16[3072,1024]{1,0:T(8,128)(2,1)} %attn_bwd.4.d0_ref.d1_ref.d_ref, bf16[3072,1024]{1,0:T(8,128)(2,1)} %attn_bwd.4.d0_ref.d1_ref.d_ref, ...), custom_call_target="tpu_custom_call" | custom-call | flops 16911433728 | bytes 44040192 | tf_op jit(solution)/shard_map/grad_normed_own/pallas_call | solution.py:285
  1944.4 45.5 %grad_w.5 = (f32[5376,4,128]{2,1,0:T(4,128)}, f32[5376,2,128]{2,1,0:T(2,128)}, f32[5376,2,128]{2,1,0:T(2,128)}) custom-call(bf16[8,384,5376]{2,1,0:T(8,128)(2,1)} %get-tuple-element.148.a_ref, bf16[3072,1024]{1,0:T(8,128)(2,1)} %attn_bwd.4.d0_ref.d1_ref.d_ref, f32[5376,1024]{1,0:T(8,128)} %grad_w.4.refs_0_), custom_call_target="tpu_custom_call" | custom-call | flops 33822867456 | bytes 83361792 | tf_op jit(solution)/shard_map/grad_w/pallas_call | solution.py:412
  2023.3 77.8 %collective-permute-done.37.near_x_ref.refs_1_ = bf16[2,384,2688]{2,1,0:T(8,128)(2,1)} collective-permute-done((bf16[2,384,2688]{2,1,0:T(8,128)(2,1)}, bf16[2,384,2688]{2,1,0:T(8,128)(2,1)}, u32[]{:S(2)}, u32[]{:S(2)}) %collective-permute-start.37) | collective-permute-done | bytes 4128800 | tf_op jit(solution)/shard_map/ppermute | solution.py:809
  2107.1 38.3 %collective-permute-done.49.refs_2_ = bf16[384,2688]{1,0:T(8,128)(2,1)S(1)} collective-permute-done((bf16[384,2688]{1,0:T(8,128)(2,1)}, bf16[384,2688]{1,0:T(8,128)(2,1)S(1)}, u32[]{:S(2)}, u32[]{:S(2)}) %collective-permute-start.49) | collective-permute-done | bytes 2064416 | tf_op jit(solution)/shard_map/ppermute | solution.py:809
  (268 shorter events, 685.1 us)
Async XLA Ops:
  7.2 227.4 %collective-permute-start.14 = (bf16[512,5376]{1,0:T(8,128)(2,1)}, bf16[512,5376]{1,0:T(8,128)(2,1)}, u32[]{:S(2)}, u32[]{:S(2)}) collective-permute-start(bf16[512,5376]{1,0:T(8,128)(2,1)} %bitcast.10.refs_0_), channel_id=1, source_target_pairs={{0,4},{1,5},{2,6},{3,7},{4,0},{5,1},{6,2},{7,3}} | collective-permute-start | bytes 16515080 | tf_op jit(solution)/shard_map/ppermute | solution.py:809
  137.0 269.7 %collective-permute-start.13 = (bf16[512,5376]{1,0:T(8,128)(2,1)}, bf16[512,5376]{1,0:T(8,128)(2,1)}, u32[]{:S(2)}, u32[]{:S(2)}) collective-permute-start(bf16[512,5376]{1,0:T(8,128)(2,1)} %bitcast.10.refs_0_), channel_id=1, source_target_pairs={{0,2},{1,3},{2,0},{3,1},{4,6},{5,7},{6,4},{7,5}} | collective-permute-start | bytes 16515080 | tf_op jit(solution)/shard_map/ppermute | solution.py:809
  230.8 158.3 %collective-permute-start.33 = (bf16[192,5376]{1,0:T(8,128)(2,1)S(1)}, bf16[192,5376]{1,0:T(8,128)(2,1)}, u32[]{:S(2)}, u32[]{:S(2)}) collective-permute-start(bf16[192,5376]{1,0:T(8,128)(2,1)S(1)} %slice.68), channel_id=1, source_target_pairs={{0,2},{1,3},{2,0},{3,1},{4,6},{5,7},{6,4},{7,5}} | collective-permute-start | bytes 6193160 | tf_op jit(solution)/shard_map/ppermute | solution.py:809
  232.8 156.2 %collective-permute-start.32 = (bf16[192,5376]{1,0:T(8,128)(2,1)S(1)}, bf16[192,5376]{1,0:T(8,128)(2,1)}, u32[]{:S(2)}, u32[]{:S(2)}) collective-permute-start(bf16[192,5376]{1,0:T(8,128)(2,1)S(1)} %slice.67), channel_id=1, source_target_pairs={{0,4},{1,5},{2,6},{3,7},{4,0},{5,1},{6,2},{7,3}} | collective-permute-start | bytes 6193160 | tf_op jit(solution)/shard_map/ppermute | solution.py:809
  234.6 176.8 %collective-permute-start.30 = (bf16[384,5376]{1,0:T(8,128)(2,1)}, bf16[384,5376]{1,0:T(8,128)(2,1)}, u32[]{:S(2)}, u32[]{:S(2)}) collective-permute-start(bf16[384,5376]{1,0:T(8,128)(2,1)} %collective-permute-done.1.refs_2_), channel_id=1, source_target_pairs={{0,1},{1,0},{2,3},{3,2},{4,5},{5,4},{6,7},{7,6}} | collective-permute-start | bytes 12386312 | tf_op jit(solution)/shard_map/ppermute | solution.py:809
  234.6 176.8 %collective-permute-start.31 = (bf16[384,5376]{1,0:T(8,128)(2,1)}, bf16[384,5376]{1,0:T(8,128)(2,1)}, u32[]{:S(2)}, u32[]{:S(2)}) collective-permute-start(bf16[384,5376]{1,0:T(8,128)(2,1)} %collective-permute-done.2.refs_3_), channel_id=1, source_target_pairs={{0,1},{1,0},{2,3},{3,2},{4,5},{5,4},{6,7},{7,6}} | collective-permute-start | bytes 12386312 | tf_op jit(solution)/shard_map/ppermute | solution.py:809
  497.4 949.7 %all-gather.8.cloned.1.call-start = ((), (), s32[]{:S(2)}) async-start(), calls=%async_computation.5 | async-start | bytes 37158912 | tf_op jit(solution)/shard_map/all_gather | solution.py:865
  572.1 977.3 %all-gather.6.cloned.1.call-start = ((), (), s32[]{:S(2)}) async-start(), calls=%async_computation.4 | async-start | bytes 37158912 | tf_op jit(solution)/shard_map/all_gather | solution.py:865
  572.1 164.6 %collective-permute-start.23 = (bf16[384,5376]{1,0:T(8,128)(2,1)}, bf16[384,5376]{1,0:T(8,128)(2,1)S(1)}, u32[]{:S(2)}, u32[]{:S(2)}) collective-permute-start(bf16[384,5376]{1,0:T(8,128)(2,1)} %pre_norm.4.refs_0_), channel_id=1, source_target_pairs={{0,4},{1,5},{2,6},{3,7},{4,0},{5,1},{6,2},{7,3}} | collective-permute-start | bytes 12386312 | tf_op jit(solution)/shard_map/ppermute | solution.py:809
  572.7 167.0 %collective-permute-start.22 = (bf16[384,5376]{1,0:T(8,128)(2,1)}, bf16[384,5376]{1,0:T(8,128)(2,1)S(1)}, u32[]{:S(2)}, u32[]{:S(2)}) collective-permute-start(bf16[384,5376]{1,0:T(8,128)(2,1)} %pre_norm.4.refs_0_), channel_id=1, source_target_pairs={{0,2},{1,3},{2,0},{3,1},{4,6},{5,7},{6,4},{7,5}} | collective-permute-start | bytes 12386312 | tf_op jit(solution)/shard_map/ppermute | solution.py:809
  573.3 258.7 %collective-permute-start.21 = (bf16[384,5376]{1,0:T(8,128)(2,1)}, bf16[384,5376]{1,0:T(8,128)(2,1)S(1)}, u32[]{:S(2)}, u32[]{:S(2)}) collective-permute-start(bf16[384,5376]{1,0:T(8,128)(2,1)} %pre_norm.4.refs_0_), channel_id=1, source_target_pairs={{0,1},{1,0},{2,3},{3,2},{4,5},{5,4},{6,7},{7,6}} | collective-permute-start | bytes 12386312 | tf_op jit(solution)/shard_map/ppermute | solution.py:809
  997.0 653.4 %all-gather.4.cloned.1.call-start = ((), (), s32[]{:S(2)}) async-start(), calls=%async_computation.3 | async-start | bytes 37158912 | tf_op jit(solution)/shard_map/all_gather | solution.py:865
  1005.2 174.4 %collective-permute-start.5 = (bf16[384,5376]{1,0:T(8,128)(2,1)}, bf16[384,5376]{1,0:T(8,128)(2,1)S(1)}, u32[]{:S(2)}, u32[]{:S(2)}) collective-permute-start(bf16[384,5376]{1,0:T(8,128)(2,1)} %pre_norm.5.refs_0_), channel_id=1, source_target_pairs={{0,4},{1,5},{2,6},{3,7},{4,0},{5,1},{6,2},{7,3}} | collective-permute-start | bytes 12386312 | tf_op jit(solution)/shard_map/ppermute | solution.py:809
  1005.7 174.8 %collective-permute-start.4 = (bf16[384,5376]{1,0:T(8,128)(2,1)}, bf16[384,5376]{1,0:T(8,128)(2,1)S(1)}, u32[]{:S(2)}, u32[]{:S(2)}) collective-permute-start(bf16[384,5376]{1,0:T(8,128)(2,1)} %pre_norm.5.refs_0_), channel_id=1, source_target_pairs={{0,2},{1,3},{2,0},{3,1},{4,6},{5,7},{6,4},{7,5}} | collective-permute-start | bytes 12386312 | tf_op jit(solution)/shard_map/ppermute | solution.py:809
  1006.2 265.3 %collective-permute-start.3 = (bf16[384,5376]{1,0:T(8,128)(2,1)}, bf16[384,5376]{1,0:T(8,128)(2,1)S(1)}, u32[]{:S(2)}, u32[]{:S(2)}) collective-permute-start(bf16[384,5376]{1,0:T(8,128)(2,1)} %pre_norm.5.refs_0_), channel_id=1, source_target_pairs={{0,1},{1,0},{2,3},{3,2},{4,5},{5,4},{6,7},{7,6}} | collective-permute-start | bytes 12386312 | tf_op jit(solution)/shard_map/ppermute | solution.py:809
  1549.3 255.0 %collective-permute-start.46 = (bf16[4,384,5376]{2,1,0:T(8,128)(2,1)}, bf16[4,384,5376]{2,1,0:T(8,128)(2,1)}, u32[]{:S(2)}, u32[]{:S(2)}) collective-permute-start(bf16[4,384,5376]{2,1,0:T(8,128)(2,1)} %grad_normed_pair.5), channel_id=1, source_target_pairs={{0,1},{1,0},{2,3},{3,2},{4,5},{5,4},{6,7},{7,6}} | collective-permute-start | bytes 49545224 | tf_op jit(solution)/shard_map/ppermute | solution.py:809
  1650.2 227.4 %collective-permute-start.41 = (bf16[4,384,5376]{2,1,0:T(8,128)(2,1)}, bf16[4,384,5376]{2,1,0:T(8,128)(2,1)}, u32[]{:S(2)}, u32[]{:S(2)}) collective-permute-start(bf16[4,384,5376]{2,1,0:T(8,128)(2,1)} %grad_normed_pair.4), channel_id=1, source_target_pairs={{0,1},{1,0},{2,3},{3,2},{4,5},{5,4},{6,7},{7,6}} | collective-permute-start | bytes 49545224 | tf_op jit(solution)/shard_map/ppermute | solution.py:809
  1759.5 149.5 %collective-permute-start.36 = (bf16[4,384,5376]{2,1,0:T(8,128)(2,1)}, bf16[4,384,5376]{2,1,0:T(8,128)(2,1)}, u32[]{:S(2)}, u32[]{:S(2)}) collective-permute-start(bf16[4,384,5376]{2,1,0:T(8,128)(2,1)} %grad_normed_pair.3), channel_id=1, source_target_pairs={{0,1},{1,0},{2,3},{3,2},{4,5},{5,4},{6,7},{7,6}} | collective-permute-start | bytes 49545224 | tf_op jit(solution)/shard_map/ppermute | solution.py:809
  1936.4 164.7 %collective-permute-start.37 = (bf16[2,384,2688]{2,1,0:T(8,128)(2,1)}, bf16[2,384,2688]{2,1,0:T(8,128)(2,1)}, u32[]{:S(2)}, u32[]{:S(2)}) collective-permute-start(bf16[2,384,2688]{2,1,0:T(8,128)(2,1)} %get-tuple-element.122), channel_id=1, source_target_pairs={{0,2},{1,3},{2,0},{3,1},{4,6},{5,7},{6,4},{7,5}} | collective-permute-start | bytes 12386312 | tf_op jit(solution)/shard_map/ppermute | solution.py:809
  1936.6 164.7 %collective-permute-start.38 = (bf16[2,384,2688]{2,1,0:T(8,128)(2,1)}, bf16[2,384,2688]{2,1,0:T(8,128)(2,1)}, u32[]{:S(2)}, u32[]{:S(2)}) collective-permute-start(bf16[2,384,2688]{2,1,0:T(8,128)(2,1)} %get-tuple-element.124), channel_id=1, source_target_pairs={{0,4},{1,5},{2,6},{3,7},{4,0},{5,1},{6,2},{7,3}} | collective-permute-start | bytes 12386312 | tf_op jit(solution)/shard_map/ppermute | solution.py:809
  1944.3 201.1 %collective-permute-start.49 = (bf16[384,2688]{1,0:T(8,128)(2,1)}, bf16[384,2688]{1,0:T(8,128)(2,1)S(1)}, u32[]{:S(2)}, u32[]{:S(2)}) collective-permute-start(bf16[384,2688]{1,0:T(8,128)(2,1)} %get-tuple-element.141), channel_id=1, source_target_pairs={{0,4},{1,5},{2,6},{3,7},{4,0},{5,1},{6,2},{7,3}} | collective-permute-start | bytes 6193160 | tf_op jit(solution)/shard_map/ppermute | solution.py:809
  2013.8 185.0 %collective-permute-start.50 = (bf16[384,2688]{1,0:T(8,128)(2,1)}, bf16[384,2688]{1,0:T(8,128)(2,1)S(1)}, u32[]{:S(2)}, u32[]{:S(2)}) collective-permute-start(bf16[384,2688]{1,0:T(8,128)(2,1)} %get-tuple-element.142), channel_id=1, source_target_pairs={{0,2},{1,3},{2,0},{3,1},{4,6},{5,7},{6,4},{7,5}} | collective-permute-start | bytes 6193160 | tf_op jit(solution)/shard_map/ppermute | solution.py:809
  2021.4 192.2 %collective-permute-start.44 = (bf16[384,2688]{1,0:T(8,128)(2,1)}, bf16[384,2688]{1,0:T(8,128)(2,1)S(1)}, u32[]{:S(2)}, u32[]{:S(2)}) collective-permute-start(bf16[384,2688]{1,0:T(8,128)(2,1)} %get-tuple-element.133), channel_id=1, source_target_pairs={{0,4},{1,5},{2,6},{3,7},{4,0},{5,1},{6,2},{7,3}} | collective-permute-start | bytes 6193160 | tf_op jit(solution)/shard_map/ppermute | solution.py:809
  2107.1 125.9 %collective-permute-start.39 = (bf16[384,2688]{1,0:T(8,128)(2,1)}, bf16[384,2688]{1,0:T(8,128)(2,1)S(1)}, u32[]{:S(2)}, u32[]{:S(2)}) collective-permute-start(bf16[384,2688]{1,0:T(8,128)(2,1)} %get-tuple-element.125), channel_id=1, source_target_pairs={{0,4},{1,5},{2,6},{3,7},{4,0},{5,1},{6,2},{7,3}} | collective-permute-start | bytes 6193160 | tf_op jit(solution)/shard_map/ppermute | solution.py:809
  (81 other events, 3622.7 us)
Sparse Core Ops, SparseCore 0:
  572.2 269.2 all-gather.7
  997.2 281.3 all-gather.5
  1447.2 151.9 all-gather.3
